TPU v7x, 32 devices: a whole 2x2x4 slice. The times are simulated.
32 devices in a mesh: fsdp: 2 (over x), ctx: 4 (over y, core), tp: 4 (over z).
Axes of the slice: x: 2, y: 2, z: 4, core: 2. Of those that a mesh axis runs over, the one named last changes fastest.
Arguments:
- tokens: bfloat16 [2, 3072, 2304], P('fsdp', 'ctx'), may hold values from -6 to 6
- cotangent: bfloat16 [2, 3072, 2304], P('fsdp', 'ctx'), may hold values from -6 to 6
- prefix_length: int32 [2], P('fsdp'), may hold values from 307 to 1536
- sequence_adapter_index: int32 [2], P('fsdp'), may hold values from 0 to 7
- gains: float32 [4, 2304], replicated, may hold values from 0.5 to 1.5
- query_weight: bfloat16 [2304, 2048], P(('fsdp', 'ctx'), 'tp'), may hold values from -0.1875 to 0.1875
- key_weight: bfloat16 [2304, 1024], P(('fsdp', 'ctx'), 'tp'), may hold values from -0.1875 to 0.1875
- value_weight: bfloat16 [2304, 1024], P(('fsdp', 'ctx'), 'tp'), may hold values from -0.125 to 0.125
- output_weight: bfloat16 [2048, 2304], P('tp', ('fsdp', 'ctx')), may hold values from -0.125 to 0.125
- gate_weight: bfloat16 [2304, 9216], P(('fsdp', 'ctx'), 'tp'), may hold values from -0.125 to 0.125
- up_weight: bfloat16 [2304, 9216], P(('fsdp', 'ctx'), 'tp'), may hold values from -0.125 to 0.125
- down_weight: bfloat16 [9216, 2304], P('tp', ('fsdp', 'ctx')), may hold values from -0.0625 to 0.0625
- adapter_first_input: bfloat16 [5, 8, 2304, 16], replicated, may hold values from -0.125 to 0.125
- adapter_second_query: bfloat16 [8, 16, 2048], P(None, None, 'tp'), may hold values from -1.5 to 1.5
- adapter_second_keyvalue: bfloat16 [2, 8, 16, 1024], P(None, None, None, 'tp'), may hold values from -1.5 to 1.5
- adapter_second_gate: bfloat16 [2, 8, 16, 9216], P(None, None, None, 'tp'), may hold values from -1.5 to 1.5
- adapter_first_output: bfloat16 [8, 2048, 16], P(None, 'tp'), may hold values from -0.125 to 0.125
- adapter_first_down: bfloat16 [8, 9216, 16], P(None, 'tp'), may hold values from -0.0625 to 0.0625
- adapter_second_output: bfloat16 [2, 8, 16, 2304], replicated, may hold values from -1.5 to 1.5
Outputs:
- activations: bfloat16 [2, 3072, 2304], P('fsdp', 'ctx')
- input_grad: float32 [2, 3072, 2304], P('fsdp', 'ctx')
- grad_a_in: float32 [5, 8, 2304, 16], P(None, None, ('fsdp', 'ctx'))
- grad_b_query: float32 [8, 16, 2048], P(None, None, 'tp')
- grad_b_kv: float32 [2, 8, 16, 1024], P(None, None, None, 'tp')
- grad_b_gate_up: float32 [2, 8, 16, 9216], P(None, None, None, 'tp')
- grad_a_out: float32 [8, 2048, 16], P(None, 'tp')
- grad_a_down: float32 [8, 9216, 16], P(None, 'tp')
- grad_b_out: float32 [2, 8, 16, 2304], P(None, None, None, ('fsdp', 'ctx'))
All inputs are finite; a program needn't handle non-finite values.
Results may differ from a plain program's by a relative error of at most 0.03.
Values may be sent and summed in bfloat16 or wider, within the bound.
A program may use at most 256 MiB of HBM per device.

v0:
```python
import math

import jax
import jax.numpy as jnp
from jax import lax
from jax.sharding import PartitionSpec as P

QUERY_HEADS = 8
KEY_HEADS = 4
HEAD_SIZE = 256


epsilon = 1e-06
soft_cap = 50.0
masked_low = -1e30
highest = lax.Precision.HIGHEST


def rms_norm(values, gain):
    return values * lax.rsqrt(jnp.mean(values * values, axis=-1, keepdims=True) + epsilon) * gain


def norm_back(values, gain, incoming):
    _, gather_rows = jax.vjp(lambda inner_product: rms_norm(inner_product, gain), values)
    return gather_rows(incoming)[0]


def rotate(values, positions, sign):
    half = values.shape[-1] // 2
    freqs = jnp.exp(
        jnp.arange(half, dtype=jnp.float32) * (-2.0 * math.log(10000.0) / values.shape[-1])
    )
    angle = positions[:, None] * freqs[None, :]
    cosine = jnp.cos(angle)[:, None, :]
    sine = sign * jnp.sin(angle)[:, None, :]
    first = values[..., :half]
    second = values[..., half:]
    return jnp.concatenate(
        [first * cosine - second * sine, second * cosine + first * sine], axis=-1
    )


def project(layer_inputs, weight):
    flat = layer_inputs.reshape(-1, layer_inputs.shape[-1])
    layer_result = jnp.dot(flat, weight, preferred_element_type=jnp.float32)
    return layer_result.reshape(layer_inputs.shape[:-1] + (weight.shape[1],))


def project_back(incoming, weight):
    flat = incoming.reshape(-1, incoming.shape[-1])
    layer_result = lax.dot_general(
        flat, weight, (((1,), (1,)), ((), ())), preferred_element_type=jnp.float32
    )
    return layer_result.reshape(incoming.shape[:-1] + (weight.shape[0],))


def lowrank(layer_inputs, down_product):
    return jnp.einsum(
        "iat,itz->iaz", layer_inputs, down_product, preferred_element_type=jnp.float32
    ).astype(jnp.bfloat16)


def expand(inner_product, upward):
    return jnp.einsum("slr,src->slc", inner_product, upward, preferred_element_type=jnp.float32)


def inner_back(incoming, upward):
    return jnp.einsum("slc,src->slr", incoming, upward, preferred_element_type=jnp.float32)


def spread_back(inner_product, down_product):
    return jnp.einsum(
        "iqm,ium->iqu", inner_product, down_product, preferred_element_type=jnp.float32
    )


def outer_grad(left, right):
    return jnp.einsum("sla,slb->sab", left, right, preferred_element_type=jnp.float32)


def adapter_choose(table, select, form):
    return jnp.einsum(form, select, table, preferred_element_type=jnp.float32).astype(jnp.bfloat16)


def to_adapters(select, grads, form):
    return jnp.einsum(form, select, grads, precision=highest, preferred_element_type=jnp.float32)


def per_device(
    tokens,
    cotangent,
    prefix_length,
    sequence_adapter_index,
    gains,
    query_weight,
    key_weight,
    value_weight,
    output_weight,
    gate_weight,
    up_weight,
    down_weight,
    adapter_first_input,
    adapter_second_query,
    adapter_second_keyvalue,
    adapter_second_gate,
    adapter_first_output,
    adapter_first_down,
    adapter_second_output,
):
    seqs, rows, width = tokens.shape
    groups = QUERY_HEADS // KEY_HEADS
    scale = HEAD_SIZE ** (-0.5)
    kv_local = key_weight.shape[1] // HEAD_SIZE
    adapter_tables = adapter_second_query.shape[0]
    select_wide = (
        sequence_adapter_index[:, None] == jnp.arange(adapter_tables, dtype=jnp.int32)[None, :]
    ).astype(jnp.float32)
    choose_reduced = select_wide.astype(jnp.bfloat16)
    first_input_factor = adapter_choose(adapter_first_input, choose_reduced, "om,lmjf->lojf")
    second_query_factor = adapter_choose(adapter_second_query, choose_reduced, "qy,yeb->qeb")
    second_keyvalue_factor = adapter_choose(
        adapter_second_keyvalue, choose_reduced, "yg,wgtl->wytl"
    )
    second_gate_factor = adapter_choose(adapter_second_gate, choose_reduced, "yg,wgtl->wytl")
    first_output_factor = adapter_choose(adapter_first_output, choose_reduced, "go,oul->gul")
    first_down_factor = adapter_choose(adapter_first_down, choose_reduced, "go,oul->gul")
    second_output_factor = adapter_choose(adapter_second_output, choose_reduced, "ti,niyf->ntyf")
    full_weights = (
        lax.all_gather(query_weight, ("fsdp", "ctx"), axis=0, tiled=True),
        lax.all_gather(key_weight, ("fsdp", "ctx"), axis=0, tiled=True),
        lax.all_gather(value_weight, ("fsdp", "ctx"), axis=0, tiled=True),
        lax.all_gather(output_weight, ("fsdp", "ctx"), axis=1, tiled=True),
        lax.all_gather(gate_weight, ("fsdp", "ctx"), axis=0, tiled=True),
        lax.all_gather(up_weight, ("fsdp", "ctx"), axis=0, tiled=True),
        lax.all_gather(down_weight, ("fsdp", "ctx"), axis=1, tiled=True),
    )
    wq_full, wk_full, wv_full, wo_full, wg_full, wu_full, wd_full = full_weights
    offset = lax.axis_index("ctx") * rows
    query_pos = offset + jnp.arange(rows, dtype=jnp.int32)
    positions = query_pos.astype(jnp.float32)
    key_pos = jnp.arange(rows * lax.axis_size("ctx"), dtype=jnp.int32)
    residual = tokens.astype(jnp.float32)
    d_final = cotangent.astype(jnp.float32)
    xn1_low = rms_norm(residual, gains[0]).astype(jnp.bfloat16)
    u_query = lowrank(xn1_low, first_input_factor[0])
    u_key = lowrank(xn1_low, first_input_factor[1])
    u_value = lowrank(xn1_low, first_input_factor[2])
    query_lin = project(xn1_low, wq_full) + expand(u_query, second_query_factor)
    key_lin = project(xn1_low, wk_full) + expand(u_key, second_keyvalue_factor[0])
    value_lin = project(xn1_low, wv_full) + expand(u_value, second_keyvalue_factor[1])
    query_rot = rotate(query_lin.reshape(seqs, rows, -1, HEAD_SIZE), positions, 1.0) * scale
    query_att = (
        query_rot.astype(jnp.bfloat16)
        .reshape(seqs, rows, kv_local, groups, HEAD_SIZE)
        .transpose(0, 2, 3, 1, 4)
    )
    key_att = (
        rotate(key_lin.reshape(seqs, rows, kv_local, HEAD_SIZE), positions, 1.0)
        .astype(jnp.bfloat16)
        .transpose(0, 2, 1, 3)
    )
    value_att = (
        value_lin.astype(jnp.bfloat16)
        .reshape(seqs, rows, kv_local, HEAD_SIZE)
        .transpose(0, 2, 1, 3)
    )
    keys_all, values_all = (
        lax.all_gather(key_att, "ctx", axis=2, tiled=True),
        lax.all_gather(value_att, "ctx", axis=2, tiled=True),
    )

    def scores(q_one, k_one, plen):
        raw = jnp.einsum("kgqd,kjd->kgqj", q_one, k_one, preferred_element_type=jnp.float32)
        visible = (key_pos[None, :] <= query_pos[:, None]) | (key_pos[None, :] < plen)
        capped = jnp.where(visible[None, None], soft_cap * jnp.tanh(raw / soft_cap), masked_low)
        return (raw, capped)

    def attend_fwd(item):
        q_one, k_one, v_one, plen = item
        _, capped = scores(q_one, k_one, plen)
        top = jnp.max(capped, axis=-1, keepdims=True)
        expo = jnp.exp(capped - top)
        total = jnp.sum(expo, axis=-1, keepdims=True)
        probs = (expo / total).astype(jnp.bfloat16)
        mixed = jnp.einsum("kgqj,kjd->kgqd", probs, v_one, preferred_element_type=jnp.float32)
        return (mixed, (top + jnp.log(total))[..., 0])

    attn_mixed, log_total = lax.map(attend_fwd, (query_att, keys_all, values_all, prefix_length))
    heads_low = attn_mixed.astype(jnp.bfloat16).transpose(0, 3, 1, 2, 4).reshape(seqs, rows, -1)
    u_out_part = jnp.einsum(
        "slc,scr->slr", heads_low, first_output_factor, preferred_element_type=jnp.float32
    )
    y_att_part = project(heads_low, wo_full)
    y_att_sum, u_out_sum = (
        lax.psum(y_att_part.astype(jnp.bfloat16), "tp").astype(jnp.float32),
        lax.psum(u_out_part.astype(jnp.bfloat16), "tp").astype(jnp.float32),
    )
    u_out = u_out_sum.astype(jnp.bfloat16)
    y_att = y_att_sum + expand(u_out, second_output_factor[0])
    hidden_one = residual + rms_norm(y_att, gains[1])
    xn2_low = rms_norm(hidden_one, gains[2]).astype(jnp.bfloat16)
    u_gate = lowrank(xn2_low, first_input_factor[3])
    u_upper = lowrank(xn2_low, first_input_factor[4])
    gate = project(xn2_low, wg_full) + expand(u_gate, second_gate_factor[0])
    upper = project(xn2_low, wu_full) + expand(u_upper, second_gate_factor[1])
    act_low = (jax.nn.gelu(gate, approximate=True) * upper).astype(jnp.bfloat16)
    u_down_part = jnp.einsum(
        "slc,scr->slr", act_low, first_down_factor, preferred_element_type=jnp.float32
    )
    y_ffn_part = project(act_low, wd_full)
    y_ffn_sum, u_down_sum = (
        lax.psum(y_ffn_part.astype(jnp.bfloat16), "tp").astype(jnp.float32),
        lax.psum(u_down_part.astype(jnp.bfloat16), "tp").astype(jnp.float32),
    )
    u_down = u_down_sum.astype(jnp.bfloat16)
    y_ffn = y_ffn_sum + expand(u_down, second_output_factor[1])
    final_low = (hidden_one + rms_norm(y_ffn, gains[3])).astype(jnp.bfloat16)
    d_yffn = norm_back(y_ffn, gains[3], d_final).astype(jnp.bfloat16)
    back_weights = (
        lax.all_gather(query_weight, ("fsdp", "ctx"), axis=0, tiled=True),
        lax.all_gather(key_weight, ("fsdp", "ctx"), axis=0, tiled=True),
        lax.all_gather(value_weight, ("fsdp", "ctx"), axis=0, tiled=True),
        lax.all_gather(output_weight, ("fsdp", "ctx"), axis=1, tiled=True),
        lax.all_gather(gate_weight, ("fsdp", "ctx"), axis=0, tiled=True),
        lax.all_gather(up_weight, ("fsdp", "ctx"), axis=0, tiled=True),
        lax.all_gather(down_weight, ("fsdp", "ctx"), axis=1, tiled=True),
    )
    wq_back, wk_back, wv_back, wo_back, wg_back, wu_back, wd_back = back_weights
    du_down = inner_back(d_yffn, second_output_factor[1]).astype(jnp.bfloat16)
    d_act = project_back(d_yffn, wd_back) + jnp.einsum(
        "slr,scr->slc", du_down, first_down_factor, preferred_element_type=jnp.float32
    )
    _, gelu_pull = jax.vjp(lambda gin, uin: jax.nn.gelu(gin, approximate=True) * uin, gate, upper)
    d_gate, d_upper = gelu_pull(d_act)
    d_gate = d_gate.astype(jnp.bfloat16)
    d_upper = d_upper.astype(jnp.bfloat16)
    du_gate_part = inner_back(d_gate, second_gate_factor[0])
    du_upper_part = inner_back(d_upper, second_gate_factor[1])
    dn2_part = project_back(d_gate, wg_back) + project_back(d_upper, wu_back)
    dn2_sum, du_gate_sum, du_upper_sum = (
        lax.psum(dn2_part.astype(jnp.bfloat16), "tp").astype(jnp.float32),
        lax.psum(du_gate_part.astype(jnp.bfloat16), "tp").astype(jnp.float32),
        lax.psum(du_upper_part.astype(jnp.bfloat16), "tp").astype(jnp.float32),
    )
    du_gate = du_gate_sum.astype(jnp.bfloat16)
    du_upper = du_upper_sum.astype(jnp.bfloat16)
    dn2 = (
        dn2_sum
        + spread_back(du_gate, first_input_factor[3])
        + spread_back(du_upper, first_input_factor[4])
    )
    d_hidden = d_final + norm_back(hidden_one, gains[2], dn2)
    d_yatt = norm_back(y_att, gains[1], d_hidden).astype(jnp.bfloat16)
    du_out = inner_back(d_yatt, second_output_factor[0]).astype(jnp.bfloat16)
    d_heads = project_back(d_yatt, wo_back) + jnp.einsum(
        "slr,scr->slc", du_out, first_output_factor, preferred_element_type=jnp.float32
    )
    d_mixed = (
        d_heads.astype(jnp.bfloat16)
        .reshape(seqs, rows, kv_local, groups, HEAD_SIZE)
        .transpose(0, 2, 3, 1, 4)
    )

    def attend_back(item):
        q_one, k_one, v_one, plen, lse_one, grad_one = item
        raw, capped = scores(q_one, k_one, plen)
        probs = jnp.exp(capped - lse_one[..., None])
        d_probs = jnp.einsum("kgqd,kjd->kgqj", grad_one, v_one, preferred_element_type=jnp.float32)
        delta = jnp.sum(probs * d_probs, axis=-1, keepdims=True)
        slope = 1.0 - jnp.square(jnp.tanh(raw / soft_cap))
        d_raw = (probs * (d_probs - delta) * slope).astype(jnp.bfloat16)
        d_q = jnp.einsum("kgqj,kjd->kgqd", d_raw, k_one, preferred_element_type=jnp.float32)
        d_k = jnp.einsum("kgqj,kgqd->kjd", d_raw, q_one, preferred_element_type=jnp.float32)
        d_v = jnp.einsum(
            "kgqj,kgqd->kjd",
            probs.astype(jnp.bfloat16),
            grad_one,
            preferred_element_type=jnp.float32,
        )
        return (d_q, d_k, d_v)

    d_query_att, d_key_all, d_value_all = lax.map(
        attend_back, (query_att, keys_all, values_all, prefix_length, log_total, d_mixed)
    )
    d_key_att, d_value_att = (
        lax.psum_scatter(
            d_key_all.astype(jnp.bfloat16), "ctx", scatter_dimension=2, tiled=True
        ).astype(jnp.float32),
        lax.psum_scatter(
            d_value_all.astype(jnp.bfloat16), "ctx", scatter_dimension=2, tiled=True
        ).astype(jnp.float32),
    )
    d_query_rot = d_query_att.transpose(0, 3, 1, 2, 4).reshape(
        seqs, rows, kv_local * groups, HEAD_SIZE
    )
    d_query = (
        (rotate(d_query_rot, positions, -1.0) * scale).reshape(seqs, rows, -1).astype(jnp.bfloat16)
    )
    d_key = (
        rotate(d_key_att.transpose(0, 2, 1, 3), positions, -1.0)
        .reshape(seqs, rows, -1)
        .astype(jnp.bfloat16)
    )
    d_value = d_value_att.transpose(0, 2, 1, 3).reshape(seqs, rows, -1).astype(jnp.bfloat16)
    du_query_part = inner_back(d_query, second_query_factor)
    du_key_part = inner_back(d_key, second_keyvalue_factor[0])
    du_value_part = inner_back(d_value, second_keyvalue_factor[1])
    dn1_part = (
        project_back(d_query, wq_back)
        + project_back(d_key, wk_back)
        + project_back(d_value, wv_back)
    )
    dn1_sum, du_query_sum, du_key_sum, du_value_sum = (
        lax.psum(dn1_part.astype(jnp.bfloat16), "tp").astype(jnp.float32),
        lax.psum(du_query_part.astype(jnp.bfloat16), "tp").astype(jnp.float32),
        lax.psum(du_key_part.astype(jnp.bfloat16), "tp").astype(jnp.float32),
        lax.psum(du_value_part.astype(jnp.bfloat16), "tp").astype(jnp.float32),
    )
    du_query = du_query_sum.astype(jnp.bfloat16)
    du_key = du_key_sum.astype(jnp.bfloat16)
    du_value = du_value_sum.astype(jnp.bfloat16)
    dn1 = (
        dn1_sum
        + spread_back(du_query, first_input_factor[0])
        + spread_back(du_key, first_input_factor[1])
        + spread_back(du_value, first_input_factor[2])
    )
    input_grad = d_hidden + norm_back(residual, gains[0], dn1)
    seq_a_in = jnp.stack(
        [
            outer_grad(xn1_low, du_query),
            outer_grad(xn1_low, du_key),
            outer_grad(xn1_low, du_value),
            outer_grad(xn2_low, du_gate),
            outer_grad(xn2_low, du_upper),
        ]
    )
    seq_b_out = jnp.stack([outer_grad(u_out, d_yatt), outer_grad(u_down, d_yffn)])
    seq_b_query = outer_grad(u_query, d_query)
    seq_b_kv = jnp.stack([outer_grad(u_key, d_key), outer_grad(u_value, d_value)])
    seq_b_gate_up = jnp.stack([outer_grad(u_gate, d_gate), outer_grad(u_upper, d_upper)])
    seq_a_out = outer_grad(heads_low, du_out)
    seq_a_down = outer_grad(act_low, du_down)
    grad_a_in = to_adapters(select_wide, seq_a_in, "sa,psdr->padr")
    grad_b_out = to_adapters(select_wide, seq_b_out, "sa,psrd->pard")
    grad_b_query = to_adapters(select_wide, seq_b_query, "sa,src->arc")
    grad_b_kv = to_adapters(select_wide, seq_b_kv, "sa,psrc->parc")
    grad_b_gate_up = to_adapters(select_wide, seq_b_gate_up, "sa,psrc->parc")
    grad_a_out = to_adapters(select_wide, seq_a_out, "sa,scr->acr")
    grad_a_down = to_adapters(select_wide, seq_a_down, "sa,scr->acr")
    grad_a_in, grad_b_out = (
        lax.psum_scatter(
            grad_a_in.astype(jnp.bfloat16), ("fsdp", "ctx"), scatter_dimension=2, tiled=True
        ).astype(jnp.float32),
        lax.psum_scatter(
            grad_b_out.astype(jnp.bfloat16), ("fsdp", "ctx"), scatter_dimension=3, tiled=True
        ).astype(jnp.float32),
    )
    grad_b_query, grad_b_kv, grad_b_gate_up, grad_a_out, grad_a_down = (
        lax.psum(grad_b_query.astype(jnp.bfloat16), ("fsdp", "ctx")).astype(jnp.float32),
        lax.psum(grad_b_kv.astype(jnp.bfloat16), ("fsdp", "ctx")).astype(jnp.float32),
        lax.psum(grad_b_gate_up.astype(jnp.bfloat16), ("fsdp", "ctx")).astype(jnp.float32),
        lax.psum(grad_a_out.astype(jnp.bfloat16), ("fsdp", "ctx")).astype(jnp.float32),
        lax.psum(grad_a_down.astype(jnp.bfloat16), ("fsdp", "ctx")).astype(jnp.float32),
    )
    return (
        final_low,
        input_grad,
        grad_a_in,
        grad_b_query,
        grad_b_kv,
        grad_b_gate_up,
        grad_a_out,
        grad_a_down,
        grad_b_out,
    )


def solution(mesh):
    in_specs = (
        P("fsdp", "ctx", None),
        P("fsdp", "ctx", None),
        P("fsdp"),
        P("fsdp"),
        P(),
        P(("fsdp", "ctx"), "tp"),
        P(("fsdp", "ctx"), "tp"),
        P(("fsdp", "ctx"), "tp"),
        P("tp", ("fsdp", "ctx")),
        P(("fsdp", "ctx"), "tp"),
        P(("fsdp", "ctx"), "tp"),
        P("tp", ("fsdp", "ctx")),
        P(),
        P(None, None, "tp"),
        P(None, None, None, "tp"),
        P(None, None, None, "tp"),
        P(None, "tp", None),
        P(None, "tp", None),
        P(),
    )
    out_specs = (
        P("fsdp", "ctx", None),
        P("fsdp", "ctx", None),
        P(None, None, ("fsdp", "ctx"), None),
        P(None, None, "tp"),
        P(None, None, None, "tp"),
        P(None, None, None, "tp"),
        P(None, "tp", None),
        P(None, "tp", None),
        P(None, None, None, ("fsdp", "ctx")),
    )
    return jax.shard_map(
        per_device, mesh=mesh, in_specs=in_specs, out_specs=out_specs, check_vma=False
    )
```

profile of v0, /device:TPU:0, one launch (start us, length us, event | category | flops | bytes accessed | tf_op | source)
XLA Modules:
  0.0 1348.7 jit_solution(7386044646849659346)
XLA Ops:
  25.2 11.4 all-gather.13.cloned.1.call-done
  44.4 18.1 %all-gather.17.cloned.1.call-done = bf16[2304,256]{1,0:T(8,128)(2,1)} async-done(((bf16[288,256]{1,0:T(8,128)(2,1)}), bf16[2304,256]{1,0:T(8,128)(2,1)}) %all-gather.17.cloned.1.call-update) | async-done | bytes 1179664 | tf_op jit(solution)/shard_map/all_gather | solution.py:131
  79.6 13.7 %all-gather.11.cloned.1.call-done = bf16[2304,512]{1,0:T(8,128)(2,1)} async-done(((bf16[288,512]{1,0:T(8,128)(2,1)}), bf16[2304,512]{1,0:T(8,128)(2,1)}) %all-gather.11.cloned.1.call-update) | async-done | bytes 2359312 | tf_op jit(solution)/shard_map/all_gather | solution.py:129
  104.7 10.2 all-gather.15.cloned.1.call-done
  114.9 7.1 fusion.63
  122.0 6.7 copy-done.21
  128.8 7.3 fusion.2
  136.5 11.3 fusion.77
  147.8 19.4 %all-gather.19.cloned.1.call-done = bf16[512,2304]{0,1:T(8,128)(2,1)} async-done(((bf16[512,288]{0,1:T(8,128)(2,1)}), bf16[512,2304]{0,1:T(8,128)(2,1)}) %all-gather.19.cloned.1.call-update) | async-done | bytes 2359312 | tf_op jit(solution)/shard_map/all_gather | solution.py:132
  167.2 5.5 fusion.32
  182.5 21.5 %psum.113 = bf16[768,16]{0,1:T(8,128)(2,1)} all-reduce(bf16[768,16]{0,1:T(8,128)(2,1)} %convolution_convert_fusion.10), channel_id=1, replica_groups=mesh['fsdp'=2,'ctx'=4,'tp'=4] {'tp'}, use_global_device_ids=true, to_apply=%region_4.5 | all-reduce | flops 12288 | bytes 49152 | tf_op jit(solution)/shard_map/psum | solution.py:196
  204.0 103.7 %all-reduce.10.cloned.1.call-done = bf16[1,768,2304]{2,1,0:T(8,128)(2,1)} async-done(((bf16[1,768,2304]{2,1,0:T(8,128)(2,1)}), bf16[1,768,2304]{2,1,0:T(8,128)(2,1)}) %all-reduce.10.cloned.1.call-update) | async-done | bytes 3538960 | tf_op jit(solution)/shard_map/psum | solution.py:195
  322.4 49.9 %all-gather.21.cloned.1.call-done = bf16[2304,2304]{1,0:T(8,128)(2,1)} async-done(((bf16[288,2304]{1,0:T(8,128)(2,1)}), bf16[2304,2304]{1,0:T(8,128)(2,1)}) %all-gather.21.cloned.1.call-update) | async-done | bytes 10616848 | tf_op jit(solution)/shard_map/all_gather | solution.py:133
  372.3 10.8 fusion.183
  387.2 50.7 %all-gather.23.cloned.1.call-done = bf16[2304,2304]{1,0:T(8,128)(2,1)} async-done(((bf16[288,2304]{1,0:T(8,128)(2,1)}), bf16[2304,2304]{1,0:T(8,128)(2,1)}) %all-gather.23.cloned.1.call-update) | async-done | bytes 10616848 | tf_op jit(solution)/shard_map/all_gather | solution.py:134
  437.9 10.9 fusion.184
  448.9 4.8 multiply_convert_fusion.2
  453.7 49.7 %all-gather.25.cloned.1.call-done = bf16[2304,2304]{0,1:T(8,128)(2,1)} async-done(((bf16[2304,288]{0,1:T(8,128)(2,1)}), bf16[2304,2304]{0,1:T(8,128)(2,1)}) %all-gather.25.cloned.1.call-update) | async-done | bytes 10616848 | tf_op jit(solution)/shard_map/all_gather | solution.py:135
  503.3 13.2 fusion.33
  521.6 21.0 %psum.115 = bf16[768,16]{0,1:T(8,128)(2,1)S(1)} all-reduce(bf16[768,16]{0,1:T(8,128)(2,1)S(1)} %convolution_convert_fusion.7), channel_id=1, replica_groups=mesh['fsdp'=2,'ctx'=4,'tp'=4] {'tp'}, use_global_device_ids=true, to_apply=%region_8.9 | all-reduce | flops 12288 | bytes 49152 | tf_op jit(solution)/shard_map/psum | solution.py:213
  542.6 109.0 %all-reduce.12.cloned.1.call-done = bf16[1,768,2304]{2,1,0:T(8,128)(2,1)} async-done(((bf16[1,768,2304]{2,1,0:T(8,128)(2,1)}), bf16[1,768,2304]{2,1,0:T(8,128)(2,1)}) %all-reduce.12.cloned.1.call-update) | async-done | bytes 3538960 | tf_op jit(solution)/shard_map/psum | solution.py:212
  651.5 4.6 fusion.14
  656.9 4.6 fusion.49
  662.5 15.2 %fusion.185 = f32[768,2304]{1,0:T(8,128)} fusion(bf16[768,2304]{1,0:T(8,128)(2,1)S(1)} %get-tuple-element.94, bf16[2304,2304]{0,1:T(8,128)(2,1)} %all-gather.25.cloned.1.call-done), kind=kOutput, calls=%fused_computation.294 | convolution fusion | flops 8153726976 | bytes 21233664 | tf_op jit(solution)/shard_map/dot_general | solution.py:51
  677.8 8.9 multiply_convert_fusion.1
  686.7 16.4 %fusion.186 = f32[768,2304]{1,0:T(8,128)} fusion(bf16[768,2304]{1,0:T(8,128)(2,1)S(1)} %get-tuple-element.93, bf16[2304,2304]{1,0:T(8,128)(2,1)} %all-gather.21.cloned.1.call-done), kind=kOutput, calls=%fused_computation.295 | convolution fusion | flops 8153726976 | bytes 21233664 | tf_op jit(solution)/shard_map/dot_general | solution.py:51
  703.1 15.0 %fusion.31 = bf16[1,768,2304]{2,1,0:T(8,128)(2,1)} fusion(f32[768,2304]{1,0:T(8,128)} %fusion.186, bf16[768,2304]{1,0:T(8,128)(2,1)S(1)} %get-tuple-element.92, bf16[2304,2304]{1,0:T(8,128)(2,1)} %all-gather.23.cloned.1.call-done), kind=kOutput, calls=%fused_computation.74 | convolution fusion | flops 8157265920 | bytes 24772608 | tf_op jit(solution)/shard_map/dot_general | solution.py:51
  727.2 21.0 %all-reduce.2 = (bf16[768,16]{0,1:T(8,128)(2,1)}, bf16[768,16]{0,1:T(8,128)(2,1)}) all-reduce(bf16[768,16]{0,1:T(8,128)(2,1)} %convolution_convert_fusion.5, bf16[768,16]{0,1:T(8,128)(2,1)} %convolution_convert_fusion.4), channel_id=1, replica_groups=mesh['fsdp'=2,'ctx'=4,'tp'=4] {'tp'}, use_global_device_ids=true, to_apply=%region_12.13 | all-reduce | flops 24576 | bytes 98304 | tf_op jit(solution)/shard_map/psum | solution.py:242
  754.9 5.1 fusion.127
  760.1 92.5 %all-reduce.14.cloned.1.call-done = bf16[1,768,2304]{2,1,0:T(8,128)(2,1)} async-done(((bf16[1,768,2304]{2,1,0:T(8,128)(2,1)}), bf16[1,768,2304]{2,1,0:T(8,128)(2,1)}) %all-reduce.14.cloned.1.call-update) | async-done | bytes 3538960 | tf_op jit(solution)/shard_map/psum | solution.py:241
  852.6 10.8 multiply_reduce_fusion.2
  863.5 7.6 multiply_reduce_fusion.1
  881.1 10.8 fusion.69
  891.8 40.0 %fusion.45 = bf16[1,1,3072,256]{2,3,1,0:T(8,128)(2,1)} fusion(f32[2,768,3072]{2,1,0:T(8,128)} %fusion.69, f32[2,768,3072]{2,1,0:T(8,128)} %copy-done.21, f32[2,768]{1,0:T(2,128)S(1)} %copy-done.84, pred[768,3072]{1,0:T(8,128)(4,1)} %fusion.10, f32[1,768,1,2,128]{4,1,3,2,0:T(8,128)} %get-tuple-element.99, f32[1,768,1,2,128]{4,1,3,2,0:T(8,128)} %copy-done.35), kind=kOutput, calls=%fused_computation.83 | convolution fusion | flops 2488668672 | bytes 43259904 | tf_op jit(solution)/shard_map/while/body/eval_jaxpr/kgqj,kgqd->kjd/dot_general | solution.py:273
  938.1 12.0 fusion.42
  950.1 39.0 %fusion.72 = f32[1,768,2,256]{3,1,2,0:T(8,128)} fusion(bf16[1,1,3072,256]{2,3,1,0:T(8,128)(2,1)} %all-gather.15.cloned.1.call-done, f32[2,768,3072]{2,1,0:T(8,128)} %fusion.69, f32[2,768,3072]{2,1,0:T(8,128)} %copy-done.21, f32[2,768]{1,0:T(2,128)S(1)} %copy-done.84, pred[768,3072]{1,0:T(8,128)(4,1)} %fusion.10), kind=kOutput, calls=%fused_computation.120 | convolution fusion | flops 2486702592 | bytes 43259904 | tf_op jit(solution)/shard_map/while/body/eval_jaxpr/kgqj,kjd->kgqd/dot_general | solution.py:272
  1009.4 8.4 copy.96
  1017.8 12.4 reshape.1115
  1033.7 4.9 fusion.188
  1053.5 15.5 %copy.94 = bf16[5,8,2304,16]{3,1,0,2:T(8,128)(2,1)} copy(bf16[5,8,2304,16]{2,3,1,0:T(8,128)(2,1)S(1)} %fusion.55) | data formatting | bytes 5898240
  1069.0 25.4 %reshape.1113 = bf16[2304,640]{1,0:T(8,128)(2,1)} reshape(bf16[2304,5,8,16]{3,2,1,0:T(8,128)(2,1)} %bitcast.390) | data formatting | bytes 5898240
  1098.2 4.8 fusion.126
  1103.1 5.1 fusion.125
  1108.2 41.1 %all-reduce.18.cloned.1.call-done = (bf16[8,16,512]{2,1,0:T(8,128)(2,1)}, bf16[2,8,16,256]{3,2,1,0:T(8,128)(2,1)}, bf16[2,8,16,2304]{3,2,1,0:T(8,128)(2,1)}, bf1...) async-done(((bf16[8,16,512]{2,1,0:T(8,128)(2,1)}, bf16[2,8,16,256]{3,2,1,0:T(8,128)(2,1)}, bf16[2,8,16,2304]{3,2,1,0:T(8,128)(2,1)}, bf16[8,512,16]{1,2,0:T(8,128)(2,1)}, ...) | async-done | bytes 2162704 | tf_op jit(solution)/shard_map/psum | solution.py:360
  1159.4 125.3 %all-reduce.16.cloned.1.call-done = bf16[1,768,2304]{2,1,0:T(8,128)(2,1)} async-done(((bf16[1,768,2304]{2,1,0:T(8,128)(2,1)}), bf16[1,768,2304]{2,1,0:T(8,128)(2,1)}) %all-reduce.16.cloned.1.call-update) | async-done | bytes 3538960 | tf_op jit(solution)/shard_map/psum | solution.py:314
  1284.7 8.3 fusion.28
  1293.0 6.4 fusion.24
  1299.5 32.7 %reduce-scatter.13.cloned.1.call-done = bf16[288,640]{1,0:T(8,128)(2,1)} async-done(((bf16[2304,640]{1,0:T(8,128)(2,1)}), bf16[288,640]{1,0:T(8,128)(2,1)}) %reduce-scatter.13.cloned.1.call-update) | async-done | bytes 368656
  (349 shorter events, 182.6 us)
Async XLA Ops:
  7.2 29.4 %all-gather.13.cloned.1.call-start = ((), (), s32[]{:S(2)}) async-start(), calls=%async_computation.5 | async-start | bytes 1327104 | tf_op jit(solution)/shard_map/all_gather | solution.py:130
  7.9 54.5 %all-gather.17.cloned.1.call-start = ((), (), s32[]{:S(2)}) async-start(), calls=%async_computation.7 | async-start | bytes 1327104 | tf_op jit(solution)/shard_map/all_gather | solution.py:131
  8.7 84.6 %all-gather.11.cloned.1.call-start = ((), (), s32[]{:S(2)}) async-start(), calls=%async_computation.4 | async-start | bytes 2654208 | tf_op jit(solution)/shard_map/all_gather | solution.py:129
  9.4 105.5 %all-gather.15.cloned.1.call-start = ((), (), s32[]{:S(2)}) async-start(), calls=%async_computation.6 | async-start | bytes 1966080 | tf_op jit(solution)/shard_map/all_gather | solution.py:168
  14.6 52.7 %copy-start.67 = (f32[768]{0:T(1024)}, f32[768]{0:T(1024)S(1)}, u32[]{:S(2)}) copy-start(f32[768]{0:T(1024)S(1)} %fusion.134) | copy-start | bytes 9220
  16.2 295.4 %copy-start.46 = (f32[2304]{0:T(1024)}, f32[2304]{0:T(1024)S(1)}, u32[]{:S(2)}) copy-start(f32[2304]{0:T(1024)S(1)} %get-tuple-element.63) | copy-start | bytes 27652
  22.5 70.7 %copy-start.2 = (bf16[768,2304]{1,0:T(8,128)(2,1)}, bf16[768,2304]{1,0:T(8,128)(2,1)S(1)}, u32[]{:S(2)}) copy-start(bf16[768,2304]{1,0:T(8,128)(2,1)S(1)} %fusion.47) | copy-start | bytes 10616836
  41.8 94.8 %all-gather.27.cloned.1.call-start = ((), (), s32[]{:S(2)}) async-start(), calls=%async_computation.18 | async-start | bytes 1966080 | tf_op jit(solution)/shard_map/all_gather | solution.py:169
  66.6 100.6 %all-gather.19.cloned.1.call-start = ((), (), s32[]{:S(2)}) async-start(), calls=%async_computation.8 | async-start | bytes 2654208 | tf_op jit(solution)/shard_map/all_gather | solution.py:132
  67.2 240.5 %all-reduce.10.cloned.1.call-start = ((), (), s32[]{:S(2)}) async-start(), calls=%async_computation.9 | async-start | bytes 7077888 | tf_op jit(solution)/shard_map/psum | solution.py:195
  97.0 17.9 %copy-start.23 = (pred[768,3072]{1,0:T(8,128)(4,1)S(1)}, pred[768,3072]{1,0:T(8,128)(4,1)}, u32[]{:S(2)}) copy-start(pred[768,3072]{1,0:T(8,128)(4,1)} %fusion.10) | copy-start | bytes 7077892
  104.7 17.4 %copy-start.35 = (f32[1,768,1,2,128]{4,1,3,2,0:T(8,128)}, f32[1,768,1,2,128]{4,1,3,2,0:T(8,128)S(1)}, u32[]{:S(2)}) copy-start(f32[1,768,1,2,128]{4,1,3,2,0:T(8,128)S(1)} %get-tuple-element.98) | copy-start | bytes 2359300
  147.8 24.9 %copy-start.26 = (bf16[2,768,256]{1,2,0:T(8,128)(2,1)}, bf16[2,768,256]{1,2,0:T(8,128)(2,1)S(1)}, u32[]{:S(2)}) copy-start(bf16[2,768,256]{1,2,0:T(8,128)(2,1)S(1)} %fusion.77) | copy-start | bytes 2359300
  172.7 199.5 %all-gather.21.cloned.1.call-start = ((), (), s32[]{:S(2)}) async-start(), calls=%async_computation.10 | async-start | bytes 11943936 | tf_op jit(solution)/shard_map/all_gather | solution.py:133
  173.5 264.4 %all-gather.23.cloned.1.call-start = ((), (), s32[]{:S(2)}) async-start(), calls=%async_computation.11 | async-start | bytes 11943936 | tf_op jit(solution)/shard_map/all_gather | solution.py:134
  174.2 329.1 %all-gather.25.cloned.1.call-start = ((), (), s32[]{:S(2)}) async-start(), calls=%async_computation.12 | async-start | bytes 11943936 | tf_op jit(solution)/shard_map/all_gather | solution.py:135
  174.8 476.7 %all-reduce.12.cloned.1.call-start = ((), (), s32[]{:S(2)}) async-start(), calls=%async_computation.13 | async-start | bytes 7077888 | tf_op jit(solution)/shard_map/psum | solution.py:212
  176.4 135.2 %copy-start.8 = (bf16[1,768,2304]{2,1,0:T(8,128)(2,1)S(1)}, bf16[1,768,2304]{2,1,0:T(8,128)(2,1)}, u32[]{:S(2)}) copy-start(bf16[1,768,2304]{2,1,0:T(8,128)(2,1)} %param.19) | copy-start | bytes 10616836
  317.2 120.7 %copy-start.5 = (bf16[768,2304]{1,0:T(8,128)(2,1)}, bf16[768,2304]{1,0:T(8,128)(2,1)S(1)}, u32[]{:S(2)}) copy-start(bf16[768,2304]{1,0:T(8,128)(2,1)S(1)} %fusion.46) | copy-start | bytes 10616836
  453.7 62.9 %copy-start.14 = (bf16[768,2304]{1,0:T(8,128)(2,1)}, bf16[768,2304]{1,0:T(8,128)(2,1)S(1)}, u32[]{:S(2)}) copy-start(bf16[768,2304]{1,0:T(8,128)(2,1)S(1)} %get-tuple-element.117) | copy-start | bytes 10616836
  516.6 135.0 %copy-start.59 = (f32[2304]{0:T(1024)S(1)}, f32[2304]{0:T(1024)}, u32[]{:S(2)}) copy-start(f32[2304]{0:T(1024)} %get-tuple-element.62) | copy-start | bytes 27652
  516.6 336.0 %all-reduce.14.cloned.1.call-start = ((), (), s32[]{:S(2)}) async-start(), calls=%async_computation.14 | async-start | bytes 7077888 | tf_op jit(solution)/shard_map/psum | solution.py:241
  518.4 137.8 %slice-start = ((s8[7077888]{0:T(1024)(128)(4,1)}), s8[2883584]{0:T(1024)(128)(4,1)S(1)}, s32[]{:S(2)}) async-start(s8[7077888]{0:T(1024)(128)(4,1)} %bitcast.384), calls=%async_computation.23 | async-start | bytes 5767168
  542.5 113.6 %copy-start.45 = (bf16[768,16]{0,1:T(8,128)(2,1)}, bf16[768,16]{0,1:T(8,128)(2,1)S(1)}, u32[]{:S(2)}) copy-start(bf16[768,16]{0,1:T(8,128)(2,1)S(1)} %psum.115) | copy-start | bytes 73732
  661.5 16.2 %copy-start.12 = (bf16[768,2304]{1,0:T(8,128)(2,1)}, bf16[768,2304]{1,0:T(8,128)(2,1)S(1)}, u32[]{:S(2)}) copy-start(bf16[768,2304]{1,0:T(8,128)(2,1)S(1)} %get-tuple-element.94) | copy-start | bytes 10616836
  661.5 16.2 %slice-start.6 = ((s8[7077888]{0:T(1024)(128)(4,1)}), s8[4194304]{0:T(1024)(128)(4,1)S(1)}, s32[]{:S(2)}) async-start(s8[7077888]{0:T(1024)(128)(4,1)} %bitcast.392), calls=%async_computation.29 | async-start | bytes 8388608
  686.7 16.4 %copy-start.19 = (bf16[768,2304]{1,0:T(8,128)(2,1)}, bf16[768,2304]{1,0:T(8,128)(2,1)S(1)}, u32[]{:S(2)}) copy-start(bf16[768,2304]{1,0:T(8,128)(2,1)S(1)} %get-tuple-element.93) | copy-start | bytes 10616836
  686.7 16.4 %copy-start.20 = (bf16[768,2304]{1,0:T(8,128)(2,1)}, bf16[768,2304]{1,0:T(8,128)(2,1)S(1)}, u32[]{:S(2)}) copy-start(bf16[768,2304]{1,0:T(8,128)(2,1)S(1)} %get-tuple-element.92) | copy-start | bytes 10616836
  703.1 16.2 %copy-start.81 = (f32[2,768]{1,0:T(2,128)S(1)}, f32[2,768]{1,0:T(2,128)}, u32[]{:S(2)}) copy-start(f32[2,768]{1,0:T(2,128)} %copy-done.80) | copy-start | bytes 18436
  703.1 16.1 %copy-start.83 = (f32[2,768]{1,0:T(2,128)S(1)}, f32[2,768]{1,0:T(2,128)}, u32[]{:S(2)}) copy-start(f32[2,768]{1,0:T(2,128)} %copy-done.82) | copy-start | bytes 18436
  718.1 30.1 %copy-start.13 = (bf16[768,2304]{1,0:T(8,128)(2,1)S(1)}, bf16[768,2304]{1,0:T(8,128)(2,1)}, u32[]{:S(2)}) copy-start(bf16[768,2304]{1,0:T(8,128)(2,1)} %copy-done.12) | copy-start | bytes 10616836
  718.1 282.7 %reduce-scatter.9.cloned.1.call-start = ((), (), s32[]{:S(2)}) async-start(), calls=%async_computation.15 | async-start | bytes 1966080 | tf_op jit(solution)/shard_map/reduce_scatter | solution.py:286
  753.7 98.9 %copy-start.61 = (f32[2304]{0:T(1024)S(1)}, f32[2304]{0:T(1024)}, u32[]{:S(2)}) copy-start(f32[2304]{0:T(1024)} %get-tuple-element.65) | copy-start | bytes 27652
  753.7 98.9 %copy-start.64 = (bf16[768,16]{0,1:T(8,128)(2,1)S(1)}, bf16[768,16]{0,1:T(8,128)(2,1)}, u32[]{:S(2)}) copy-start(bf16[768,16]{0,1:T(8,128)(2,1)} %get-tuple-element.87) | copy-start | bytes 73732
  754.9 108.5 %slice-start.2 = ((s8[7077888]{0:T(1024)(128)(4,1)}), s8[2883584]{0:T(1024)(128)(4,1)S(1)}, s32[]{:S(2)}) async-start(s8[7077888]{0:T(1024)(128)(4,1)} %bitcast.386), calls=%async_computation.25 | async-start | bytes 5767168
  852.6 18.5 %slice-start.4 = ((s8[7077888]{0:T(1024)(128)(4,1)}), s8[4194304]{0:T(1024)(128)(4,1)S(1)}, s32[]{:S(2)}) async-start(s8[7077888]{0:T(1024)(128)(4,1)} %bitcast.388), calls=%async_computation.27 | async-start | bytes 8388608
  891.8 44.4 %copy-start.86 = (f32[8]{0:T(128)S(1)}, f32[8]{0:T(128)}, u32[]{:S(2)}) copy-start(f32[8]{0:T(128)} %compare_convert_fusion.1) | copy-start | bytes 100
  931.9 73.9 %reduce-scatter.11.cloned.1.call-start = ((), (), s32[]{:S(2)}) async-start(), calls=%async_computation.16 | async-start | bytes 1966080 | tf_op jit(solution)/shard_map/reduce_scatter | solution.py:289
  950.1 98.2 %all-reduce.20.cloned.1.call-start = ((), (), s32[]{:S(2)}) async-start(), calls=%async_computation.22 | async-start | bytes 147456 | tf_op jit(solution)/shard_map/psum | solution.py:316
  1007.6 86.9 %reduce-scatter.15.cloned.1.call-start = ((), (), s32[]{:S(2)}) async-start(), calls=%async_computation.20 | async-start | bytes 1327104
  1030.2 119.0 %all-reduce.18.cloned.1.call-start = ((), (), s32[]{:S(2)}) async-start(), calls=%async_computation.21 | async-start | bytes 4325376 | tf_op jit(solution)/shard_map/psum | solution.py:360
  1039.9 244.8 %all-reduce.16.cloned.1.call-start = ((), (), s32[]{:S(2)}) async-start(), calls=%async_computation.17 | async-start | bytes 7077888 | tf_op jit(solution)/shard_map/psum | solution.py:314
  1048.2 284.0 %reduce-scatter.13.cloned.1.call-start = ((), (), s32[]{:S(2)}) async-start(), calls=%async_computation.19 | async-start | bytes 3317760
  1069.0 29.2 %copy-start.50 = (bf16[768,16]{0,1:T(8,128)(2,1)S(1)}, bf16[768,16]{0,1:T(8,128)(2,1)}, u32[]{:S(2)}) copy-start(bf16[768,16]{0,1:T(8,128)(2,1)} %get-tuple-element.71) | copy-start | bytes 73732
  1103.1 181.6 %copy-start.9 = (bf16[1,768,2304]{2,1,0:T(8,128)(2,1)S(1)}, bf16[1,768,2304]{2,1,0:T(8,128)(2,1)}, u32[]{:S(2)}) copy-start(bf16[1,768,2304]{2,1,0:T(8,128)(2,1)} %param.19) | copy-start | bytes 10616836
  1103.1 181.6 %copy-start.58 = (f32[2304]{0:T(1024)S(1)}, f32[2304]{0:T(1024)}, u32[]{:S(2)}) copy-start(f32[2304]{0:T(1024)} %copy-done.57) | copy-start | bytes 27652
  1159.4 133.6 %copy-start.73 = (f32[768]{0:T(1024)S(1)}, f32[768]{0:T(1024)}, u32[]{:S(2)}) copy-start(f32[768]{0:T(1024)} %copy-done.72) | copy-start | bytes 9220
  1293.0 49.0 %copy-start.1 = (bf16[5,8,2304,16]{2,3,1,0:T(8,128)(2,1)S(1)}, bf16[5,8,2304,16]{2,3,1,0:T(8,128)(2,1)}, u32[]{:S(2)}) copy-start(bf16[5,8,2304,16]{2,3,1,0:T(8,128)(2,1)} %param.31) | copy-start | bytes 8847364
  (69 other events, 457.2 us)
Sparse Core Ops, SparseCore 0:
  9.9 26.6 all-gather.12
  38.4 23.9 all-gather.16
  64.3 28.8 all-gather.10
  95.2 19.6 all-gather.14
  116.9 19.6 all-gather.26
  138.3 28.8 all-gather.18
  172.9 134.7 all-reduce.9
  309.6 62.6 all-gather.20
  374.2 63.6 all-gather.22
  439.6 63.6 all-gather.24
  516.7 134.7 all-reduce.11
  718.3 134.2 all-reduce.13
  932.0 27.0 reduce-scatter.8
  961.5 28.0 reduce-scatter.10
  1007.8 33.6 all-reduce.19
  1045.1 36.8 reduce-scatter.14
  1086.2 62.9 all-reduce.17
  1151.5 133.1 all-reduce.15
  1288.1 44.0 reduce-scatter.12
where the time goes:
time: 1360 us; the launch traced here: 1350 us
  waiting for transfers between devices  732 us (54%)
  matrix products  353 us (26%)
  local copies, waits for them, and re-layouts  103 us (8%)
  other arithmetic  79.2 us (6%)
  blocking collectives  63.5 us (5%)
  between operations  16.6 us (1%)
    psum x1, waiting for transfers between devices, per_device(): lax.psum(dn1_part.astype(jnp.bfloat16), 'tp').astype(jnp.float32)  125 us
    psum x1, waiting for transfers between devices, per_device(): lax.psum(y_ffn_part.astype(jnp.bfloat16), 'tp').astype(jnp.float32)  109 us
    psum x1, waiting for transfers between devices, per_device(): lax.psum(y_att_part.astype(jnp.bfloat16), 'tp').astype(jnp.float32)  104 us
    psum x1, waiting for transfers between devices, per_device(): lax.psum(dn2_part.astype(jnp.bfloat16), 'tp').astype(jnp.float32)  92.5 us
    unnamed x206, local copies, waits for them, and re-layouts  92.2 us
    dot_general x7, matrix products, project_back(): lax.dot_general(flat, weight, (((1,), (1,)), ((), ())), preferred_element...  60.8 us
    all_gather x1, waiting for transfers between devices, per_device(): lax.all_gather(up_weight, ('fsdp', 'ctx'), axis=0, tiled=True)  50.7 us
    all_gather x1, waiting for transfers between devices, per_device(): lax.all_gather(gate_weight, ('fsdp', 'ctx'), axis=0, tiled=True)  49.9 us
  transfers between devices with their start and end apart: 19, of which 15 were waited for; matrix products, arithmetic and copies ran while one was open for 26% of the time, Pallas kernels for 0%

commit v1 on v0

v1 whole, which is shorter than its diff:
```python
import functools
import math

import jax
import jax.numpy as jnp
from jax import lax
from jax.experimental import pallas as pl
from jax.experimental.pallas import tpu as pltpu
from jax.sharding import PartitionSpec as P

QUERY_HEADS = 8
KEY_HEADS = 4
HEAD_SIZE = 256

epsilon = 1e-06
soft_cap = 50.0
masked_low = -1e30
MESH = pl.DeviceIdType.MESH
f32 = jnp.float32
bf16 = jnp.bfloat16


def rms_norm(values, gain):
    return values * lax.rsqrt(jnp.mean(values * values, axis=-1, keepdims=True) + epsilon) * gain


def norm_back(values, gain, incoming):
    scale = lax.rsqrt(jnp.mean(values * values, axis=-1, keepdims=True) + epsilon)
    unit = values * scale
    weighted = incoming * gain
    return scale * (weighted - unit * jnp.mean(weighted * unit, axis=-1, keepdims=True))


def rotate(values, cosine, sine):
    half = values.shape[-1] // 2
    first = values[..., :half]
    second = values[..., half:]
    return jnp.concatenate(
        [first * cosine - second * sine, second * cosine + first * sine], axis=-1
    )


def dot_nn(left, right):
    return lax.dot_general(left, right, (((1,), (0,)), ((), ())), preferred_element_type=f32)


def dot_nt(left, right):
    return lax.dot_general(left, right, (((1,), (1,)), ((), ())), preferred_element_type=f32)


def dot_tn(left, right):
    return lax.dot_general(left, right, (((0,), (0,)), ((), ())), preferred_element_type=f32)


def sum_kernel(count, width, chunks, slots, *refs):
    lefts = refs[:count]
    rights = refs[count : 2 * count]
    refs = refs[2 * count :]
    terms = None
    if slots:
        terms, out, every = refs[:3]
        refs = refs[3:]
    else:
        out = refs[0]
        refs = refs[1:]
    part, mine, got_a, got_b, a_send, a_recv, b_send, b_recv, c_send, c_recv = refs[:10]
    z = lax.axis_index("tp")
    inner = (z == 1) | (z == 2)
    outer = (z == 0) | (z == 3)
    pair = z + 1 - 2 * lax.rem(z, 2)
    across = 3 - z
    barrier = pltpu.get_barrier_semaphore()

    def greet(axis, peer):
        pl.semaphore_signal(barrier, inc=1, device_id={axis: peer}, device_id_type=MESH)

    others = 0
    if slots:
        at = lax.axis_index("ctx")
        core = lax.rem(at, 2)
        row = lax.div(at, 2)
        core_peer = at + 1 - 2 * core
        row_peer = at + 2 - 4 * row
        seq = lax.axis_index("fsdp")
        others = 2 + slots - 1
        greet("ctx", core_peer)
        greet("ctx", row_peer)
        for d in range(1, slots):
            greet("fsdp", lax.rem(seq + d, slots))
    greet("tp", pair)

    @pl.when(inner)
    def _():
        greet("tp", across)
        pl.semaphore_wait(barrier, others + 2)

    @pl.when(outer)
    def _():
        pl.semaphore_wait(barrier, others + 1)

    def cols(c):
        return pl.ds(pl.multiple_of(c * width, width), width)

    def remote(source, target, send, recv, axis, peer):
        return pltpu.make_async_remote_copy(
            source, target, send, recv, device_id={axis: peer}, device_id_type=MESH
        )

    def copy_a(c):
        return remote(mine.at[c], got_a.at[c], a_send.at[c], a_recv.at[c], "tp", pair)

    def copy_b(c):
        return remote(mine.at[c], got_b.at[c], b_send.at[c], b_recv.at[c], "tp", across)

    def copy_c(c):
        place = out.at[:, cols(c)]
        return remote(place, place, c_send.at[c], c_recv.at[c], "tp", pair)

    def finish(c):
        copy_b(c).wait_recv()
        out[:, cols(c)] = (mine[c].astype(f32) + got_b[c].astype(f32)).astype(bf16)
        copy_c(c).start()

    if slots:
        from_core, with_core, from_row, held, held_a, held_b, full, g_send, g_recv = refs[10:]
        summed = held_a.shape[0]
        rest = pl.ds(summed, full.shape[0] - summed)

        def core_copy(j):
            source = terms.at[2 * j + 1 - core]
            return remote(source, from_core.at[j], g_send.at[j], g_recv.at[j], "ctx", core_peer)

        def row_copy():
            source = with_core.at[1 - row]
            return remote(source, from_row, g_send.at[2], g_recv.at[2], "ctx", row_peer)

        def line_a():
            source = held.at[pl.ds(0, summed)]
            return remote(source, held_a, g_send.at[3], g_recv.at[3], "tp", pair)

        def line_b():
            source = held.at[pl.ds(0, summed)]
            return remote(source, held_b, g_send.at[4], g_recv.at[4], "tp", across)

        def line_c():
            place = full.at[pl.ds(0, summed)]
            return remote(place, place, g_send.at[5], g_recv.at[5], "tp", pair)

        def seq_copy(d):
            peer = lax.rem(seq + d, slots)
            return remote(
                full, every.at[seq, at], g_send.at[8 + d], g_recv.at[8 + d], "fsdp", peer
            )

        def row_back():
            place = every.at[:, at]
            return remote(place, place, g_send.at[6], g_recv.at[6], "ctx", row_peer)

        def core_back(j):
            place = every.at[:, 2 * j + core]
            return remote(place, place, g_send.at[7 + j], g_recv.at[7 + j], "ctx", core_peer)

        core_copy(0).start()
        core_copy(1).start()

        def reduce_terms(c):
            @pl.when(c == 1)
            def _():
                for j in range(2):
                    core_copy(j).wait_recv()
                    total = terms[2 * j + core].astype(f32) + from_core[j].astype(f32)
                    with_core[j] = total.astype(bf16)
                row_copy().start()

            @pl.when(c == 3)
            def _():
                row_copy().wait_recv()
                held[...] = (with_core[row].astype(f32) + from_row[...].astype(f32)).astype(bf16)
                full[rest, :] = held[rest, :]

            @pl.when((c == 3) & outer)
            def _():
                line_a().start()

            @pl.when((c == 6) & inner)
            def _():
                line_a().wait_recv()
                total = held[:summed].astype(f32) + held_a[...].astype(f32)
                held[:summed] = total.astype(bf16)
                line_b().start()

            @pl.when((c == 8) & inner)
            def _():
                line_b().wait_recv()
                total = held[:summed].astype(f32) + held_b[...].astype(f32)
                full[:summed] = total.astype(bf16)
                line_c().start()

            @pl.when((c == 11) & outer)
            def _():
                line_c().wait_recv()

            @pl.when(c == 11)
            def _():
                every[seq, at] = full[...]
                for d in range(1, slots):
                    seq_copy(d).start()

            @pl.when(c == 13)
            def _():
                for d in range(1, slots):
                    seq_copy(d).wait_recv()
                row_back().start()

            @pl.when(c == 15)
            def _():
                row_back().wait_recv()
                core_back(0).start()
                core_back(1).start()

    def body(c, carry):
        for i, (left, right) in enumerate(zip(lefts, rights)):
            for m in range(0, left.shape[0], 256):
                term = dot_nt(left[m : m + 256, :], right[cols(c), :])
                part[m : m + 256, :] = term if i == 0 else part[m : m + 256, :] + term

        @pl.when(outer)
        def _():
            mine[c] = part[...].astype(bf16)
            copy_a(c).start()

        @pl.when(inner)
        def _():
            copy_a(c).wait_recv()
            mine[c] = (part[...] + got_a[c].astype(f32)).astype(bf16)
            copy_b(c).start()

        @pl.when(inner & (c >= 1))
        def _():
            finish(c - 1)

        if slots:
            reduce_terms(c)
        return carry

    lax.fori_loop(0, chunks, body, 0)

    @pl.when(inner)
    def _():
        finish(chunks - 1)

        def drain(c, carry):
            copy_b(c).wait_send()
            copy_c(c).wait_send()
            return carry

        lax.fori_loop(0, chunks, drain, 0)

    @pl.when(outer)
    def _():
        def drain(c, carry):
            copy_a(c).wait_send()
            copy_c(c).wait_recv()
            return carry

        lax.fori_loop(0, chunks, drain, 0)

    if slots:
        for j in range(2):
            core_copy(j).wait_send()
            core_back(j).wait()
        row_copy().wait_send()
        row_back().wait_send()
        for d in range(1, slots):
            seq_copy(d).wait_send()

        @pl.when(outer)
        def _():
            line_a().wait_send()

        @pl.when(inner)
        def _():
            line_b().wait_send()
            line_c().wait_send()


def matmul_sum(lefts, rights, collective_id, width=128, terms=None, slots=0, summed=0):
    rows = lefts[0].shape[0]
    total = rights[0].shape[0]
    chunks = total // width
    flops = sum(2 * rows * total * left.shape[1] for left in lefts)
    moved = sum(left.size + right.size for left, right in zip(lefts, rights)) + rows * total
    scratch = (
        [pltpu.VMEM((rows, width), f32)]
        + [pltpu.VMEM((chunks, rows, width), bf16)] * 3
        + [pltpu.SemaphoreType.DMA((chunks,))] * 6
    )
    shapes = [jax.ShapeDtypeStruct((rows, total), bf16)]
    operands = [*lefts, *rights]
    if slots:
        assert chunks >= 17
        block = terms.shape[1:]
        lead = (summed, block[1])
        operands.append(terms)
        shapes.append(jax.ShapeDtypeStruct((slots, *terms.shape), bf16))
        scratch += [
            pltpu.VMEM((2, *block), bf16),
            pltpu.VMEM((2, *block), bf16),
            pltpu.VMEM(block, bf16),
            pltpu.VMEM(block, bf16),
            pltpu.VMEM(lead, bf16),
            pltpu.VMEM(lead, bf16),
            pltpu.VMEM(block, bf16),
            pltpu.SemaphoreType.DMA((9 + slots,)),
            pltpu.SemaphoreType.DMA((9 + slots,)),
        ]
    vmem = pl.BlockSpec(memory_space=pltpu.VMEM)
    result = pl.pallas_call(
        functools.partial(sum_kernel, len(lefts), width, chunks, slots),
        out_shape=shapes,
        in_specs=[vmem] * len(operands),
        out_specs=[vmem] * len(shapes),
        scratch_shapes=scratch,
        compiler_params=pltpu.CompilerParams(
            collective_id=collective_id, has_side_effects=True, vmem_limit_bytes=60 * 1024 * 1024
        ),
        cost_estimate=pl.CostEstimate(flops=flops, bytes_accessed=2 * moved, transcendentals=0),
        name=f"matmul_sum_{collective_id}",
    )(*operands)
    return result if slots else result[0]


def swap(values, step):
    return lax.ppermute(values, "ctx", [(i, i ^ step) for i in range(lax.axis_size("ctx"))])


def per_device(
    tokens,
    cotangent,
    prefix_length,
    sequence_adapter_index,
    gains,
    query_weight,
    key_weight,
    value_weight,
    output_weight,
    gate_weight,
    up_weight,
    down_weight,
    adapter_first_input,
    adapter_second_query,
    adapter_second_keyvalue,
    adapter_second_gate,
    adapter_first_output,
    adapter_first_down,
    adapter_second_output,
):
    seqs, rows, width = tokens.shape
    assert seqs == 1 and lax.axis_size("ctx") == 4 and lax.axis_size("tp") == 4
    groups = QUERY_HEADS // KEY_HEADS
    scale = HEAD_SIZE ** (-0.5)
    q_cols = query_weight.shape[1]
    k_cols = key_weight.shape[1]
    adapter_count, rank = adapter_second_query.shape[:2]
    both = ("fsdp", "ctx")
    adapter = sequence_adapter_index[0]

    def chosen(table, dim):
        return lax.dynamic_index_in_dim(table, adapter, dim, keepdims=False)

    attn_local = jnp.concatenate(
        [query_weight, key_weight, value_weight, output_weight.T], axis=1
    )
    attn_full = lax.all_gather(attn_local, both, axis=0, tiled=True)
    gate_full = lax.all_gather(gate_weight, both, axis=0, tiled=True)
    up_full = lax.all_gather(up_weight, both, axis=0, tiled=True)
    down_full = lax.all_gather(down_weight.T, both, axis=0, tiled=True)
    qkv_cols = q_cols + 2 * k_cols
    qkv_full = attn_full[:, :qkv_cols]
    out_full = attn_full[:, qkv_cols:]

    a_in = chosen(adapter_first_input, 1)
    b_query = chosen(adapter_second_query, 0)
    b_kv = chosen(adapter_second_keyvalue, 1)
    b_gate = chosen(adapter_second_gate, 1)
    a_out = chosen(adapter_first_output, 0)
    a_down = chosen(adapter_first_down, 0)
    b_out = chosen(adapter_second_output, 1)
    a_qkv = jnp.concatenate([a_in[0], a_in[1], a_in[2]], axis=1)
    a_gu = jnp.concatenate([a_in[3], a_in[4]], axis=1)

    ctx = lax.axis_index("ctx")
    query_pos = ctx * rows + jnp.arange(rows, dtype=jnp.int32)
    half = HEAD_SIZE // 2
    freqs = jnp.exp(jnp.arange(half, dtype=f32) * (-2.0 * math.log(10000.0) / HEAD_SIZE))
    angle = query_pos.astype(f32)[:, None] * freqs[None, :]
    cosine = jnp.cos(angle)[:, None, :]
    sine = jnp.sin(angle)[:, None, :]

    residual = tokens[0].astype(f32)
    d_final = cotangent[0].astype(f32)
    n1 = rms_norm(residual, gains[0]).astype(bf16)
    u_qkv = dot_nn(n1, a_qkv).astype(bf16)
    lin = dot_nn(n1, qkv_full)
    query = lin[:, :q_cols] + dot_nn(u_qkv[:, :rank], b_query)
    key = lin[:, q_cols : q_cols + k_cols] + dot_nn(u_qkv[:, rank : 2 * rank], b_kv[0])
    value = lin[:, q_cols + k_cols :] + dot_nn(u_qkv[:, 2 * rank :], b_kv[1])
    qa = (rotate(query.reshape(rows, -1, HEAD_SIZE), cosine, sine) * scale).astype(bf16)
    ka = rotate(key.reshape(rows, -1, HEAD_SIZE), cosine, sine).reshape(rows, -1).astype(bf16)
    va = value.astype(bf16)

    own = jnp.stack([ka, va])
    from_row = swap(own, 2)
    near = jnp.stack([own, from_row])
    far = swap(near, 1)
    blocks = jnp.concatenate([near, far])
    keys = blocks[:, 0].reshape(-1, HEAD_SIZE)
    values = blocks[:, 1].reshape(-1, HEAD_SIZE)
    block_of = jnp.stack([ctx, ctx ^ 2, ctx ^ 1, ctx ^ 3])
    key_pos = (block_of[:, None] * rows + jnp.arange(rows, dtype=jnp.int32)[None, :]).reshape(-1)
    visible = (key_pos[None, :] <= query_pos[:, None]) | (key_pos[None, :] < prefix_length[0])

    q_heads = qa.transpose(1, 0, 2)
    raw = jnp.einsum("gqd,kd->gqk", q_heads, keys, preferred_element_type=f32)
    capped = jnp.where(visible[None], soft_cap * jnp.tanh(raw / soft_cap), masked_low)
    top = jnp.max(capped, axis=-1, keepdims=True)
    expo = jnp.exp(capped - top)
    total = jnp.sum(expo, axis=-1, keepdims=True)
    probs = (expo / total).astype(bf16)
    mixed = jnp.einsum("gqk,kd->gqd", probs, values, preferred_element_type=f32)
    lse = top + jnp.log(total)
    ob = mixed.astype(bf16).transpose(1, 0, 2).reshape(rows, -1)

    u_out = dot_nn(ob, a_out).astype(bf16)
    y_att = matmul_sum([ob, u_out], [out_full, b_out[0].T], 1).astype(f32)
    h1 = residual + rms_norm(y_att, gains[1])
    n2 = rms_norm(h1, gains[2]).astype(bf16)
    u_gu = dot_nn(n2, a_gu).astype(bf16)
    gate = dot_nn(n2, gate_full) + dot_nn(u_gu[:, :rank], b_gate[0])
    upper = dot_nn(n2, up_full) + dot_nn(u_gu[:, rank:], b_gate[1])
    act = (jax.nn.gelu(gate, approximate=True) * upper).astype(bf16)
    u_down = dot_nn(act, a_down).astype(bf16)
    y_ffn = matmul_sum([act, u_down], [down_full, b_out[1].T], 2).astype(f32)
    final = (h1 + rms_norm(y_ffn, gains[3])).astype(bf16)

    e_ffn = norm_back(y_ffn, gains[3], d_final).astype(bf16)
    du_down = dot_nt(e_ffn, b_out[1]).astype(bf16)
    d_act = dot_nn(e_ffn, down_full) + dot_nt(du_down, a_down)
    _, gelu_pull = jax.vjp(lambda gin, uin: jax.nn.gelu(gin, approximate=True) * uin, gate, upper)
    d_gate, d_up = gelu_pull(d_act)
    d_gate = d_gate.astype(bf16)
    d_up = d_up.astype(bf16)
    du_gate = dot_nt(d_gate, b_gate[0]).astype(bf16)
    du_up = dot_nt(d_up, b_gate[1]).astype(bf16)
    du_gu = jnp.concatenate([du_gate, du_up], axis=1)
    dn2 = matmul_sum([d_gate, d_up, du_gu], [gate_full, up_full, a_gu], 3).astype(f32)
    dh1 = d_final + norm_back(h1, gains[2], dn2)
    e_att = norm_back(y_att, gains[1], dh1).astype(bf16)
    du_out = dot_nt(e_att, b_out[0]).astype(bf16)
    d_ob = (dot_nn(e_att, out_full) + dot_nt(du_out, a_out)).astype(bf16)
    d_mixed = d_ob.reshape(rows, -1, HEAD_SIZE).transpose(1, 0, 2)

    p_back = jnp.exp(capped - lse)
    d_probs = jnp.einsum("gqd,kd->gqk", d_mixed, values, preferred_element_type=f32)
    delta = jnp.sum(p_back * d_probs, axis=-1, keepdims=True)
    slope = 1.0 - jnp.square(jnp.tanh(raw / soft_cap))
    d_raw = (p_back * (d_probs - delta) * slope).astype(bf16)
    dqa = jnp.einsum("gqk,kd->gqd", d_raw, keys, preferred_element_type=f32)
    dka = jnp.einsum("gqk,gqd->kd", d_raw, q_heads, preferred_element_type=f32)
    dva = jnp.einsum(
        "gqk,gqd->kd", p_back.astype(bf16), d_mixed, preferred_element_type=f32
    )
    d_blocks = jnp.stack([dka, dva]).reshape(2, 4, rows, -1)
    got_far = swap(d_blocks[:, 2:].astype(bf16), 1)
    d_near = d_blocks[:, :2] + got_far.astype(f32)
    got_row = swap(d_near[:, 1].astype(bf16), 2)
    d_own = d_near[:, 0] + got_row.astype(f32)

    d_query = (rotate(dqa.transpose(1, 0, 2), cosine, -sine) * scale).reshape(rows, -1)
    d_key = rotate(d_own[0].reshape(rows, -1, HEAD_SIZE), cosine, -sine).reshape(rows, -1)
    d_query = d_query.astype(bf16)
    d_key = d_key.astype(bf16)
    d_value = d_own[1].astype(bf16)
    d_qkv = jnp.concatenate([d_query, d_key, d_value], axis=1)
    du_query = dot_nt(d_query, b_query).astype(bf16)
    du_key = dot_nt(d_key, b_kv[0]).astype(bf16)
    du_value = dot_nt(d_value, b_kv[1]).astype(bf16)
    du_qkv = jnp.concatenate([du_query, du_key, du_value], axis=1)

    wide = jnp.concatenate(
        [
            dot_tn(du_qkv, n1),
            dot_tn(du_gu, n2),
            dot_tn(u_out, e_att),
            dot_tn(u_down, e_ffn),
        ]
    )
    hidden = d_gate.shape[1]
    g_b_gate = dot_tn(u_gu[:, :rank], d_gate)
    g_b_up = dot_tn(u_gu[:, rank:], d_up)
    g_a_down = dot_tn(du_down, act)
    g_b_query = dot_tn(u_qkv[:, :rank], d_query)
    g_b_key = dot_tn(u_qkv[:, rank : 2 * rank], d_key)
    g_b_value = dot_tn(u_qkv[:, 2 * rank :], d_value)
    g_a_out = dot_tn(du_out, ob)
    small = jnp.concatenate([g_b_query, g_b_key, g_b_value, g_a_out], axis=1)
    small = jnp.pad(small, ((0, 0), (0, hidden - small.shape[1])))
    split = jnp.concatenate([g_b_gate, g_b_up, g_a_down, small])

    slots = lax.axis_size("fsdp")
    first = ((ctx == 0) & (lax.axis_index("tp") == 0)).astype(f32)
    note = jnp.full((1, width), adapter.astype(f32) * first)
    wide = jnp.pad(jnp.concatenate([wide, note]), ((0, 8 * rank - wide.shape[0] - 1), (0, 0)))
    terms = jnp.concatenate(
        [wide.reshape(4, 2 * rank, width), split.reshape(4, rank, width)], axis=1
    ).astype(bf16)
    dn1, every = matmul_sum(
        [d_qkv, du_qkv], [qkv_full, a_qkv], 4, terms=terms, slots=slots, summed=2 * rank
    )
    dn1 = dn1.astype(f32)
    input_grad = dh1 + norm_back(residual, gains[0], dn1)

    wide_all = every[:, :, : 2 * rank].astype(f32).reshape(slots, 8 * rank, width)
    split_all = every[:, :, 2 * rank :].astype(f32).reshape(slots, 4 * rank, width)
    used = wide_all[:, 7 * rank, 0].astype(jnp.int32)
    select = (used[:, None] == jnp.arange(adapter_count, dtype=jnp.int32)[None, :]).astype(f32)

    def to_adapters(terms):
        return jnp.sum(select[:, :, None, None] * terms[:, None], axis=0)

    share = width // (slots * lax.axis_size("ctx"))
    start = (lax.axis_index("fsdp") * lax.axis_size("ctx") + ctx) * share
    wide_own = to_adapters(lax.dynamic_slice_in_dim(wide_all, start, share, axis=2))
    wide_own = wide_own[:, : 7 * rank].reshape(adapter_count, 7, rank, share)
    split_own = to_adapters(split_all).reshape(adapter_count, 4, rank, hidden)
    grad_a_in = wide_own[:, :5].transpose(1, 0, 3, 2)
    grad_b_out = wide_own[:, 5:].transpose(1, 0, 2, 3)
    small_own = split_own[:, 3]
    grad_b_query = small_own[:, :, :q_cols]
    grad_b_kv = jnp.stack(
        [small_own[:, :, q_cols : q_cols + k_cols], small_own[:, :, q_cols + k_cols : qkv_cols]]
    )
    grad_a_out = small_own[:, :, qkv_cols : qkv_cols + q_cols].transpose(0, 2, 1)
    grad_b_gate_up = split_own[:, :2].transpose(1, 0, 2, 3)
    grad_a_down = split_own[:, 2].transpose(0, 2, 1)
    return (
        final[None],
        input_grad[None],
        grad_a_in,
        grad_b_query,
        grad_b_kv,
        grad_b_gate_up,
        grad_a_out,
        grad_a_down,
        grad_b_out,
    )


def solution(mesh):
    both = ("fsdp", "ctx")
    in_specs = (
        P("fsdp", "ctx", None),
        P("fsdp", "ctx", None),
        P("fsdp"),
        P("fsdp"),
        P(),
        P(both, "tp"),
        P(both, "tp"),
        P(both, "tp"),
        P("tp", both),
        P(both, "tp"),
        P(both, "tp"),
        P("tp", both),
        P(),
        P(None, None, "tp"),
        P(None, None, None, "tp"),
        P(None, None, None, "tp"),
        P(None, "tp", None),
        P(None, "tp", None),
        P(),
    )
    out_specs = (
        P("fsdp", "ctx", None),
        P("fsdp", "ctx", None),
        P(None, None, both, None),
        P(None, None, "tp"),
        P(None, None, None, "tp"),
        P(None, None, None, "tp"),
        P(None, "tp", None),
        P(None, "tp", None),
        P(None, None, None, both),
    )
    return jax.shard_map(
        per_device, mesh=mesh, in_specs=in_specs, out_specs=out_specs, check_vma=False
    )
```

time: 1360 us -> 816 us (0.60)
  waiting for transfers between devices: 732 us -> 79.2 us
  Pallas kernels: 0 us -> 402 us
  matrix products: 353 us -> 166 us
  blocking collectives: 63.5 us -> 0 us
  local copies, waits for them, and re-layouts: 103 us -> 52.3 us
    psum x6 -> x0, waiting for transfers between devices: 472 us -> none  [the longest x1 125 us: per_device(): lax.psum(dn1_part.astype(jnp.bfloat16), 'tp').astype(jnp.float32)]
    pallas_call x0 -> x4, Pallas kernels: none -> 402 us  [matmul_sum(): pl.pallas_call(functools.partial(sum_kernel, len(lefts), width, chunks, s...]
    dot_general x69 -> x39, matrix products: 353 us -> 139 us  [the longest x14 73.5 us: dot_nn(): lax.dot_general(left, right, (((1,), (0,)), ((), ())), preferred_element_...]
    all_gather x9 -> x4, waiting for transfers between devices: 223 us -> 35.1 us  [the longest x1 35.1 us: per_device(): attn_full = lax.all_gather(attn_local, both, axis=0, tiled=True)]
    unnamed x206 -> x202, local copies, waits for them, and re-layouts: 92.2 us -> 16.3 us
    psum x3 -> x0, blocking collectives: 63.5 us -> none  [the longest x1 21.5 us: per_device(): lax.psum(u_out_part.astype(jnp.bfloat16), 'tp').astype(jnp.float32)]
    ppermute x0 -> x4, waiting for transfers between devices: none -> 42.1 us  [swap(): lax.ppermute(values, 'ctx', [(i, i ^ step) for i in range(lax.axis_size('...]
    unnamed x21 -> x4, waiting for transfers between devices: 37.4 us -> 1.91 us
  transfers between devices with their start and end apart: 19 -> 8, of which waited for: 15 -> 3; matrix products, arithmetic and copies ran while one was open for 26% -> 17% of each run, Pallas kernels for 0% -> 12%
where the time goes in v1:
time: 816 us; the launch traced here: 812 us
  Pallas kernels  402 us (49%)
  matrix products  166 us (20%)
  other arithmetic  91.6 us (11%)
  waiting for transfers between devices  79.2 us (10%)
  local copies, waits for them, and re-layouts  52.3 us (6%)
  between operations  16.7 us (2%)
    pallas_call x4, Pallas kernels, matmul_sum(): pl.pallas_call(functools.partial(sum_kernel, len(lefts), width, chunks, s...  402 us
    dot_general x14, matrix products, dot_nn(): lax.dot_general(left, right, (((1,), (0,)), ((), ())), preferred_element_...  73.5 us
    ppermute x4, waiting for transfers between devices, swap(): lax.ppermute(values, 'ctx', [(i, i ^ step) for i in range(lax.axis_size('...  42.1 us
    all_gather x1, waiting for transfers between devices, per_device(): attn_full = lax.all_gather(attn_local, both, axis=0, tiled=True)  35.1 us
    sub x1, matrix products, per_device(): d_raw = (p_back * (d_probs - delta) * slope).astype(bf16)  26.8 us
    reduce_sum x4, other arithmetic, norm_back(): jnp.mean(weighted * unit, axis=-1, keepdims=True)  21.7 us
    dot_general x9, matrix products, dot_nt(): lax.dot_general(left, right, (((1,), (1,)), ((), ())), preferred_element_...  17.2 us
  transfers between devices with their start and end apart: 8, of which 3 were waited for; matrix products, arithmetic and copies ran while one was open for 17% of the time, Pallas kernels for 12%

profile of v1, /device:TPU:0, one launch (start us, length us, event | category | flops | bytes accessed | tf_op | source)
XLA Modules:
  0.0 811.6 jit_solution(2215513089398160306)
XLA Ops:
  7.2 2.2 pad_maximum_fusion.4
  14.1 2.8 fusion.45
  23.5 3.3 convolution_convert_fusion.8
  26.8 35.1 %all-gather.5.cloned.1.call-done = bf16[2304,1536]{1,0:T(8,128)(2,1)} async-done(((bf16[288,1536]{1,0:T(8,128)(2,1)}), bf16[2304,1536]{1,0:T(8,128)(2,1)}) %all-gather.5.cloned.1.call-update) | async-done | bytes 7077904 | tf_op jit(solution)/shard_map/all_gather | solution.py:374
  62.0 7.1 fusion.166
  76.4 2.6 fusion.100
  79.0 27.2 %collective-permute-done = bf16[2,768,256]{2,1,0:T(8,128)(2,1)S(1)} collective-permute-done((bf16[2,768,256]{2,1,0:T(8,128)(2,1)}, bf16[2,768,256]{2,1,0:T(8,128)(2,1)S(1)}, u32[]{:S(2)}, u32[]{:S(2)}) %collective-permute-start) | collective-permute-done | bytes 786464 | tf_op jit(solution)/shard_map/ppermute | solution.py:334
  107.7 2.4 compare_or_fusion
  110.1 2.3 slice_add_fusion
  112.4 3.0 reshape.464
  115.4 3.3 slice.257.refs_2_
  118.8 5.2 slice.244.refs_2_
  129.0 7.7 fusion.111
  136.8 7.7 fusion.2
  144.5 12.0 %fusion.60 = bf16[2,768,256]{1,2,0:T(8,128)(2,1)} fusion(bf16[3072,256,1]{1,0,2:T(8,128)(2,1)S(1)} %bitcast.269, f32[2,768]{1,0:T(2,128)S(1)} %fusion.2, f32[2,768]{1,0:T(2,128)S(1)} %get-tuple-element.78, f32[2,768,3072]{2,1,0:T(8,128)} %copy-done.19, pred[768,3072]{1,0:T(8,128)(4,1)S(1)} %compare_or_fusion), kind=kOutput, calls=%fused_computation.109 | convolution fusion | flops 2444623872 | bytes 23605248 | tf_op jit(solution)/shard_map/gqk,kd->gqd/dot_general | solution.py:430
  156.5 2.3 copy.133.refs_0_
  158.8 2.2 convolution_convert_fusion.7.refs_1_
  161.0 97.1 %matmul_sum_1.1 = bf16[768,2304]{1,0:T(8,128)(2,1)} custom-call(bf16[768,512]{1,0:T(8,128)(2,1)} %copy.133.refs_0_, bf16[768,16]{1,0:T(8,128)(2,1)} %convolution_convert_fusion.7.refs_1_, bf16[2304,512]{1,0:T(8,128)(2,1)} %slice.257.refs_2_, bf16[2304,16]{1,0:T(8,128)(2,1)} %bitcast.264), custom_call_target="tpu_custom_call" | custom-call | flops 1868562432 | bytes 6782976 | tf_op jit(solution)/shard_map/matmul_sum_1/pallas_call | solution.py:318
  258.2 3.0 fusion.27
  261.2 5.2 multiply_reduce_fusion.3
  267.1 2.4 multiply_convert_fusion.3
  273.1 11.9 %fusion.173 = f32[768,2304]{1,0:T(8,128)S(1)} fusion(bf16[768,2304]{1,0:T(8,128)(2,1)} %copy-done.11, bf16[2304,2304]{1,0:T(8,128)(2,1)} %all-gather.7.cloned.1.call-done.refs_3_), kind=kOutput, calls=%fused_computation.293 | convolution fusion | flops 8153726976 | bytes 21233664 | tf_op jit(solution)/shard_map/dot_general | solution.py:44
  285.0 4.1 convolution_add_fusion.2
  289.1 12.0 %fusion.174 = f32[768,2304]{1,0:T(8,128)S(1)} fusion(bf16[768,2304]{1,0:T(8,128)(2,1)} %copy-done.11, bf16[2304,2304]{1,0:T(8,128)(2,1)} %all-gather.9.cloned.1.call-done.refs_4_), kind=kOutput, calls=%fused_computation.294 | convolution fusion | flops 8153726976 | bytes 21233664 | tf_op jit(solution)/shard_map/dot_general | solution.py:44
  301.1 4.9 multiply_convert_fusion.2
  307.7 2.6 fusion.107.refs_1_
  310.3 98.2 %matmul_sum_2.1 = bf16[768,2304]{1,0:T(8,128)(2,1)} custom-call(bf16[768,2304]{1,0:T(8,128)(2,1)} %copy-done.20, bf16[768,16]{1,0:T(8,128)(2,1)} %fusion.107.refs_1_, bf16[2304,2304]{1,0:T(8,128)(2,1)} %all-gather.11.cloned.1.call-done.refs_2_, bf16[2304,16]{1,0:T(8,128)(2,1)} %bitcast.274), custom_call_target="tpu_custom_call" | custom-call | flops 8210350080 | bytes 17793024 | tf_op jit(solution)/shard_map/matmul_sum_2/pallas_call | solution.py:318
  408.6 2.9 fusion.31
  411.5 4.7 fusion.30
  419.5 15.2 %fusion.175 = f32[768,2304]{1,0:T(8,128)} fusion(bf16[768,2304]{1,0:T(8,128)(2,1)S(1)} %fusion.22, bf16[2304,2304]{1,0:T(8,128)(2,1)} %all-gather.11.cloned.1.call-done.refs_2_), kind=kOutput, calls=%fused_computation.295 | convolution fusion | flops 8153726976 | bytes 21233664 | tf_op jit(solution)/shard_map/dot_general | solution.py:44
  434.7 9.1 %multiply_convert_fusion.1 = (bf16[768,2304]{1,0:T(8,128)(2,1)S(1)}, bf16[768,2304]{1,0:T(8,128)(2,1)S(1)}) fusion(f32[768,2304]{1,0:T(8,128)S(1)} %bitcast.245, f32[768,2304]{1,0:T(8,128)} %get-tuple-element.81, f32[768,2304]{1,0:T(8,128)} %fusion.175, bf16[768,16]{0,1:T(8,128)(2,1)S(1)} %convolution_convert_fusion.14, bf16[8,2304,16]{1,2,0:T(8,128)(2,1)} %param.36, ...), kind=kOutput, calls=%fused_computation.66 | convolution fusion | flops 100859904 | bytes 28409860 | tf_op jit(solution)/shard_map/dot_general | solution.py:48
  448.3 101.0 %matmul_sum_3.1 = bf16[768,2304]{1,0:T(8,128)(2,1)} custom-call(bf16[768,2304]{1,0:T(8,128)(2,1)} %copy-done.15, bf16[768,2304]{1,0:T(8,128)(2,1)} %copy-done.17, bf16[768,32]{1,0:T(8,128)(2,1)} %copy.107.refs_2_, bf16[2304,2304]{1,0:T(8,128)(2,1)} %all-gather.7.cloned.1.call-done.refs_3_, bf16[2304,2304]{1,0:T(8,128)(2,1)} %all-gather.9.cloned.1.call-done.refs_4_, ...), custom_call_target="tpu_custom_call" | custom-call | flops 16420700160 | bytes 32047104 | tf_op jit(solution)/shard_map/matmul_sum_3/pallas_call | solution.py:318
  549.3 6.5 multiply_reduce_fusion.2
  556.5 5.9 fusion.23
  562.5 4.9 fusion.26
  568.4 4.0 fusion.164
  574.7 26.8 %multiply_convert_fusion = bf16[2,768,3072]{2,1,0:T(8,128)(2,1)} fusion(f32[2,768,3072]{2,1,0:T(8,128)} %copy-done.19, f32[2,768]{1,0:T(2,128)S(1)} %copy-done.91, bf16[3072,256,1]{1,0,2:T(8,128)(2,1)} %bitcast.268, bf16[768,2,256]{2,0,1:T(8,128)(2,1)} %copy.109, pred[768,3072]{1,0:T(8,128)(4,1)S(1)} %compare_or_fusion), kind=kOutput, calls=%fused_computation.1 | convolution fusion | flops 4902621696 | bytes 33036288 | tf_op jit(solution)/shard_map/sub | solution.py:467
  601.6 11.1 %fusion.9 = f32[3072,256,1]{1,0,2:T(8,128)S(1)} fusion(f32[2,768]{1,0:T(2,128)S(1)} %copy-done.91, bf16[768,2,256]{2,0,1:T(8,128)(2,1)S(1)} %copy-done.39, f32[2,768,3072]{2,1,0:T(8,128)} %copy-done.19, pred[768,3072]{1,0:T(8,128)(4,1)S(1)} %compare_or_fusion), kind=kOutput, calls=%fused_computation.19 | convolution fusion | flops 2439512064 | bytes 25171968 | tf_op jit(solution)/shard_map/gqk,gqd->kd/dot_general | solution.py:470
  612.7 3.0 fusion.122
  617.2 2.8 convolution_bitcast_fusion
  623.3 2.3 collective-permute-start.3
  627.9 14.9 %collective-permute-done.3 = bf16[2,768,256]{2,1,0:T(8,128)(2,1)S(1)} collective-permute-done((bf16[2,768,256]{2,1,0:T(8,128)(2,1)S(1)}, bf16[2,768,256]{2,1,0:T(8,128)(2,1)S(1)}, u32[]{:S(2)}, u32[]{:S(2)}) %collective-permute-start.3) | collective-permute-done | bytes 786464 | tf_op jit(solution)/shard_map/ppermute | solution.py:334
  650.6 2.7 fusion.48
  653.3 2.6 fusion.50
  655.9 2.6 fusion.49
  659.6 105.9 %matmul_sum_4.1 = (bf16[768,2304]{1,0:T(8,128)(2,1)}, bf16[2,4,48,2304]{3,2,1,0:T(8,128)(2,1)}) custom-call(bf16[768,1024]{1,0:T(8,128)(2,1)} %pad_maximum_fusion.3.refs_0_, bf16[768,48]{1,0:T(8,128)(2,1)} %copy.115.refs_1_, bf16[2304,1024]{1,0:T(8,128)(2,1)} %slice.244.refs_2_, bf16[2304,48]{1,0:T(8,128)(2,1)} %copy.116.refs_3_, ...), custom_call_target="tpu_custom_call" | custom-call | flops 3793747968 | bytes 10125312 | tf_op jit(solution)/shard_map/matmul_sum_4/pallas_call | solution.py:318
  781.2 4.6 fusion.33
  785.9 14.8 %fusion.37 = (f32[1,768,2304]{2,1,0:T(8,128)}, bf16[1,768,2304]{2,1,0:T(8,128)(2,1)}) fusion(bf16[768,2304]{1,0:T(8,128)(2,1)} %get-tuple-element.11, bf16[1,768,2304]{2,1,0:T(8,128)(2,1)} %param.19, f32[768]{0:T(1024)S(1)} %broadcast_multiply_fusion, f32[2304]{0:T(1024)S(1)} %copy-done.76, f32[768]{0:T(1024)S(1)} %copy-done.86, f32[768]{0:T(1024)S(1)} %copy-done.83, ...), kind=kLoop, calls=%fused_computation.54 | loop fusion | flops 44236800 | bytes 31905792 | tf_op jit(solution)/shard_map/broadcast_in_dim | solution.py:548
  (311 shorter events, 76.5 us)
Async XLA Ops:
  7.2 277.8 %copy-start = (bf16[2,8,16,2304]{3,2,1,0:T(8,128)(2,1)S(1)}, bf16[2,8,16,2304]{3,2,1,0:T(8,128)(2,1)}, u32[]{:S(2)}) copy-start(bf16[2,8,16,2304]{3,2,1,0:T(8,128)(2,1)} %param.34) | copy-start | bytes 3538948
  7.2 54.8 %all-gather.5.cloned.1.call-start = ((), (), s32[]{:S(2)}) async-start(), calls=%async_computation | async-start | bytes 7962624 | tf_op jit(solution)/shard_map/all_gather | solution.py:374
  9.5 263.6 %all-gather.7.cloned.1.call-start = ((), (), s32[]{:S(2)}) async-start(), calls=%async_computation.1 | async-start | bytes 11943936 | tf_op jit(solution)/shard_map/all_gather | solution.py:375
  10.3 278.8 %all-gather.9.cloned.1.call-start = ((), (), s32[]{:S(2)}) async-start(), calls=%async_computation.2 | async-start | bytes 11943936 | tf_op jit(solution)/shard_map/all_gather | solution.py:376
  11.0 299.3 %all-gather.11.cloned.1.call-start = ((), (), s32[]{:S(2)}) async-start(), calls=%async_computation.3 | async-start | bytes 11943936 | tf_op jit(solution)/shard_map/all_gather | solution.py:377
  11.6 64.8 %copy-start.92 = (f32[128]{0:T(128)}, f32[128]{0:T(128)S(1)}, u32[]{:S(2)}) copy-start(f32[128]{0:T(128)S(1)} %multiply_exponential_fusion) | copy-start | bytes 1540
  11.8 64.6 %copy-start.77 = (s32[3072]{0:T(1024)}, s32[3072]{0:T(1024)S(1)}, u32[]{:S(2)}) copy-start(s32[3072]{0:T(1024)S(1)} %add.169) | copy-start | bytes 36868
  14.1 47.9 %copy-start.74 = (f32[2304]{0:T(1024)}, f32[2304]{0:T(1024)S(1)}, u32[]{:S(2)}) copy-start(f32[2304]{0:T(1024)S(1)} %get-tuple-element.42) | copy-start | bytes 27652
  16.8 45.1 %copy-start.84 = (f32[768]{0:T(1024)}, f32[768]{0:T(1024)S(1)}, u32[]{:S(2)}) copy-start(f32[768]{0:T(1024)S(1)} %add_rsqrt_fusion.3) | copy-start | bytes 9220
  17.5 58.9 %copy-start.80 = (f32[768]{0:T(1024)}, f32[768]{0:T(1024)S(1)}, u32[]{:S(2)}) copy-start(f32[768]{0:T(1024)S(1)} %fusion.148) | copy-start | bytes 9220
  18.5 8.3 %copy-start.46 = (bf16[1,1,16,2304]{3,2,1,0:T(8,128)(2,1)}, bf16[1,1,16,2304]{3,2,1,0:T(8,128)(2,1)S(1)}, u32[]{:S(2)}) copy-start(bf16[1,1,16,2304]{3,2,1,0:T(8,128)(2,1)S(1)} %get-tuple-element.68) | copy-start | bytes 221188
  18.5 8.3 %copy-start.48 = (bf16[1,1,16,2304]{3,2,1,0:T(8,128)(2,1)}, bf16[1,1,16,2304]{3,2,1,0:T(8,128)(2,1)S(1)}, u32[]{:S(2)}) copy-start(bf16[1,1,16,2304]{3,2,1,0:T(8,128)(2,1)S(1)} %get-tuple-element.67) | copy-start | bytes 221188
  26.8 43.3 %copy-start.64 = (bf16[768,48]{0,1:T(8,128)(2,1)}, bf16[768,48]{0,1:T(8,128)(2,1)S(1)}, u32[]{:S(2)}) copy-start(bf16[768,48]{0,1:T(8,128)(2,1)S(1)} %convolution_convert_fusion.8) | copy-start | bytes 221188
  74.0 33.6 %copy-start.23 = (bf16[1,2,768,256]{3,2,1,0:T(8,128)(2,1)}, bf16[1,2,768,256]{3,2,1,0:T(8,128)(2,1)S(1)}, u32[]{:S(2)}) copy-start(bf16[1,2,768,256]{3,2,1,0:T(8,128)(2,1)S(1)} %get-tuple-element.73) | copy-start | bytes 2359300
  74.0 32.2 %collective-permute-start = (bf16[2,768,256]{2,1,0:T(8,128)(2,1)}, bf16[2,768,256]{2,1,0:T(8,128)(2,1)S(1)}, u32[]{:S(2)}, u32[]{:S(2)}) collective-permute-start(bf16[2,768,256]{2,1,0:T(8,128)(2,1)} %get-tuple-element.74), channel_id=1, source_target_pairs={{0,8},{4,12},{8,0},{12,4},{1,9},{5,13},{9,1},{13,5},{2,10},{6,14},... | collective-permute-start | bytes 2359304 | tf_op jit(solution)/shard_map/ppermute | solution.py:334
  76.4 33.7 %copy-start.32 = (f32[768,1024]{1,0:T(8,128)S(1)}, f32[768,1024]{1,0:T(8,128)}, u32[]{:S(2)}) copy-start(f32[768,1024]{1,0:T(8,128)} %copy-done.31) | copy-start | bytes 9437188
  107.7 18.3 %collective-permute-start.1 = (bf16[2,2,768,256]{3,2,1,0:T(8,128)(2,1)}, bf16[2,2,768,256]{3,2,1,0:T(8,128)(2,1)}, u32[]{:S(2)}, u32[]{:S(2)}) collective-permute-start(bf16[2,2,768,256]{3,2,1,0:T(8,128)(2,1)} %pad_maximum_fusion.2), channel_id=1, source_target_pairs={{0,4},{4,0},{8,12},{12,8},{1,5},{5,1},{9,13},{13,9},{2,6},{6,2},{1... | collective-permute-start | bytes 4718600 | tf_op jit(solution)/shard_map/ppermute | solution.py:334
  115.4 8.5 %copy-start.25 = (f32[768,2,256]{2,1,0:T(2,128)S(1)}, f32[768,2,256]{2,1,0:T(2,128)}, u32[]{:S(2)}) copy-start(f32[768,2,256]{2,1,0:T(2,128)} %reshape.464) | copy-start | bytes 4718596
  129.0 7.7 copy-start.34
  136.7 7.7 copy-start.87
  144.5 12.1 %copy-start.89 = (f32[2,768]{1,0:T(2,128)}, f32[2,768]{1,0:T(2,128)S(1)}, u32[]{:S(2)}) copy-start(f32[2,768]{1,0:T(2,128)S(1)} %fusion.2) | copy-start | bytes 18436
  258.2 8.3 %copy-start.88 = (f32[2,768]{1,0:T(2,128)S(1)}, f32[2,768]{1,0:T(2,128)}, u32[]{:S(2)}) copy-start(f32[2,768]{1,0:T(2,128)} %copy-done.87) | copy-start | bytes 18436
  258.2 8.3 %copy-start.90 = (f32[2,768]{1,0:T(2,128)S(1)}, f32[2,768]{1,0:T(2,128)}, u32[]{:S(2)}) copy-start(f32[2,768]{1,0:T(2,128)} %copy-done.89) | copy-start | bytes 18436
  258.2 8.9 %copy-start.2 = (bf16[1,768,2304]{2,1,0:T(8,128)(2,1)S(1)}, bf16[1,768,2304]{2,1,0:T(8,128)(2,1)}, u32[]{:S(2)}) copy-start(bf16[1,768,2304]{2,1,0:T(8,128)(2,1)} %param.19) | copy-start | bytes 10616836
  258.2 8.9 %copy-start.5 = (bf16[768,2304]{1,0:T(8,128)(2,1)S(1)}, bf16[768,2304]{1,0:T(8,128)(2,1)}, u32[]{:S(2)}) copy-start(bf16[768,2304]{1,0:T(8,128)(2,1)} %matmul_sum_1.1) | copy-start | bytes 10616836
  258.2 8.9 %copy-start.55 = (f32[2304]{0:T(1024)S(1)}, f32[2304]{0:T(1024)}, u32[]{:S(2)}) copy-start(f32[2304]{0:T(1024)} %get-tuple-element.43) | copy-start | bytes 27652
  273.1 11.9 %copy-start.50 = (bf16[768,32]{0,1:T(8,128)(2,1)S(1)}, bf16[768,32]{0,1:T(8,128)(2,1)}, u32[]{:S(2)}) copy-start(bf16[768,32]{0,1:T(8,128)(2,1)} %convolution_convert_fusion.9) | copy-start | bytes 147460
  289.1 12.0 %copy-start.14 = (f32[768,2304]{1,0:T(8,128)S(1)}, f32[768,2304]{1,0:T(8,128)}, u32[]{:S(2)}) copy-start(f32[768,2304]{1,0:T(8,128)} %convolution_add_fusion.2) | copy-start | bytes 21233668
  289.1 12.0 %copy-start.51 = (bf16[768,32]{0,1:T(8,128)(2,1)S(1)}, bf16[768,32]{0,1:T(8,128)(2,1)}, u32[]{:S(2)}) copy-start(bf16[768,32]{0,1:T(8,128)(2,1)} %convolution_convert_fusion.9) | copy-start | bytes 147460
  310.3 101.2 %copy-start.66 = (f32[2304]{0:T(1024)S(1)}, f32[2304]{0:T(1024)}, u32[]{:S(2)}) copy-start(f32[2304]{0:T(1024)} %get-tuple-element.40) | copy-start | bytes 27652
  418.4 16.3 %copy-start.12 = (bf16[768,2304]{1,0:T(8,128)(2,1)}, bf16[768,2304]{1,0:T(8,128)(2,1)S(1)}, u32[]{:S(2)}) copy-start(bf16[768,2304]{1,0:T(8,128)(2,1)S(1)} %fusion.22) | copy-start | bytes 10616836
  418.4 16.3 %slice-start = ((s8[7077888]{0:T(1024)(128)(4,1)}), s8[4194304]{0:T(1024)(128)(4,1)S(1)}, s32[]{:S(2)}) async-start(s8[7077888]{0:T(1024)(128)(4,1)} %bitcast.244), calls=%async_computation.4 | async-start | bytes 8388608
  419.5 15.2 %copy-start.72 = (bf16[768,16]{0,1:T(8,128)(2,1)}, bf16[768,16]{0,1:T(8,128)(2,1)S(1)}, u32[]{:S(2)}) copy-start(bf16[768,16]{0,1:T(8,128)(2,1)S(1)} %convolution_convert_fusion.14) | copy-start | bytes 73732
  419.5 15.2 %slice-start.1 = ((s8[7077888]{0:T(1024)(128)(4,1)}), s8[2883584]{0:T(1024)(128)(4,1)S(1)}, s32[]{:S(2)}) async-start(s8[7077888]{0:T(1024)(128)(4,1)} %bitcast.244), calls=%async_computation.5 | async-start | bytes 5767168
  448.3 101.0 %copy-start.56 = (f32[2304]{0:T(1024)S(1)}, f32[2304]{0:T(1024)}, u32[]{:S(2)}) copy-start(f32[2304]{0:T(1024)} %get-tuple-element.43) | copy-start | bytes 27652
  448.3 101.0 %copy-start.70 = (f32[768]{0:T(1024)S(1)}, f32[768]{0:T(1024)}, u32[]{:S(2)}) copy-start(f32[768]{0:T(1024)} %copy-done.69) | copy-start | bytes 9220
  574.7 26.8 %copy-start.39 = (bf16[768,2,256]{2,0,1:T(8,128)(2,1)S(1)}, bf16[768,2,256]{2,0,1:T(8,128)(2,1)}, u32[]{:S(2)}) copy-start(bf16[768,2,256]{2,0,1:T(8,128)(2,1)} %copy.109) | copy-start | bytes 2359300
  601.5 11.1 %copy-start.40 = (f32[768,2,128]{2,0,1:T(8,128)S(1)}, f32[768,2,128]{2,0,1:T(8,128)}, u32[]{:S(2)}) copy-start(f32[768,2,128]{2,0,1:T(8,128)} %get-tuple-element.59) | copy-start | bytes 2359300
  601.5 11.1 %copy-start.41 = (f32[768,2,128]{2,0,1:T(8,128)S(1)}, f32[768,2,128]{2,0,1:T(8,128)}, u32[]{:S(2)}) copy-start(f32[768,2,128]{2,0,1:T(8,128)} %get-tuple-element.60) | copy-start | bytes 2359300
  601.6 11.1 %copy-start.95 = (bf16[2,768,3072]{2,1,0:T(8,128)(2,1)S(1)}, bf16[2,768,3072]{2,1,0:T(8,128)(2,1)}, u32[]{:S(2)}) copy-start(bf16[2,768,3072]{2,1,0:T(8,128)(2,1)} %multiply_convert_fusion) | copy-start | bytes 28311556
  616.0 6.9 collective-permute-start.2
  623.3 19.5 %collective-permute-start.3 = (bf16[2,768,256]{2,1,0:T(8,128)(2,1)S(1)}, bf16[2,768,256]{2,1,0:T(8,128)(2,1)S(1)}, u32[]{:S(2)}, u32[]{:S(2)}) collective-permute-start(bf16[2,768,256]{2,1,0:T(8,128)(2,1)S(1)} %fusion.66), channel_id=1, source_target_pairs={{0,8},{4,12},{8,0},{12,4},{1,9},{5,13},{9,1},{13,5},{2,10},{6,14},... | collective-permute-start | bytes 2359304 | tf_op jit(solution)/shard_map/ppermute | solution.py:334
  626.7 17.5 %copy-start.81 = (f32[768]{0:T(1024)S(1)}, f32[768]{0:T(1024)}, u32[]{:S(2)}) copy-start(f32[768]{0:T(1024)} %copy-done.80) | copy-start | bytes 9220
  626.7 17.5 %copy-start.93 = (f32[128]{0:T(128)S(1)}, f32[128]{0:T(128)}, u32[]{:S(2)}) copy-start(f32[128]{0:T(128)} %copy-done.92) | copy-start | bytes 1540
  627.3 19.9 %copy-start.4 = (bf16[1,768,2304]{2,1,0:T(8,128)(2,1)S(1)}, bf16[1,768,2304]{2,1,0:T(8,128)(2,1)}, u32[]{:S(2)}) copy-start(bf16[1,768,2304]{2,1,0:T(8,128)(2,1)} %param.19) | copy-start | bytes 10616836
  627.3 20.0 %copy-start.75 = (f32[2304]{0:T(1024)S(1)}, f32[2304]{0:T(1024)}, u32[]{:S(2)}) copy-start(f32[2304]{0:T(1024)} %copy-done.74) | copy-start | bytes 27652
  627.3 19.9 %copy-start.85 = (f32[768]{0:T(1024)S(1)}, f32[768]{0:T(1024)}, u32[]{:S(2)}) copy-start(f32[768]{0:T(1024)} %copy-done.84) | copy-start | bytes 9220
  785.9 18.9 %copy-start.1 = (bf16[2,8,16,2304]{3,2,1,0:T(8,128)(2,1)S(1)}, bf16[2,8,16,2304]{3,2,1,0:T(8,128)(2,1)}, u32[]{:S(2)}) copy-start(bf16[2,8,16,2304]{3,2,1,0:T(8,128)(2,1)} %param.34) | copy-start | bytes 3538948
  (58 other events, 266.1 us)
Sparse Core Ops, SparseCore 0:
  10.5 51.4 all-gather.4
  63.8 76.0 all-gather.6
  141.8 63.6 all-gather.8
  207.3 63.6 all-gather.10

commit v2 on v1

--- a/solution.py
+++ b/solution.py
@@ -330,6 +330,355 @@
     return result if slots else result[0]
 
 
+def ffn_kernel(
+    n2_all,
+    cot_all,
+    u_gu,
+    gain,
+    b_gate,
+    a_down,
+    b_down,
+    a_gu,
+    gate_all,
+    up_all,
+    down_all,
+    y_all,
+    dn2_all,
+    act_all,
+    e_all,
+    dg_all,
+    du_all,
+    w_gate,
+    w_up,
+    w_down,
+    n2_buf,
+    cot_buf,
+    act_buf,
+    e_buf,
+    dg_buf,
+    du_buf,
+    keep_up,
+    keep_gate,
+    part,
+    mine,
+    got_a,
+    got_b,
+    total,
+    load_sem,
+    in_sem,
+    out_sem,
+    a_send,
+    a_recv,
+    b_send,
+    b_recv,
+    c_send,
+    c_recv,
+):
+    n, rows, width = n2_all.shape
+    ring = mine.shape[0]
+    rank = b_down.shape[0]
+    tile = width // 3
+    z = lax.axis_index("tp")
+    inner = (z == 1) | (z == 2)
+    outer = (z == 0) | (z == 3)
+    pair = z + 1 - 2 * lax.rem(z, 2)
+    across = 3 - z
+
+    weights = [
+        pltpu.make_async_copy(source, target, load_sem.at[i])
+        for i, (source, target) in enumerate(
+            ((gate_all, w_gate), (up_all, w_up), (down_all, w_down))
+        )
+    ]
+
+    def n2_copy(c):
+        return pltpu.make_async_copy(n2_all.at[c], n2_buf.at[lax.rem(c, 2)], in_sem.at[lax.rem(c, 2)])
+
+    def cot_copy(c):
+        slot = lax.rem(c, 2)
+        return pltpu.make_async_copy(cot_all.at[c], cot_buf.at[slot], in_sem.at[2 + slot])
+
+    n2_copy(0).start()
+    for copy in weights:
+        copy.start()
+    n2_copy(1).start()
+    cot_copy(0).start()
+    cot_copy(1).start()
+
+    barrier = pltpu.get_barrier_semaphore()
+    pl.semaphore_signal(barrier, inc=1, device_id={"tp": pair}, device_id_type=MESH)
+
+    @pl.when(inner)
+    def _():
+        pl.semaphore_signal(barrier, inc=1, device_id={"tp": across}, device_id_type=MESH)
+        pl.semaphore_wait(barrier, 2)
+
+    @pl.when(outer)
+    def _():
+        pl.semaphore_wait(barrier, 1)
+
+    def remote(source, target, send, recv, peer):
+        return pltpu.make_async_remote_copy(
+            source, target, send, recv, device_id={"tp": peer}, device_id_type=MESH
+        )
+
+    def copy_a(k):
+        slot = lax.rem(k, ring)
+        return remote(mine.at[slot], got_a.at[slot], a_send.at[k], a_recv.at[k], pair)
+
+    def copy_b(k):
+        slot = lax.rem(k, ring)
+        return remote(mine.at[slot], got_b.at[slot], b_send.at[k], b_recv.at[k], across)
+
+    def copy_c(k):
+        place = total.at[lax.rem(k, n)]
+        return remote(place, place, c_send.at[k], c_recv.at[k], pair)
+
+    def finish(k):
+        slot = lax.rem(k, ring)
+        copy_b(k).wait_recv()
+        total[lax.rem(k, n)] = (mine[slot].astype(f32) + got_b[slot].astype(f32)).astype(bf16)
+        copy_c(k).start()
+
+    def exchange(k):
+        slot = lax.rem(k, ring)
+
+        @pl.when(outer & (k >= ring))
+        def _():
+            copy_c(k - ring).wait_recv()
+            copy_a(k - ring).wait_send()
+
+        @pl.when(outer)
+        def _():
+            mine[slot] = part[...].astype(bf16)
+            copy_a(k).start()
+
+        @pl.when(inner & (k >= ring))
+        def _():
+            copy_b(k - ring).wait_send()
+
+        @pl.when(inner)
+        def _():
+            copy_a(k).wait_recv()
+            mine[slot] = (part[...] + got_a[slot].astype(f32)).astype(bf16)
+            copy_b(k).start()
+
+        @pl.when(inner & (k >= n + 1))
+        def _():
+            copy_c(k - 1 - n).wait_send()
+
+        @pl.when(inner & (k >= 1))
+        def _():
+            finish(k - 1)
+
+    def put(i, buf, target, c):
+        return pltpu.make_async_copy(buf, target.at[c], out_sem.at[i])
+
+    def act_out(c):
+        return put(0, act_buf, act_all, c)
+
+    def forward(k, carry):
+        n2_copy(k).wait()
+
+        @pl.when(k == 0)
+        def _():
+            weights[0].wait()
+            weights[1].wait()
+
+        @pl.when(k >= 1)
+        def _():
+            act_out(k - 1).wait()
+
+        slot = lax.rem(k, 2)
+        u_here = u_gu[k]
+        for i in range(3):
+            cols = slice(i * tile, (i + 1) * tile)
+            gate = dot_nn(n2_buf[slot], w_gate[:, cols]) + dot_nn(u_here[:, :rank], b_gate[0, :, cols])
+            upper = dot_nn(n2_buf[slot], w_up[:, cols]) + dot_nn(u_here[:, rank:], b_gate[1, :, cols])
+            square = gate * gate
+            slant = math.sqrt(2.0 / math.pi)
+            bend = jnp.tanh(slant * (gate + 0.044715 * (square * gate)))
+            side = 0.5 * (1.0 + bend)
+            curve = gate * side
+            rise = side + 0.5 * gate * (1.0 - bend * bend) * (
+                slant * (1.0 + 3.0 * 0.044715 * square)
+            )
+            act_buf[:, cols] = (curve * upper).astype(bf16)
+            keep_up[k, :, cols] = curve.astype(bf16)
+            keep_gate[k, :, cols] = (rise * upper).astype(bf16)
+
+        @pl.when(k + 2 < n)
+        def _():
+            n2_copy(k + 2).start()
+
+        act_out(k).start()
+
+        @pl.when(k == 0)
+        def _():
+            weights[2].wait()
+
+        u_down = dot_nt(act_buf[...], a_down[...]).astype(bf16)
+        for i in range(3):
+            cols = slice(i * tile, (i + 1) * tile)
+            part[:, cols] = dot_nt(act_buf[...], w_down[cols, :]) + dot_nn(u_down, b_down[:, cols])
+        exchange(k)
+        return carry
+
+    def back_out(i, c):
+        if i == 0:
+            return put(1, e_buf, e_all, c)
+        if i == 1:
+            return put(2, dg_buf, dg_all, c)
+        if i == 2:
+            return put(3, du_buf, du_all, c)
+        return put(4, total.at[c], y_all, c)
+
+    def backward(c, carry):
+        cot_copy(c).wait()
+        back_out(3, c).start()
+
+        @pl.when(c >= 1)
+        def _():
+            for i in range(3):
+                back_out(i, c - 1).wait()
+
+        slot = lax.rem(c, 2)
+
+        def norm(i, inside):
+            lines = pl.ds(pl.multiple_of(i * 16, 16), 16)
+            values = total[c, lines, :].astype(f32)
+            scale = lax.rsqrt(jnp.mean(values * values, axis=-1, keepdims=True) + epsilon)
+            unit = values * scale
+            weighted = cot_buf[slot, lines, :].astype(f32) * gain[...]
+            e_buf[lines, :] = (
+                scale * (weighted - unit * jnp.mean(weighted * unit, axis=-1, keepdims=True))
+            ).astype(bf16)
+            return inside
+
+        lax.fori_loop(0, rows // 16, norm, 0)
+
+        @pl.when(c + 2 < n)
+        def _():
+            cot_copy(c + 2).start()
+
+        back_out(0, c).start()
+        du_down = dot_nt(e_buf[...], b_down[...]).astype(bf16)
+        for i in range(3):
+            cols = slice(i * tile, (i + 1) * tile)
+            d_act = dot_nn(e_buf[...], w_down[:, cols]) + dot_nn(du_down, a_down[:, cols])
+            dg_buf[:, cols] = (d_act * keep_gate[c, :, cols].astype(f32)).astype(bf16)
+            du_buf[:, cols] = (d_act * keep_up[c, :, cols].astype(f32)).astype(bf16)
+        back_out(1, c).start()
+        back_out(2, c).start()
+        du_gate = dot_nt(dg_buf[...], b_gate[0]).astype(bf16)
+        du_up = dot_nt(du_buf[...], b_gate[1]).astype(bf16)
+        for i in range(3):
+            cols = slice(i * tile, (i + 1) * tile)
+            part[:, cols] = (
+                dot_nt(dg_buf[...], w_gate[cols, :])
+                + dot_nt(du_buf[...], w_up[cols, :])
+                + dot_nn(du_gate, a_gu[0, :, cols])
+                + dot_nn(du_up, a_gu[1, :, cols])
+            )
+        back_out(3, c).wait()
+        exchange(n + c)
+        return carry
+
+    def result(c):
+        return pltpu.make_async_copy(total.at[c], dn2_all.at[c], out_sem.at[5 + c])
+
+    lax.fori_loop(0, n, forward, 0)
+    lax.fori_loop(0, n, backward, 0)
+    act_out(n - 1).wait()
+    for i in range(3):
+        back_out(i, n - 1).wait()
+
+    @pl.when(inner)
+    def _():
+        copy_c(n - 1).wait_send()
+        finish(2 * n - 1)
+
+        def drain(k, carry):
+            copy_b(k).wait_send()
+            return carry
+
+        lax.fori_loop(2 * n - ring, 2 * n, drain, 0)
+
+        def drain_c(k, carry):
+            copy_c(k).wait_send()
+            return carry
+
+        lax.fori_loop(n, 2 * n, drain_c, 0)
+
+    @pl.when(outer)
+    def _():
+        def drain(k, carry):
+            copy_c(k).wait_recv()
+            copy_a(k).wait_send()
+            return carry
+
+        lax.fori_loop(2 * n - ring, 2 * n, drain, 0)
+
+    for c in range(n):
+        result(c).start()
+    for c in range(n):
+        result(c).wait()
+
+
+def feed_forward(
+    n2, cot, u_gu, gain, b_gate, a_down, b_down, a_gu, gate_full, up_full, down_full, collective_id
+):
+    rows, width = n2.shape
+    hidden = gate_full.shape[1]
+    assert hidden == width
+    step = 128
+    n = rows // step
+    ring = 4
+    full = jax.ShapeDtypeStruct((n, step, width), bf16)
+    vmem = pl.BlockSpec(memory_space=pltpu.VMEM)
+    anywhere = pl.BlockSpec(memory_space=pl.ANY)
+    block = pltpu.VMEM((step, width), bf16)
+    results = pl.pallas_call(
+        ffn_kernel,
+        out_shape=[full] * 6,
+        in_specs=[anywhere] * 2 + [vmem] * 6 + [anywhere] * 3,
+        out_specs=[anywhere] * 6,
+        scratch_shapes=[pltpu.VMEM((width, width), bf16)] * 3
+        + [pltpu.VMEM((2, step, width), bf16)] * 2
+        + [block] * 4
+        + [pltpu.VMEM((n, step, width), bf16)] * 2
+        + [pltpu.VMEM((step, width), f32)]
+        + [pltpu.VMEM((ring, step, width), bf16)] * 3
+        + [pltpu.VMEM((n, step, width), bf16)]
+        + [
+            pltpu.SemaphoreType.DMA((3,)),
+            pltpu.SemaphoreType.DMA((4,)),
+            pltpu.SemaphoreType.DMA((5 + n,)),
+        ]
+        + [pltpu.SemaphoreType.DMA((2 * n,))] * 6,
+        compiler_params=pltpu.CompilerParams(
+            collective_id=collective_id, has_side_effects=True, vmem_limit_bytes=67043328
+        ),
+        cost_estimate=pl.CostEstimate(
+            flops=12 * rows * width * hidden, bytes_accessed=60 * 2**20, transcendentals=rows * hidden
+        ),
+        name=f"feed_forward_{collective_id}",
+    )(
+        n2.reshape(n, step, width),
+        cot.reshape(n, step, width),
+        u_gu.reshape(n, step, -1),
+        gain,
+        b_gate,
+        a_down,
+        b_down,
+        a_gu,
+        gate_full,
+        up_full,
+        down_full,
+    )
+    return [value.reshape(rows, width) for value in results]
+
+
 def swap(values, step):
     return lax.ppermute(values, "ctx", [(i, i ^ step) for i in range(lax.axis_size("ctx"))])
 
@@ -436,24 +785,28 @@
     h1 = residual + rms_norm(y_att, gains[1])
     n2 = rms_norm(h1, gains[2]).astype(bf16)
     u_gu = dot_nn(n2, a_gu).astype(bf16)
-    gate = dot_nn(n2, gate_full) + dot_nn(u_gu[:, :rank], b_gate[0])
-    upper = dot_nn(n2, up_full) + dot_nn(u_gu[:, rank:], b_gate[1])
-    act = (jax.nn.gelu(gate, approximate=True) * upper).astype(bf16)
+    y_ffn, dn2, act, e_ffn, d_gate, d_up = feed_forward(
+        n2,
+        cotangent[0],
+        u_gu,
+        gains[3][None],
+        b_gate,
+        a_down.T,
+        b_out[1],
+        jnp.stack([a_in[3].T, a_in[4].T]),
+        gate_full,
+        up_full,
+        down_full,
+        2,
+    )
+    y_ffn = y_ffn.astype(f32)
+    dn2 = dn2.astype(f32)
+    final = (h1 + rms_norm(y_ffn, gains[3])).astype(bf16)
     u_down = dot_nn(act, a_down).astype(bf16)
-    y_ffn = matmul_sum([act, u_down], [down_full, b_out[1].T], 2).astype(f32)
-    final = (h1 + rms_norm(y_ffn, gains[3])).astype(bf16)
-
-    e_ffn = norm_back(y_ffn, gains[3], d_final).astype(bf16)
     du_down = dot_nt(e_ffn, b_out[1]).astype(bf16)
-    d_act = dot_nn(e_ffn, down_full) + dot_nt(du_down, a_down)
-    _, gelu_pull = jax.vjp(lambda gin, uin: jax.nn.gelu(gin, approximate=True) * uin, gate, upper)
-    d_gate, d_up = gelu_pull(d_act)
-    d_gate = d_gate.astype(bf16)
-    d_up = d_up.astype(bf16)
     du_gate = dot_nt(d_gate, b_gate[0]).astype(bf16)
     du_up = dot_nt(d_up, b_gate[1]).astype(bf16)
     du_gu = jnp.concatenate([du_gate, du_up], axis=1)
-    dn2 = matmul_sum([d_gate, d_up, du_gu], [gate_full, up_full, a_gu], 3).astype(f32)
     dh1 = d_final + norm_back(h1, gains[2], dn2)
     e_att = norm_back(y_att, gains[1], dh1).astype(bf16)
     du_out = dot_nt(e_att, b_out[0]).astype(bf16)

time: 816 us -> 782 us (0.958)
  matrix products: 166 us -> 125 us
  local copies, waits for them, and re-layouts: 52.3 us -> 66.3 us
  other arithmetic: 91.6 us -> 83.1 us
    pallas_call x0 -> x1, Pallas kernels: none -> 202 us  [feed_forward(): pl.pallas_call(ffn_kernel, out_shape=[full] * 6, in_specs=[anywhere] * 2...]
    pallas_call x4 -> x2, Pallas kernels: 402 us -> 201 us  [matmul_sum(): pl.pallas_call(functools.partial(sum_kernel, len(lefts), width, chunks, s...]
    dot_general x14 -> x8, matrix products: 73.5 us -> 19.3 us  [dot_nn(): lax.dot_general(left, right, (((1,), (0,)), ((), ())), preferred_element_...]
    dot_general x11, matrix products: 11.6 us -> 24.8 us  [dot_tn(): lax.dot_general(left, right, (((0,), (0,)), ((), ())), preferred_element_...]
    reduce_sum x4 -> x3, other arithmetic: 21.7 us -> 16.4 us  [norm_back(): jnp.mean(weighted * unit, axis=-1, keepdims=True)]
    dot_general x9 -> x7, matrix products: 17.2 us -> 13.1 us  [dot_nt(): lax.dot_general(left, right, (((1,), (1,)), ((), ())), preferred_element_...]
  transfers between devices with their start and end apart: 8 -> 8, of which waited for: 3 -> 3; matrix products, arithmetic and copies ran while one was open for 17% -> 15% of each run, Pallas kernels for 12% -> 12%
where the time goes in v2:
time: 782 us; the launch traced here: 770 us
  Pallas kernels  403 us (52%)
  matrix products  125 us (16%)
  other arithmetic  83.1 us (11%)
  waiting for transfers between devices  73.4 us (9%)
  local copies, waits for them, and re-layouts  66.3 us (8%)
  between operations  16.6 us (2%)
    pallas_call x1, Pallas kernels, feed_forward(): pl.pallas_call(ffn_kernel, out_shape=[full] * 6, in_specs=[anywhere] * 2...  202 us
    pallas_call x2, Pallas kernels, matmul_sum(): pl.pallas_call(functools.partial(sum_kernel, len(lefts), width, chunks, s...  201 us
    ppermute x4, waiting for transfers between devices, swap(): lax.ppermute(values, 'ctx', [(i, i ^ step) for i in range(lax.axis_size('...  41.3 us
    all_gather x1, waiting for transfers between devices, per_device(): attn_full = lax.all_gather(attn_local, both, axis=0, tiled=True)  30.2 us
    sub x1, matrix products, per_device(): d_raw = (p_back * (d_probs - delta) * slope).astype(bf16)  28.8 us
    dot_general x11, matrix products, dot_tn(): lax.dot_general(left, right, (((0,), (0,)), ((), ())), preferred_element_...  24.8 us
    dot_general x8, matrix products, dot_nn(): lax.dot_general(left, right, (((1,), (0,)), ((), ())), preferred_element_...  19.3 us
    reduce_sum x3, other arithmetic, norm_back(): jnp.mean(weighted * unit, axis=-1, keepdims=True)  16.4 us
  transfers between devices with their start and end apart: 8, of which 3 were waited for; matrix products, arithmetic and copies ran while one was open for 15% of the time, Pallas kernels for 12%

profile of v2, /device:TPU:0, one launch (start us, length us, event | category | flops | bytes accessed | tf_op | source)
XLA Modules:
  0.0 770.1 jit_solution(2103385209144273051)
XLA Ops:
  7.2 2.2 pad_maximum_fusion.4
  15.9 1.9 copy.101.refs_3_
  20.9 2.0 copy.110.refs_3_
  25.6 2.6 fusion.92
  29.8 1.9 convolution_convert_fusion.8
  31.7 30.2 %all-gather.5.cloned.1.call-done = bf16[2304,1536]{1,0:T(8,128)(2,1)} async-done(((bf16[288,1536]{1,0:T(8,128)(2,1)}), bf16[2304,1536]{1,0:T(8,128)(2,1)}) %all-gather.5.cloned.1.call-update) | async-done | bytes 7077904 | tf_op jit(solution)/shard_map/all_gather | solution.py:723
  61.9 5.8 fusion.159
  75.4 30.4 %collective-permute-done = bf16[2,768,256]{2,1,0:T(8,128)(2,1)S(1)} collective-permute-done((bf16[2,768,256]{2,1,0:T(8,128)(2,1)S(1)}, bf16[2,768,256]{2,1,0:T(8,128)(2,1)S(1)}, u32[]{:S(2)}, u32[]{:S(2)}) %collective-permute-start) | collective-permute-done | bytes 786464 | tf_op jit(solution)/shard_map/ppermute | solution.py:683
  107.3 3.3 compare_or_fusion
  110.6 2.3 slice_add_fusion
  112.9 3.1 reshape.493
  116.0 3.2 slice.255.refs_2_
  119.2 5.2 slice.242.refs_2_
  129.5 8.6 %fusion.102 = (f32[2,768]{1,0:T(2,128)S(1)}, f32[2,768,3072]{2,1,0:T(8,128)S(1)}) fusion(pred[768,3072]{1,0:T(8,128)(4,1)} %compare_or_fusion, bf16[3072,256,1]{1,0,2:T(8,128)(2,1)S(1)} %bitcast.294, f32[768,2,128]{2,0,1:T(8,128)} %get-tuple-element.72, f32[768,2,128]{2,0,1:T(8,128)} %get-tuple-element.71), kind=kOutput, calls=%fused_computation.190 | convolution fusion | flops 2435971584 | bytes 24385536 | tf_op jit(solution)/shard_map/gqd,kd->gqk/dot_general | solution.py:773
  138.1 8.8 %fusion.2 = f32[2,768]{1,0:T(2,128)S(1)} fusion(f32[2,768]{1,0:T(2,128)S(1)} %get-tuple-element.91, f32[2,768,3072]{2,1,0:T(8,128)S(1)} %get-tuple-element.92, pred[768,3072]{1,0:T(8,128)(4,1)} %compare_or_fusion), kind=kLoop, calls=%fused_computation.9 | loop fusion | flops 23591424 | bytes 21245952 | tf_op jit(solution)/shard_map/reduce_sum | solution.py:777
  147.0 13.3 %fusion.49 = bf16[2,768,256]{1,2,0:T(8,128)(2,1)} fusion(bf16[3072,256,1]{1,0,2:T(8,128)(2,1)S(1)} %bitcast.297, f32[2,768]{1,0:T(2,128)S(1)} %fusion.2, f32[2,768]{1,0:T(2,128)S(1)} %get-tuple-element.91, f32[2,768,3072]{2,1,0:T(8,128)} %copy-done.14, pred[768,3072]{1,0:T(8,128)(4,1)} %compare_or_fusion), kind=kOutput, calls=%fused_computation.87 | convolution fusion | flops 2444623872 | bytes 23605248 | tf_op jit(solution)/shard_map/gqk,kd->gqd/dot_general | solution.py:779
  160.3 2.3 copy.126.refs_0_
  162.6 2.2 convolution_convert_fusion.7.refs_1_
  164.8 96.1 %matmul_sum_1.1 = bf16[768,2304]{1,0:T(8,128)(2,1)} custom-call(bf16[768,512]{1,0:T(8,128)(2,1)} %copy.126.refs_0_, bf16[768,16]{1,0:T(8,128)(2,1)} %convolution_convert_fusion.7.refs_1_, bf16[2304,512]{1,0:T(8,128)(2,1)} %slice.255.refs_2_, bf16[2304,16]{1,0:T(8,128)(2,1)} %copy.101.refs_3_), custom_call_target="tpu_custom_call" | custom-call | flops 1868562432 | bytes 6782976 | tf_op jit(solution)/shard_map/matmul_sum_1/pallas_call | solution.py:318
  261.0 2.9 fusion.21
  265.9 2.2 multiply_convert_fusion.1
  273.1 201.7 %feed_forward_2.1 = (bf16[6,128,2304]{2,1,0:T(8,128)(2,1)}, bf16[6,128,2304]{2,1,0:T(8,128)(2,1)}, bf16[6,128,2304]{2,1,0:T(8,128)(2,1)}, bf16[6,128,2304]{2,1,0...) custom-call(bf16[6,128,2304]{2,1,0:T(8,128)(2,1)} %bitcast.264, ...), custom_call_target="tpu_custom_call" | custom-call | flops 48922361856 | bytes 62914560 | tf_op jit(solution)/shard_map/feed_forward_2/pallas_call | solution.py:641
  474.9 6.7 fusion.31
  482.1 6.0 fusion.17
  488.1 5.1 fusion.20
  493.3 2.0 convolution_convert_fusion.15
  495.3 3.9 fusion.157
  499.2 2.0 add_convert_fusion
  501.2 2.3 copy.103
  503.5 28.8 %multiply_convert_fusion = bf16[2,768,3072]{2,1,0:T(8,128)(2,1)} fusion(f32[2,768,3072]{2,1,0:T(8,128)} %copy-done.14, f32[2,768]{1,0:T(2,128)} %log_add_fusion, bf16[3072,256,1]{1,0,2:T(8,128)(2,1)} %bitcast.296, bf16[768,2,256]{2,0,1:T(8,128)(2,1)} %copy.103, pred[768,3072]{1,0:T(8,128)(4,1)} %compare_or_fusion), kind=kOutput, calls=%fused_computation.1 | convolution fusion | flops 4902621696 | bytes 33036288 | tf_op jit(solution)/shard_map/sub | solution.py:820
  532.4 11.3 %fusion.9 = f32[3072,256,1]{1,0,2:T(8,128)S(1)} fusion(f32[2,768]{1,0:T(2,128)} %log_add_fusion, bf16[768,2,256]{2,0,1:T(8,128)(2,1)} %copy.103, f32[2,768,3072]{2,1,0:T(8,128)} %copy-done.14, pred[768,3072]{1,0:T(8,128)(4,1)} %compare_or_fusion), kind=kOutput, calls=%fused_computation.17 | convolution fusion | flops 2439512064 | bytes 25171968 | tf_op jit(solution)/shard_map/gqk,gqd->kd/dot_general | solution.py:823
  543.7 3.0 fusion.114
  546.8 2.8 convolution_bitcast_fusion
  552.1 2.0 convolution_convert_fusion.14
  555.9 2.6 convolution_convert_fusion.12
  558.4 2.7 convolution_convert_fusion.13
  567.4 5.7 convolution_convert_fusion.2
  573.1 10.9 %collective-permute-done.3 = bf16[2,768,256]{2,1,0:T(8,128)(2,1)} collective-permute-done((bf16[2,768,256]{2,1,0:T(8,128)(2,1)}, bf16[2,768,256]{2,1,0:T(8,128)(2,1)}, u32[]{:S(2)}, u32[]{:S(2)}) %collective-permute-start.3) | collective-permute-done | bytes 786464 | tf_op jit(solution)/shard_map/ppermute | solution.py:683
  587.6 2.0 fusion.74
  596.9 3.6 fusion.38
  601.7 5.7 fusion.39
  611.9 105.2 %matmul_sum_4.1 = (bf16[768,2304]{1,0:T(8,128)(2,1)}, bf16[2,4,48,2304]{3,2,1,0:T(8,128)(2,1)}) custom-call(bf16[768,1024]{1,0:T(8,128)(2,1)} %pad_maximum_fusion.3.refs_0_, bf16[768,48]{1,0:T(8,128)(2,1)} %copy.109.refs_1_, bf16[2304,1024]{1,0:T(8,128)(2,1)} %slice.242.refs_2_, bf16[2304,48]{1,0:T(8,128)(2,1)} %copy.110.refs_3_, ...), custom_call_target="tpu_custom_call" | custom-call | flops 3793747968 | bytes 10125312 | tf_op jit(solution)/shard_map/matmul_sum_4/pallas_call | solution.py:318
  731.0 2.0 constant_dynamic-slice_fusion
  734.9 2.4 multiply_reduce_fusion.4
  737.2 2.8 copy.113
  742.5 3.7 fusion.23
  747.3 4.0 copy.115
  753.8 9.4 %fusion.27 = (f32[1,768,2304]{2,1,0:T(8,128)}, bf16[768,2304]{1,0:T(8,128)(2,1)}) fusion(bf16[768,2304]{1,0:T(8,128)(2,1)S(1)} %copy-done.15, bf16[1,768,2304]{2,1,0:T(8,128)(2,1)S(1)} %copy-done.1, f32[768]{0:T(1024)S(1)} %broadcast_multiply_fusion, f32[2304]{0:T(1024)S(1)} %copy-done.67, f32[768]{0:T(1024)} %copy-done.75, f32[768]{0:T(1024)S(1)} %copy-done.74, ...), kind=kLoop, calls=%fused_computation.38 | loop fusion | flops 44236800 | bytes 31905792 | tf_op jit(solution)/shard_map/broadcast_in_dim | solution.py:901
  (277 shorter events, 82.5 us)
Async XLA Ops:
  7.2 54.8 %all-gather.5.cloned.1.call-start = ((), (), s32[]{:S(2)}) async-start(), calls=%async_computation | async-start | bytes 7962624 | tf_op jit(solution)/shard_map/all_gather | solution.py:723
  9.4 13.6 %copy-start = (bf16[1,768,2304]{2,1,0:T(8,128)(2,1)S(1)}, bf16[1,768,2304]{2,1,0:T(8,128)(2,1)}, u32[]{:S(2)}) copy-start(bf16[1,768,2304]{2,1,0:T(8,128)(2,1)} %param.19) | copy-start | bytes 10616836
  9.4 263.7 %all-gather.7.cloned.1.call-start = ((), (), s32[]{:S(2)}) async-start(), calls=%async_computation.1 | async-start | bytes 11943936 | tf_op jit(solution)/shard_map/all_gather | solution.py:724
  10.2 263.0 %all-gather.9.cloned.1.call-start = ((), (), s32[]{:S(2)}) async-start(), calls=%async_computation.2 | async-start | bytes 11943936 | tf_op jit(solution)/shard_map/all_gather | solution.py:725
  10.9 262.2 %all-gather.11.cloned.1.call-start = ((), (), s32[]{:S(2)}) async-start(), calls=%async_computation.3 | async-start | bytes 11943936 | tf_op jit(solution)/shard_map/all_gather | solution.py:726
  13.0 10.9 %copy-start.68 = (s32[3072]{0:T(1024)}, s32[3072]{0:T(1024)S(1)}, u32[]{:S(2)}) copy-start(s32[3072]{0:T(1024)S(1)} %add.151) | copy-start | bytes 36868
  23.0 6.8 copy-start.49
  23.0 6.8 copy-start.51
  23.0 45.8 %copy-start.71 = (f32[768]{0:T(1024)}, f32[768]{0:T(1024)S(1)}, u32[]{:S(2)}) copy-start(f32[768]{0:T(1024)S(1)} %fusion.139) | copy-start | bytes 9220
  25.6 240.2 %copy-start.38 = (f32[2304]{0:T(1024)}, f32[2304]{0:T(1024)S(1)}, u32[]{:S(2)}) copy-start(f32[2304]{0:T(1024)S(1)} %get-tuple-element.54) | copy-start | bytes 27652
  61.9 6.9 copy-start.84
  67.8 7.0 copy-start.52
  67.8 7.0 copy-start.53
  70.7 36.6 %copy-start.69 = (s32[3072]{0:T(1024)S(1)}, s32[3072]{0:T(1024)}, u32[]{:S(2)}) copy-start(s32[3072]{0:T(1024)} %copy-done.68) | copy-start | bytes 36868
  70.7 36.6 %copy-start.82 = (pred[3072]{0:T(1024)(128)(4,1)S(1)}, pred[3072]{0:T(1024)(128)(4,1)}, u32[]{:S(2)}) copy-start(pred[3072]{0:T(1024)(128)(4,1)} %broadcast_compare_fusion) | copy-start | bytes 9220
  71.8 34.0 %copy-start.22 = (bf16[1,2,768,256]{3,2,1,0:T(8,128)(2,1)}, bf16[1,2,768,256]{3,2,1,0:T(8,128)(2,1)S(1)}, u32[]{:S(2)}) copy-start(bf16[1,2,768,256]{3,2,1,0:T(8,128)(2,1)S(1)} %get-tuple-element.85) | copy-start | bytes 2359300
  71.9 34.0 %collective-permute-start = (bf16[2,768,256]{2,1,0:T(8,128)(2,1)S(1)}, bf16[2,768,256]{2,1,0:T(8,128)(2,1)S(1)}, u32[]{:S(2)}, u32[]{:S(2)}) collective-permute-start(bf16[2,768,256]{2,1,0:T(8,128)(2,1)S(1)} %get-tuple-element.86), channel_id=1, source_target_pairs={{0,8},{4,12},{8,0},{12,4},{1,9},{5,13},{9,1},{13,5},{2,10},{6,14},... | collective-permute-start | bytes 2359304 | tf_op jit(solution)/shard_map/ppermute | solution.py:683
  107.3 19.1 %collective-permute-start.1 = (bf16[2,2,768,256]{3,2,1,0:T(8,128)(2,1)}, bf16[2,2,768,256]{3,2,1,0:T(8,128)(2,1)}, u32[]{:S(2)}, u32[]{:S(2)}) collective-permute-start(bf16[2,2,768,256]{3,2,1,0:T(8,128)(2,1)} %pad_maximum_fusion.2), channel_id=1, source_target_pairs={{0,4},{4,0},{8,12},{12,8},{1,5},{5,1},{9,13},{13,9},{2,6},{6,2},{1... | collective-permute-start | bytes 4718600 | tf_op jit(solution)/shard_map/ppermute | solution.py:683
  129.5 8.6 %copy-start.31 = (bf16[4,1,768,256]{3,2,1,0:T(8,128)(2,1)}, bf16[4,1,768,256]{3,2,1,0:T(8,128)(2,1)S(1)}, u32[]{:S(2)}) copy-start(bf16[4,1,768,256]{3,2,1,0:T(8,128)(2,1)S(1)} %get-tuple-element.60) | copy-start | bytes 4718596
  138.1 8.9 %copy-start.14 = (f32[2,768,3072]{2,1,0:T(8,128)}, f32[2,768,3072]{2,1,0:T(8,128)S(1)}, u32[]{:S(2)}) copy-start(f32[2,768,3072]{2,1,0:T(8,128)S(1)} %get-tuple-element.92) | copy-start | bytes 56623108
  138.1 8.9 %copy-start.78 = (f32[2,768]{1,0:T(2,128)}, f32[2,768]{1,0:T(2,128)S(1)}, u32[]{:S(2)}) copy-start(f32[2,768]{1,0:T(2,128)S(1)} %get-tuple-element.91) | copy-start | bytes 18436
  138.1 8.9 %copy-start.33 = (bf16[4,1,768,256]{3,2,1,0:T(8,128)(2,1)S(1)}, bf16[4,1,768,256]{3,2,1,0:T(8,128)(2,1)}, u32[]{:S(2)}) copy-start(bf16[4,1,768,256]{3,2,1,0:T(8,128)(2,1)} %get-tuple-element.61) | copy-start | bytes 4718596
  147.0 13.3 %copy-start.80 = (f32[2,768]{1,0:T(2,128)}, f32[2,768]{1,0:T(2,128)S(1)}, u32[]{:S(2)}) copy-start(f32[2,768]{1,0:T(2,128)S(1)} %fusion.2) | copy-start | bytes 18436
  474.9 6.8 copy-start.1
  474.9 6.8 copy-start.3
  474.9 7.2 copy-start.5
  474.9 7.2 copy-start.39
  474.9 7.2 copy-start.44
  474.9 7.2 copy-start.61
  474.9 7.1 copy-start.63
  532.3 11.4 %copy-start.36 = (f32[768,2,128]{2,0,1:T(8,128)S(1)}, f32[768,2,128]{2,0,1:T(8,128)}, u32[]{:S(2)}) copy-start(f32[768,2,128]{2,0,1:T(8,128)} %get-tuple-element.71) | copy-start | bytes 2359300
  532.3 11.4 %copy-start.37 = (f32[768,2,128]{2,0,1:T(8,128)S(1)}, f32[768,2,128]{2,0,1:T(8,128)}, u32[]{:S(2)}) copy-start(f32[768,2,128]{2,0,1:T(8,128)} %get-tuple-element.72) | copy-start | bytes 2359300
  532.3 11.4 %copy-start.87 = (bf16[2,768,3072]{2,1,0:T(8,128)(2,1)S(1)}, bf16[2,768,3072]{2,1,0:T(8,128)(2,1)}, u32[]{:S(2)}) copy-start(bf16[2,768,3072]{2,1,0:T(8,128)(2,1)} %multiply_convert_fusion) | copy-start | bytes 28311556
  550.8 12.3 %collective-permute-start.2 = (bf16[2,2,768,256]{3,2,0,1:T(8,128)(2,1)S(1)}, bf16[2,2,768,256]{3,2,0,1:T(8,128)(2,1)S(1)}, u32[]{:S(2)}, u32[]{:S(2)}) collective-permute-start(bf16[2,2,768,256]{3,2,0,1:T(8,128)(2,1)S(1)} %fusion.43), channel_id=1, source_target_pairs={{0,4},{4,0},{8,12},{12,8},{1,5},{5,1},{9,13},{13,9},{2,6},{6,2},{1... | collective-permute-start | bytes 4718600 | tf_op jit(solution)/shard_map/ppermute | solution.py:683
  552.1 9.0 %copy-start.18 = (bf16[2,96,8,256]{3,2,0,1:T(8,128)(2,1)}, bf16[2,96,8,256]{3,2,0,1:T(8,128)(2,1)S(1)}, u32[]{:S(2)}) copy-start(bf16[2,96,8,256]{3,2,0,1:T(8,128)(2,1)S(1)} %copy.131) | copy-start | bytes 2359300
  564.5 19.5 %collective-permute-start.3 = (bf16[2,768,256]{2,1,0:T(8,128)(2,1)}, bf16[2,768,256]{2,1,0:T(8,128)(2,1)}, u32[]{:S(2)}, u32[]{:S(2)}) collective-permute-start(bf16[2,768,256]{2,1,0:T(8,128)(2,1)} %fusion.55), channel_id=1, source_target_pairs={{0,8},{4,12},{8,0},{12,4},{1,9},{5,13},{9,1},{13,5},{2,10},{6,14},... | collective-permute-start | bytes 2359304 | tf_op jit(solution)/shard_map/ppermute | solution.py:683
  573.1 13.7 %copy-start.59 = (bf16[768,48]{0,1:T(8,128)(2,1)S(1)}, bf16[768,48]{0,1:T(8,128)(2,1)}, u32[]{:S(2)}) copy-start(bf16[768,48]{0,1:T(8,128)(2,1)} %convolution_convert_fusion.8) | copy-start | bytes 221188
  573.1 14.5 %copy-start.72 = (f32[768]{0:T(1024)S(1)}, f32[768]{0:T(1024)}, u32[]{:S(2)}) copy-start(f32[768]{0:T(1024)} %copy-done.71) | copy-start | bytes 9220
  573.1 14.5 %copy-start.85 = (f32[128]{0:T(128)S(1)}, f32[128]{0:T(128)}, u32[]{:S(2)}) copy-start(f32[128]{0:T(128)} %copy-done.83) | copy-start | bytes 1540
  740.1 13.7 %copy-start.17 = (bf16[6,128,2304]{2,1,0:T(8,128)(2,1)S(1)}, bf16[6,128,2304]{2,1,0:T(8,128)(2,1)}, u32[]{:S(2)}) copy-start(bf16[6,128,2304]{2,1,0:T(8,128)(2,1)} %get-tuple-element.17) | copy-start | bytes 10616836
  742.5 11.2 %copy-start.11 = (bf16[1,768,2304]{2,1,0:T(8,128)(2,1)S(1)}, bf16[1,768,2304]{2,1,0:T(8,128)(2,1)}, u32[]{:S(2)}) copy-start(bf16[1,768,2304]{2,1,0:T(8,128)(2,1)} %param.20) | copy-start | bytes 10616836
  742.5 11.2 %copy-start.15 = (bf16[768,2304]{1,0:T(8,128)(2,1)S(1)}, bf16[768,2304]{1,0:T(8,128)(2,1)}, u32[]{:S(2)}) copy-start(bf16[768,2304]{1,0:T(8,128)(2,1)} %get-tuple-element.23) | copy-start | bytes 10616836
  746.2 7.5 copy-start.4
  746.2 7.5 copy-start.6
  746.2 7.5 copy-start.45
  746.3 7.5 copy-start.64
  746.3 7.5 copy-start.67
  746.3 7.5 copy-start.74
  (48 other events, 170.0 us)
Sparse Core Ops, SparseCore 0:
  10.4 51.4 all-gather.4
  63.8 77.9 all-gather.6
  143.7 63.6 all-gather.8
  209.2 63.6 all-gather.10

commit v3 on v2

--- a/solution.py
+++ b/solution.py
@@ -14,7 +14,6 @@
 
 epsilon = 1e-06
 soft_cap = 50.0
-masked_low = -1e30
 MESH = pl.DeviceIdType.MESH
 f32 = jnp.float32
 bf16 = jnp.bfloat16
@@ -32,12 +31,13 @@
 
 
 def rotate(values, cosine, sine):
-    half = values.shape[-1] // 2
-    first = values[..., :half]
-    second = values[..., half:]
-    return jnp.concatenate(
-        [first * cosine - second * sine, second * cosine + first * sine], axis=-1
-    )
+    half = HEAD_SIZE // 2
+    parts = []
+    for at in range(0, values.shape[1], HEAD_SIZE):
+        first = values[:, at : at + half]
+        second = values[:, at + half : at + HEAD_SIZE]
+        parts += [first * cosine - second * sine, second * cosine + first * sine]
+    return jnp.concatenate(parts, axis=1)
 
 
 def dot_nn(left, right):
@@ -339,9 +339,7 @@
     a_down,
     b_down,
     a_gu,
-    gate_all,
-    up_all,
-    down_all,
+    ffn_all,
     y_all,
     dn2_all,
     act_all,
@@ -385,10 +383,10 @@
     across = 3 - z
 
     weights = [
-        pltpu.make_async_copy(source, target, load_sem.at[i])
-        for i, (source, target) in enumerate(
-            ((gate_all, w_gate), (up_all, w_up), (down_all, w_down))
+        pltpu.make_async_copy(
+            ffn_all.at[:, pl.ds(i * width, width)], target, load_sem.at[i]
         )
+        for i, target in enumerate((w_gate, w_up, w_down))
     ]
 
     def n2_copy(c):
@@ -626,10 +624,10 @@
 
 
 def feed_forward(
-    n2, cot, u_gu, gain, b_gate, a_down, b_down, a_gu, gate_full, up_full, down_full, collective_id
+    n2, cot, u_gu, gain, b_gate, a_down, b_down, a_gu, ffn_full, collective_id
 ):
     rows, width = n2.shape
-    hidden = gate_full.shape[1]
+    hidden = ffn_full.shape[1] // 3
     assert hidden == width
     step = 128
     n = rows // step
@@ -641,7 +639,7 @@
     results = pl.pallas_call(
         ffn_kernel,
         out_shape=[full] * 6,
-        in_specs=[anywhere] * 2 + [vmem] * 6 + [anywhere] * 3,
+        in_specs=[anywhere] * 2 + [vmem] * 6 + [anywhere],
         out_specs=[anywhere] * 6,
         scratch_shapes=[pltpu.VMEM((width, width), bf16)] * 3
         + [pltpu.VMEM((2, step, width), bf16)] * 2
@@ -672,11 +670,146 @@
         a_down,
         b_down,
         a_gu,
-        gate_full,
-        up_full,
-        down_full,
+        ffn_full,
     )
     return [value.reshape(rows, width) for value in results]
+
+
+def attend_kernel(tile, bases, q, limit, keys, values, out, sums):
+    rows = q.shape[0]
+    block = keys.shape[0] // bases.shape[0]
+    last = limit[...]
+    acc = jnp.zeros((rows, HEAD_SIZE), f32)
+    norm = jnp.zeros((rows, 1), f32)
+    for i in range(keys.shape[0] // tile):
+        span = slice(i * tile, (i + 1) * tile)
+        base = bases[i * tile // block] + (i * tile) % block
+        raw = dot_nt(q[...], keys[span, :])
+        weight = jnp.exp(soft_cap * jnp.tanh(raw * (1.0 / soft_cap)))
+        place = lax.broadcasted_iota(jnp.int32, (rows, tile), 1) + base
+        weight = jnp.where(place <= last, weight, 0.0)
+        norm = norm + jnp.sum(weight, axis=-1, keepdims=True)
+        acc = acc + dot_nn(weight.astype(bf16), values[span, :])
+    out[...] = (acc / norm).astype(bf16)
+    sums[...] = norm
+
+
+def attend(q, limit, keys, values, bases):
+    rows, cols = q.shape
+    step = 256
+    return pl.pallas_call(
+        functools.partial(attend_kernel, 768),
+        out_shape=[
+            jax.ShapeDtypeStruct((rows, cols), bf16),
+            jax.ShapeDtypeStruct((cols // HEAD_SIZE, rows, 1), f32),
+        ],
+        grid=(rows // step, cols // HEAD_SIZE),
+        in_specs=[
+            pl.BlockSpec(memory_space=pltpu.SMEM),
+            pl.BlockSpec((step, HEAD_SIZE), lambda i, g: (i, g)),
+            pl.BlockSpec((step, 1), lambda i, g: (i, 0)),
+            pl.BlockSpec(keys.shape, lambda i, g: (0, 0)),
+            pl.BlockSpec(keys.shape, lambda i, g: (0, 0)),
+        ],
+        out_specs=[
+            pl.BlockSpec((step, HEAD_SIZE), lambda i, g: (i, g)),
+            pl.BlockSpec((None, step, 1), lambda i, g: (g, i, 0)),
+        ],
+        compiler_params=pltpu.CompilerParams(vmem_limit_bytes=50 * 2**20),
+        cost_estimate=pl.CostEstimate(
+            flops=4 * rows * cols * keys.shape[0],
+            bytes_accessed=8 * 2**20,
+            transcendentals=2 * rows * cols * keys.shape[0] // HEAD_SIZE,
+        ),
+        name="attend",
+    )(bases, q, limit, keys, values)
+
+
+def attend_back_kernel(
+    tile, bases, q, d_out, limit, inverse, delta, keys, values, dq, near, far, dk_sum, dv_sum
+):
+    rows = q.shape[0]
+    total = keys.shape[0]
+    block = total // bases.shape[0]
+    here = pl.program_id(0) * pl.num_programs(1) + pl.program_id(1)
+    steps = pl.num_programs(0) * pl.num_programs(1)
+
+    @pl.when(here == 0)
+    def _():
+        dk_sum[...] = jnp.zeros_like(dk_sum)
+        dv_sum[...] = jnp.zeros_like(dv_sum)
+
+    last = limit[...]
+    scale = inverse[...]
+    shift = delta[...]
+    dq_sum = jnp.zeros((rows, HEAD_SIZE), f32)
+    for i in range(total // tile):
+        span = slice(i * tile, (i + 1) * tile)
+        base = bases[i * tile // block] + (i * tile) % block
+        raw = dot_nt(keys[span, :], q[...])
+        bend = jnp.tanh(raw * (1.0 / soft_cap))
+        place = lax.broadcasted_iota(jnp.int32, (tile, rows), 0) + base
+        weight = jnp.where(place <= last, jnp.exp(soft_cap * bend) * scale, 0.0)
+        d_weight = dot_nt(values[span, :], d_out[...])
+        d_raw = (weight * (d_weight - shift) * (1.0 - bend * bend)).astype(bf16)
+        dv_sum[span, :] += dot_nn(weight.astype(bf16), d_out[...])
+        dk_sum[span, :] += dot_nn(d_raw, q[...])
+        dq_sum = dq_sum + dot_tn(d_raw, keys[span, :])
+    dq[...] = dq_sum
+
+    @pl.when(here == steps - 1)
+    def _():
+        half = total // 2
+        near[0] = dk_sum[:half]
+        near[1] = dv_sum[:half]
+        far[0] = dk_sum[half:].astype(bf16)
+        far[1] = dv_sum[half:].astype(bf16)
+
+
+def attend_back(q, d_out, limit, inverse, delta, keys, values, bases):
+    rows, cols = q.shape
+    step = 256
+    total = keys.shape[0]
+    mat = pl.BlockSpec((step, HEAD_SIZE), lambda i, g: (i, g))
+    line = pl.BlockSpec((None, 1, step), lambda i, g: (g, 0, i))
+    whole = pl.BlockSpec(keys.shape, lambda i, g: (0, 0))
+    half = (2, total // 2, HEAD_SIZE)
+    return pl.pallas_call(
+        functools.partial(attend_back_kernel, 768),
+        out_shape=[
+            jax.ShapeDtypeStruct((rows, cols), f32),
+            jax.ShapeDtypeStruct(half, f32),
+            jax.ShapeDtypeStruct(half, bf16),
+        ],
+        grid=(rows // step, cols // HEAD_SIZE),
+        in_specs=[
+            pl.BlockSpec(memory_space=pltpu.SMEM),
+            mat,
+            mat,
+            pl.BlockSpec((1, step), lambda i, g: (0, i)),
+            line,
+            line,
+            whole,
+            whole,
+        ],
+        out_specs=[
+            mat,
+            pl.BlockSpec(half, lambda i, g: (0, 0, 0)),
+            pl.BlockSpec(half, lambda i, g: (0, 0, 0)),
+        ],
+        scratch_shapes=[pltpu.VMEM((total, HEAD_SIZE), f32)] * 2,
+        compiler_params=pltpu.CompilerParams(vmem_limit_bytes=60 * 2**20),
+        cost_estimate=pl.CostEstimate(
+            flops=10 * rows * cols * total,
+            bytes_accessed=16 * 2**20,
+            transcendentals=2 * rows * cols * total // HEAD_SIZE,
+        ),
+        name="attend_back",
+    )(bases, q, d_out, limit, inverse, delta, keys, values)
+
+
+def q_pairs(q_cols, k_cols):
+    return k_cols == HEAD_SIZE and q_cols == QUERY_HEADS // KEY_HEADS * HEAD_SIZE
 
 
 def swap(values, step):
@@ -706,7 +839,7 @@
 ):
     seqs, rows, width = tokens.shape
     assert seqs == 1 and lax.axis_size("ctx") == 4 and lax.axis_size("tp") == 4
-    groups = QUERY_HEADS // KEY_HEADS
+    assert q_pairs(query_weight.shape[1], key_weight.shape[1])
     scale = HEAD_SIZE ** (-0.5)
     q_cols = query_weight.shape[1]
     k_cols = key_weight.shape[1]
@@ -717,16 +850,15 @@
     def chosen(table, dim):
         return lax.dynamic_index_in_dim(table, adapter, dim, keepdims=False)
 
-    attn_local = jnp.concatenate(
-        [query_weight, key_weight, value_weight, output_weight.T], axis=1
-    )
-    attn_full = lax.all_gather(attn_local, both, axis=0, tiled=True)
-    gate_full = lax.all_gather(gate_weight, both, axis=0, tiled=True)
-    up_full = lax.all_gather(up_weight, both, axis=0, tiled=True)
-    down_full = lax.all_gather(down_weight.T, both, axis=0, tiled=True)
+    def gathered(*parts):
+        return lax.all_gather(jnp.concatenate(parts, axis=1), both, axis=0, tiled=True)
+
+    kv_full = gathered(key_weight, value_weight)
+    query_full = gathered(query_weight, output_weight.T)
+    ffn_full = gathered(gate_weight, up_weight, down_weight.T)
     qkv_cols = q_cols + 2 * k_cols
-    qkv_full = attn_full[:, :qkv_cols]
-    out_full = attn_full[:, qkv_cols:]
+    out_full = query_full[:, q_cols:]
+    query_full = query_full[:, :q_cols]
 
     a_in = chosen(adapter_first_input, 1)
     b_query = chosen(adapter_second_query, 0)
@@ -743,42 +875,29 @@
     half = HEAD_SIZE // 2
     freqs = jnp.exp(jnp.arange(half, dtype=f32) * (-2.0 * math.log(10000.0) / HEAD_SIZE))
     angle = query_pos.astype(f32)[:, None] * freqs[None, :]
-    cosine = jnp.cos(angle)[:, None, :]
-    sine = jnp.sin(angle)[:, None, :]
+    cosine = jnp.cos(angle)
+    sine = jnp.sin(angle)
 
     residual = tokens[0].astype(f32)
     d_final = cotangent[0].astype(f32)
     n1 = rms_norm(residual, gains[0]).astype(bf16)
     u_qkv = dot_nn(n1, a_qkv).astype(bf16)
-    lin = dot_nn(n1, qkv_full)
-    query = lin[:, :q_cols] + dot_nn(u_qkv[:, :rank], b_query)
-    key = lin[:, q_cols : q_cols + k_cols] + dot_nn(u_qkv[:, rank : 2 * rank], b_kv[0])
-    value = lin[:, q_cols + k_cols :] + dot_nn(u_qkv[:, 2 * rank :], b_kv[1])
-    qa = (rotate(query.reshape(rows, -1, HEAD_SIZE), cosine, sine) * scale).astype(bf16)
-    ka = rotate(key.reshape(rows, -1, HEAD_SIZE), cosine, sine).reshape(rows, -1).astype(bf16)
+    lin_kv = dot_nn(n1, kv_full)
+    query = dot_nn(n1, query_full) + dot_nn(u_qkv[:, :rank], b_query)
+    key = lin_kv[:, :k_cols] + dot_nn(u_qkv[:, rank : 2 * rank], b_kv[0])
+    value = lin_kv[:, k_cols:] + dot_nn(u_qkv[:, 2 * rank :], b_kv[1])
+    qa = (rotate(query, cosine, sine) * scale).astype(bf16)
+    ka = rotate(key, cosine, sine).astype(bf16)
     va = value.astype(bf16)
 
     own = jnp.stack([ka, va])
     from_row = swap(own, 2)
-    near = jnp.stack([own, from_row])
+    near = jnp.concatenate([own, from_row], axis=1)
     far = swap(near, 1)
-    blocks = jnp.concatenate([near, far])
-    keys = blocks[:, 0].reshape(-1, HEAD_SIZE)
-    values = blocks[:, 1].reshape(-1, HEAD_SIZE)
-    block_of = jnp.stack([ctx, ctx ^ 2, ctx ^ 1, ctx ^ 3])
-    key_pos = (block_of[:, None] * rows + jnp.arange(rows, dtype=jnp.int32)[None, :]).reshape(-1)
-    visible = (key_pos[None, :] <= query_pos[:, None]) | (key_pos[None, :] < prefix_length[0])
-
-    q_heads = qa.transpose(1, 0, 2)
-    raw = jnp.einsum("gqd,kd->gqk", q_heads, keys, preferred_element_type=f32)
-    capped = jnp.where(visible[None], soft_cap * jnp.tanh(raw / soft_cap), masked_low)
-    top = jnp.max(capped, axis=-1, keepdims=True)
-    expo = jnp.exp(capped - top)
-    total = jnp.sum(expo, axis=-1, keepdims=True)
-    probs = (expo / total).astype(bf16)
-    mixed = jnp.einsum("gqk,kd->gqd", probs, values, preferred_element_type=f32)
-    lse = top + jnp.log(total)
-    ob = mixed.astype(bf16).transpose(1, 0, 2).reshape(rows, -1)
+    keys, values = jnp.concatenate([near, far], axis=1)
+    bases = jnp.stack([ctx, ctx ^ 2, ctx ^ 1, ctx ^ 3]) * rows
+    limit = jnp.maximum(query_pos, prefix_length[0] - 1)
+    ob, sums = attend(qa, limit[:, None], keys, values, bases)
 
     u_out = dot_nn(ob, a_out).astype(bf16)
     y_att = matmul_sum([ob, u_out], [out_full, b_out[0].T], 1).astype(f32)
@@ -794,47 +913,48 @@
         a_down.T,
         b_out[1],
         jnp.stack([a_in[3].T, a_in[4].T]),
-        gate_full,
-        up_full,
-        down_full,
+        ffn_full,
         2,
     )
-    y_ffn = y_ffn.astype(f32)
     dn2 = dn2.astype(f32)
-    final = (h1 + rms_norm(y_ffn, gains[3])).astype(bf16)
+    dh1 = d_final + norm_back(h1, gains[2], dn2)
+    e_att = norm_back(y_att, gains[1], dh1).astype(bf16)
+    du_out = dot_nt(e_att, b_out[0]).astype(bf16)
+    d_ob = (dot_nn(e_att, out_full) + dot_nt(du_out, a_out)).astype(bf16)
+    overlap = d_ob.astype(f32) * ob.astype(f32)
+    delta = jnp.stack(
+        [
+            jnp.sum(overlap[:, at : at + HEAD_SIZE], axis=-1)[None]
+            for at in range(0, q_cols, HEAD_SIZE)
+        ]
+    )
+    dqa, d_near, d_far = attend_back(
+        qa,
+        d_ob,
+        limit[None],
+        (1.0 / sums)[..., 0][:, None],
+        delta,
+        keys,
+        values,
+        bases,
+    )
+    d_query = (rotate(dqa, cosine, -sine) * scale).astype(bf16)
+    d_near = d_near + swap(d_far, 1).astype(f32)
+    d_row = d_near[:, rows:].astype(bf16)
+    d_row, y_ffn, act, e_ffn, d_gate, d_up, e_att, du_out, d_query = lax.optimization_barrier(
+        (d_row, y_ffn, act, e_ffn, d_gate, d_up, e_att, du_out, d_query)
+    )
+    d_own = d_near[:, :rows] + swap(d_row, 2).astype(f32)
+    final = (h1 + rms_norm(y_ffn.astype(f32), gains[3])).astype(bf16)
     u_down = dot_nn(act, a_down).astype(bf16)
     du_down = dot_nt(e_ffn, b_out[1]).astype(bf16)
     du_gate = dot_nt(d_gate, b_gate[0]).astype(bf16)
     du_up = dot_nt(d_up, b_gate[1]).astype(bf16)
     du_gu = jnp.concatenate([du_gate, du_up], axis=1)
-    dh1 = d_final + norm_back(h1, gains[2], dn2)
-    e_att = norm_back(y_att, gains[1], dh1).astype(bf16)
-    du_out = dot_nt(e_att, b_out[0]).astype(bf16)
-    d_ob = (dot_nn(e_att, out_full) + dot_nt(du_out, a_out)).astype(bf16)
-    d_mixed = d_ob.reshape(rows, -1, HEAD_SIZE).transpose(1, 0, 2)
-
-    p_back = jnp.exp(capped - lse)
-    d_probs = jnp.einsum("gqd,kd->gqk", d_mixed, values, preferred_element_type=f32)
-    delta = jnp.sum(p_back * d_probs, axis=-1, keepdims=True)
-    slope = 1.0 - jnp.square(jnp.tanh(raw / soft_cap))
-    d_raw = (p_back * (d_probs - delta) * slope).astype(bf16)
-    dqa = jnp.einsum("gqk,kd->gqd", d_raw, keys, preferred_element_type=f32)
-    dka = jnp.einsum("gqk,gqd->kd", d_raw, q_heads, preferred_element_type=f32)
-    dva = jnp.einsum(
-        "gqk,gqd->kd", p_back.astype(bf16), d_mixed, preferred_element_type=f32
-    )
-    d_blocks = jnp.stack([dka, dva]).reshape(2, 4, rows, -1)
-    got_far = swap(d_blocks[:, 2:].astype(bf16), 1)
-    d_near = d_blocks[:, :2] + got_far.astype(f32)
-    got_row = swap(d_near[:, 1].astype(bf16), 2)
-    d_own = d_near[:, 0] + got_row.astype(f32)
-
-    d_query = (rotate(dqa.transpose(1, 0, 2), cosine, -sine) * scale).reshape(rows, -1)
-    d_key = rotate(d_own[0].reshape(rows, -1, HEAD_SIZE), cosine, -sine).reshape(rows, -1)
-    d_query = d_query.astype(bf16)
-    d_key = d_key.astype(bf16)
+
+    d_key = rotate(d_own[0], cosine, -sine).astype(bf16)
     d_value = d_own[1].astype(bf16)
-    d_qkv = jnp.concatenate([d_query, d_key, d_value], axis=1)
+    d_kv = jnp.concatenate([d_key, d_value], axis=1)
     du_query = dot_nt(d_query, b_query).astype(bf16)
     du_key = dot_nt(d_key, b_kv[0]).astype(bf16)
     du_value = dot_nt(d_value, b_kv[1]).astype(bf16)
@@ -868,7 +988,7 @@
         [wide.reshape(4, 2 * rank, width), split.reshape(4, rank, width)], axis=1
     ).astype(bf16)
     dn1, every = matmul_sum(
-        [d_qkv, du_qkv], [qkv_full, a_qkv], 4, terms=terms, slots=slots, summed=2 * rank
+        [d_query, d_kv, du_qkv], [query_full, kv_full, a_qkv], 4, terms=terms, slots=slots, summed=2 * rank
     )
     dn1 = dn1.astype(f32)
     input_grad = dh1 + norm_back(residual, gains[0], dn1)

time: 782 us -> 716 us (0.916)
  matrix products: 125 us -> 53.8 us
  Pallas kernels: 403 us -> 442 us
  local copies, waits for them, and re-layouts: 66.3 us -> 40.6 us
  other arithmetic: 83.1 us -> 68 us
  waiting for transfers between devices: 73.4 us -> 82.8 us
    dot_general x5 -> x0, matrix products: 39.1 us -> none  [the longest x1 13.3 us: per_device(): mixed = jnp.einsum('gqk,kd->gqd', probs, values, preferred_element_type=f32)]
    pallas_call x0 -> x2, Pallas kernels: none -> 33.7 us  [the longest x1 22.5 us: attend_back(): pl.pallas_call(functools.partial(attend_back_kernel, 768), out_shape=[jax...]
    sub x1 -> x0, matrix products: 28.8 us -> none  [per_device(): d_raw = (p_back * (d_probs - delta) * slope).astype(bf16)]
    all_gather x4 -> x3, waiting for transfers between devices: 30.2 us -> 46.5 us  [gathered(): lax.all_gather(jnp.concatenate(parts, axis=1), both, axis=0, tiled=True)]
    dot_general x8 -> x9, matrix products: 19.3 us -> 20.7 us  [dot_nn(): lax.dot_general(left, right, (((1,), (0,)), ((), ())), preferred_element_...]
  transfers between devices with their start and end apart: 8 -> 7, of which waited for: 3 -> 4; matrix products, arithmetic and copies ran while one was open for 15% -> 10% of each run, Pallas kernels for 12% -> 15%
where the time goes in v3:
time: 716 us; the launch traced here: 707 us
  Pallas kernels  442 us (62%)
  waiting for transfers between devices  82.8 us (12%)
  other arithmetic  68 us (9%)
  matrix products  53.8 us (8%)
  local copies, waits for them, and re-layouts  40.6 us (6%)
  between operations  17 us (2%)
    pallas_call x1, Pallas kernels, feed_forward(): pl.pallas_call(ffn_kernel, out_shape=[full] * 6, in_specs=[anywhere] * 2...  205 us
    pallas_call x2, Pallas kernels, matmul_sum(): pl.pallas_call(functools.partial(sum_kernel, len(lefts), width, chunks, s...  203 us
    all_gather x3, waiting for transfers between devices, gathered(): lax.all_gather(jnp.concatenate(parts, axis=1), both, axis=0, tiled=True)  46.5 us
    ppermute x4, waiting for transfers between devices, swap(): lax.ppermute(values, 'ctx', [(i, i ^ step) for i in range(lax.axis_size('...  36.3 us
    pallas_call x1, Pallas kernels, attend_back(): pl.pallas_call(functools.partial(attend_back_kernel, 768), out_shape=[jax...  22.5 us
    dot_general x9, matrix products, dot_nn(): lax.dot_general(left, right, (((1,), (0,)), ((), ())), preferred_element_...  20.7 us
    dot_general x11, matrix products, dot_tn(): lax.dot_general(left, right, (((0,), (0,)), ((), ())), preferred_element_...  19.8 us
  transfers between devices with their start and end apart: 7, of which 4 were waited for; matrix products, arithmetic and copies ran while one was open for 10% of the time, Pallas kernels for 15%

profile of v3, /device:TPU:0, one launch (start us, length us, event | category | flops | bytes accessed | tf_op | source)
XLA Modules:
  0.0 707.4 jit_solution(10728267080467485100)
XLA Ops:
  7.2 1.9 pad_maximum_fusion.8
  9.2 1.9 pad_maximum_fusion.6
  11.2 3.2 pad_maximum_fusion
  17.6 2.0 copy.80.refs_3_
  22.2 1.7 dynamic-slice_bitcast_fusion.13
  24.9 1.8 copy-done.13
  26.7 1.8 convolution_convert_fusion.8
  28.5 13.6 %all-gather.6.cloned.1.call-done.refs_4_ = bf16[2304,512]{1,0:T(8,128)(2,1)} async-done(((bf16[288,512]{1,0:T(8,128)(2,1)}), bf16[2304,512]{1,0:T(8,128)(2,1)}) %all-gather.6.cloned.1.call-update) | async-done | bytes 2359312 | tf_op jit(solution)/shard_map/all_gather | solution.py:854
  42.1 4.7 fusion.142
  46.9 1.7 fusion.39
  48.6 1.9 convolution_add_fusion.2
  50.5 32.9 %all-gather.4.cloned.1.call-done = bf16[2304,1024]{1,0:T(8,128)(2,1)} async-done(((bf16[288,1024]{1,0:T(8,128)(2,1)}), bf16[2304,1024]{1,0:T(8,128)(2,1)}) %all-gather.4.cloned.1.call-update) | async-done | bytes 4718608 | tf_op jit(solution)/shard_map/all_gather | solution.py:854
  83.4 3.7 fusion.139
  88.4 1.9 fusion.83
  94.0 1.6 dynamic-slice_bitcast_fusion.b_gate
  95.6 25.3 %collective-permute-done = bf16[2,768,256]{2,1,0:T(8,128)(2,1)S(1)} collective-permute-done((bf16[2,768,256]{2,1,0:T(8,128)(2,1)S(1)}, bf16[2,768,256]{2,1,0:T(8,128)(2,1)S(1)}, u32[]{:S(2)}, u32[]{:S(2)}) %collective-permute-start) | collective-permute-done | bytes 786464 | tf_op jit(solution)/shard_map/ppermute | solution.py:816
  122.1 2.6 fusion.141
  124.7 1.6 pad_maximum_fusion.1
  126.4 1.9 slice_bitcast_fusion.1
  128.3 11.2 %attend.1 = (bf16[768,512]{1,0:T(8,128)(2,1)S(1)}, f32[2,768,1]{2,1,0:T(8,128)S(1)}) custom-call(s32[4]{0:T(128)S(1)} %add_multiply_fusion.bases, bf16[768,512]{1,0:T(8,128)(2,1)S(1)} %fusion.34.q, s32[768,1]{1,0:T(8,128)S(1)} %add_maximum_fusion.limit, bf16[3072,256]{1,0:T(8,128)(2,1)} %get-tuple-element.93.keys, bf16[3072,256]{1,0:T(8,128)(2,1)} %get-tuple-element.92.values), custom_call_target="tpu_custom_call" | custom-call | flops 4831838208 | bytes 8388608 | tf_op jit(solution)/shard_map/attend/pallas_call | solution.py:700
  140.5 1.7 convolution_convert_fusion.7.refs_1_
  142.2 96.6 %matmul_sum_1.1 = bf16[768,2304]{1,0:T(8,128)(2,1)} custom-call(bf16[768,512]{1,0:T(8,128)(2,1)} %copy-done, bf16[768,16]{1,0:T(8,128)(2,1)} %convolution_convert_fusion.7.refs_1_, bf16[2304,512]{1,0:T(8,128)(2,1)} %get-tuple-element.91.refs_2_, bf16[2304,16]{1,0:T(8,128)(2,1)} %copy.80.refs_3_), custom_call_target="tpu_custom_call" | custom-call | flops 1868562432 | bytes 6782976 | tf_op jit(solution)/shard_map/matmul_sum_1/pallas_call | solution.py:318
  238.9 2.9 fusion.10
  241.9 3.9 multiply_reduce_fusion.1
  246.0 2.2 multiply_convert_fusion
  248.2 1.7 copy-done.16
  249.9 1.8 convolution_convert_fusion.9
  253.3 205.1 %feed_forward_2.1 = (bf16[6,128,2304]{2,1,0:T(8,128)(2,1)}, bf16[6,128,2304]{2,1,0:T(8,128)(2,1)}, bf16[6,128,2304]{2,1,0:T(8,128)(2,1)}, bf16[6,128,2304]{2,1,0...) custom-call(bf16[6,128,2304]{2,1,0:T(8,128)(2,1)} %bitcast.203, ...), custom_call_target="tpu_custom_call" | custom-call | flops 48922361856 | bytes 62914560 | tf_op jit(solution)/shard_map/feed_forward_2/pallas_call | solution.py:639
  458.5 6.5 fusion.24
  465.7 5.9 fusion.6
  471.7 5.2 fusion.9
  476.9 2.0 fusion.96
  478.9 2.0 fusion.137
  480.9 2.0 convert_multiply_fusion.8
  483.9 22.5 %attend_back.1 = (f32[768,512]{1,0:T(8,128)}, f32[2,1536,256]{2,1,0:T(8,128)}, bf16[2,1536,256]{2,1,0:T(8,128)(2,1)}) custom-call(s32[4]{0:T(128)} %copy-done.3, bf16[768,512]{1,0:T(8,128)(2,1)} %copy-done.2, bf16[768,512]{1,0:T(8,128)(2,1)} %get-tuple-element.125.d_out, s32[1,768]{1,0:T(1,128)} %add_maximum_fusion.1.limit, f32[2,1,768]{2,1,0:T(1,128)} %bitcast.229, ...), custom_call_target="tpu_custom_call" | custom-call | flops 12079595520 | bytes 16777216 | tf_op jit(solution)/shard_map/attend_back/pallas_call | solution.py:777
  507.6 3.8 fusion.65
  515.2 2.7 convolution_convert_fusion.13
  522.8 2.7 convolution_convert_fusion.12
  525.5 1.9 collective-permute-start.3
  527.5 1.6 convolution_convert_fusion.14
  530.3 4.6 convolution_convert_fusion.2
  535.0 11.0 %collective-permute-done.3 = bf16[2,768,256]{2,1,0:T(8,128)(2,1)} collective-permute-done((bf16[2,768,256]{2,1,0:T(8,128)(2,1)}, bf16[2,768,256]{2,1,0:T(8,128)(2,1)}, u32[]{:S(2)}, u32[]{:S(2)}) %collective-permute-start.3) | collective-permute-done | bytes 786464 | tf_op jit(solution)/shard_map/ppermute | solution.py:816
  545.9 1.8 slice_add_fusion
  549.7 1.8 fusion.70
  559.3 4.7 fusion.30
  565.6 1.7 copy.85.refs_2_
  570.1 106.1 %matmul_sum_4.1 = (bf16[768,2304]{1,0:T(8,128)(2,1)}, bf16[2,4,48,2304]{3,2,1,0:T(8,128)(2,1)}) custom-call(bf16[768,512]{1,0:T(8,128)(2,1)} %copy-done.29, bf16[768,512]{1,0:T(8,128)(2,1)} %pad_maximum_fusion.5.refs_1_, bf16[768,48]{1,0:T(8,128)(2,1)} %copy.85.refs_2_, bf16[2304,512]{1,0:T(8,128)(2,1)} %get-tuple-element.90.refs_3_, ...), custom_call_target="tpu_custom_call" | custom-call | flops 3793747968 | bytes 10125312 | tf_op jit(solution)/shard_map/matmul_sum_4/pallas_call | solution.py:318
  691.9 8.5 %fusion.20 = (f32[1,768,2304]{2,1,0:T(8,128)}, bf16[1,768,2304]{2,1,0:T(8,128)(2,1)}) fusion(bf16[768,2304]{1,0:T(8,128)(2,1)S(1)} %copy-done.24, bf16[1,768,2304]{2,1,0:T(8,128)(2,1)S(1)} %copy-done.7, f32[768]{0:T(1024)S(1)} %get-tuple-element.127, f32[2304]{0:T(1024)S(1)} %copy-done.58, f32[768]{0:T(1024)S(1)} %copy-done.65, f32[768]{0:T(1024)S(1)} %copy-done.70, ...), kind=kLoop, calls=%fused_computation.28 | loop fusion | flops 44236800 | bytes 31905792 | tf_op jit(solution)/shard_map/broadcast_in_dim | solution.py:1021
  (252 shorter events, 56.4 us)
Async XLA Ops:
  7.2 34.9 %all-gather.6.cloned.1.call-start = ((), (), s32[]{:S(2)}) async-start(), calls=%async_computation.1 | async-start | bytes 2654208 | tf_op jit(solution)/shard_map/all_gather | solution.py:854
  9.1 74.2 %all-gather.4.cloned.1.call-start = ((), (), s32[]{:S(2)}) async-start(), calls=%async_computation | async-start | bytes 5308416 | tf_op jit(solution)/shard_map/all_gather | solution.py:854
  11.1 242.2 %all-gather.8.cloned.1.call-start = ((), (), s32[]{:S(2)}) async-start(), calls=%async_computation.2 | async-start | bytes 35831808 | tf_op jit(solution)/shard_map/all_gather | solution.py:854
  14.4 5.8 copy-start.4
  20.2 68.2 %copy-start.66 = (f32[768]{0:T(1024)}, f32[768]{0:T(1024)S(1)}, u32[]{:S(2)}) copy-start(f32[768]{0:T(1024)S(1)} %add_convert_fusion.1) | copy-start | bytes 9220
  22.2 223.7 %copy-start.44 = (f32[2304]{0:T(1024)}, f32[2304]{0:T(1024)S(1)}, u32[]{:S(2)}) copy-start(f32[2304]{0:T(1024)S(1)} %get-tuple-element.83) | copy-start | bytes 27652
  28.5 54.9 %copy-start.14 = (bf16[768,2304]{1,0:T(8,128)(2,1)S(1)}, bf16[768,2304]{1,0:T(8,128)(2,1)}, u32[]{:S(2)}) copy-start(bf16[768,2304]{1,0:T(8,128)(2,1)} %copy-done.13) | copy-start | bytes 10616836
  87.1 35.0 %slice-start = ((s8[4718592]{0:T(1024)(128)(4,1)}), s8[4194304]{0:T(1024)(128)(4,1)S(1)}, s32[]{:S(2)}) async-start(s8[4718592]{0:T(1024)(128)(4,1)} %bitcast.220), calls=%async_computation.3 | async-start | bytes 8388608
  90.4 30.9 %copy-start.50 = (bf16[1,16,2304]{2,1,0:T(8,128)(2,1)S(1)}, bf16[1,16,2304]{2,1,0:T(8,128)(2,1)}, u32[]{:S(2)}) copy-start(bf16[1,16,2304]{2,1,0:T(8,128)(2,1)} %get-tuple-element.94) | copy-start | bytes 221188
  90.4 30.9 %copy-start.51 = (bf16[1,16,2304]{2,1,0:T(8,128)(2,1)S(1)}, bf16[1,16,2304]{2,1,0:T(8,128)(2,1)}, u32[]{:S(2)}) copy-start(bf16[1,16,2304]{2,1,0:T(8,128)(2,1)} %get-tuple-element.95) | copy-start | bytes 221188
  90.4 31.7 %slice-start.1 = ((s8[4718592]{0:T(1024)(128)(4,1)}), s8[524288]{0:T(1024)(128)(4,1)S(1)}, s32[]{:S(2)}) async-start(s8[4718592]{0:T(1024)(128)(4,1)} %bitcast.220), calls=%async_computation.4 | async-start | bytes 1048576
  90.5 30.5 %collective-permute-start = (bf16[2,768,256]{2,1,0:T(8,128)(2,1)S(1)}, bf16[2,768,256]{2,1,0:T(8,128)(2,1)S(1)}, u32[]{:S(2)}, u32[]{:S(2)}) collective-permute-start(bf16[2,768,256]{2,1,0:T(8,128)(2,1)S(1)} %pad_maximum_fusion.4), channel_id=1, source_target_pairs={{0,8},{4,12},{8,0},{12,4},{1,9},{5,13},{9,1},{13,5},{2,10},{6,14},... | collective-permute-start | bytes 2359304 | tf_op jit(solution)/shard_map/ppermute | solution.py:816
  121.1 3.6 collective-permute-start.1
  121.3 7.0 copy-start.3
  122.1 6.1 copy-start.2
  458.5 6.5 copy-start.6
  458.5 6.5 copy-start.9
  458.5 7.2 %copy-start.11 = (bf16[6,128,2304]{2,1,0:T(8,128)(2,1)S(1)}, bf16[6,128,2304]{2,1,0:T(8,128)(2,1)}, u32[]{:S(2)}) copy-start(bf16[6,128,2304]{2,1,0:T(8,128)(2,1)} %get-tuple-element.32) | copy-start | bytes 10616836
  458.5 7.2 %copy-start.45 = (f32[2304]{0:T(1024)S(1)}, f32[2304]{0:T(1024)}, u32[]{:S(2)}) copy-start(f32[2304]{0:T(1024)} %copy-done.44) | copy-start | bytes 27652
  458.5 7.2 %copy-start.48 = (f32[2304]{0:T(1024)S(1)}, f32[2304]{0:T(1024)}, u32[]{:S(2)}) copy-start(f32[2304]{0:T(1024)} %get-tuple-element.85) | copy-start | bytes 27652
  458.5 7.2 %copy-start.56 = (f32[768]{0:T(1024)S(1)}, f32[768]{0:T(1024)}, u32[]{:S(2)}) copy-start(f32[768]{0:T(1024)} %copy-done.55) | copy-start | bytes 9220
  458.5 7.2 %copy-start.60 = (f32[768]{0:T(1024)S(1)}, f32[768]{0:T(1024)}, u32[]{:S(2)}) copy-start(f32[768]{0:T(1024)} %copy-done.59) | copy-start | bytes 9220
  465.7 6.0 copy-start.69
  465.7 6.0 copy-start.20
  465.7 13.2 %slice-start.2 = ((s8[4718592]{0:T(1024)(128)(4,1)}), s8[4194304]{0:T(1024)(128)(4,1)S(1)}, s32[]{:S(2)}) async-start(s8[4718592]{0:T(1024)(128)(4,1)} %bitcast.222), calls=%async_computation.5 | async-start | bytes 8388608
  471.7 7.2 %slice-start.3 = ((s8[4718592]{0:T(1024)(128)(4,1)}), s8[524288]{0:T(1024)(128)(4,1)S(1)}, s32[]{:S(2)}) async-start(s8[4718592]{0:T(1024)(128)(4,1)} %bitcast.222), calls=%async_computation.6 | async-start | bytes 1048576
  483.9 22.6 %copy-start.39 = (bf16[2304,16]{0,1:T(8,128)(2,1)S(1)}, bf16[2304,16]{0,1:T(8,128)(2,1)}, u32[]{:S(2)}) copy-start(bf16[2304,16]{0,1:T(8,128)(2,1)} %copy-done.38) | copy-start | bytes 221188
  483.9 22.6 %copy-start.41 = (bf16[2304,16]{0,1:T(8,128)(2,1)S(1)}, bf16[2304,16]{0,1:T(8,128)(2,1)}, u32[]{:S(2)}) copy-start(bf16[2304,16]{0,1:T(8,128)(2,1)} %copy-done.40) | copy-start | bytes 221188
  483.9 22.6 %copy-start.43 = (bf16[2304,16]{0,1:T(8,128)(2,1)S(1)}, bf16[2304,16]{0,1:T(8,128)(2,1)}, u32[]{:S(2)}) copy-start(bf16[2304,16]{0,1:T(8,128)(2,1)} %copy-done.42) | copy-start | bytes 221188
  483.9 23.7 %copy-start.67 = (f32[768]{0:T(1024)S(1)}, f32[768]{0:T(1024)}, u32[]{:S(2)}) copy-start(f32[768]{0:T(1024)} %copy-done.66) | copy-start | bytes 9220
  483.9 23.7 %copy-start.75 = (f32[128]{0:T(128)S(1)}, f32[128]{0:T(128)}, u32[]{:S(2)}) copy-start(f32[128]{0:T(128)} %multiply_exponential_fusion) | copy-start | bytes 1540
  506.3 5.1 collective-permute-start.2
  511.4 16.0 %copy-start.29 = (bf16[768,512]{1,0:T(8,128)(2,1)}, bf16[768,512]{1,0:T(8,128)(2,1)S(1)}, u32[]{:S(2)}) copy-start(bf16[768,512]{1,0:T(8,128)(2,1)S(1)} %fusion.35.refs_0_) | copy-start | bytes 2359300
  511.9 6.0 copy-start.46
  522.8 7.5 %copy-start.27 = (bf16[6,128,2304]{2,1,0:T(8,128)(2,1)S(1)}, bf16[6,128,2304]{2,1,0:T(8,128)(2,1)}, u32[]{:S(2)}) copy-start(bf16[6,128,2304]{2,1,0:T(8,128)(2,1)} %get-tuple-element.37) | copy-start | bytes 10616836
  525.5 20.4 %collective-permute-start.3 = (bf16[2,768,256]{2,1,0:T(8,128)(2,1)}, bf16[2,768,256]{2,1,0:T(8,128)(2,1)}, u32[]{:S(2)}, u32[]{:S(2)}) collective-permute-start(bf16[2,768,256]{2,1,0:T(8,128)(2,1)} %slice.353), channel_id=1, source_target_pairs={{0,8},{4,12},{8,0},{12,4},{1,9},{5,13},{9,1},{13,5},{2,10},{6,14},... | collective-permute-start | bytes 2359304 | tf_op jit(solution)/shard_map/ppermute | solution.py:816
  535.0 12.9 %copy-start.37 = (bf16[768,48]{0,1:T(8,128)(2,1)S(1)}, bf16[768,48]{0,1:T(8,128)(2,1)}, u32[]{:S(2)}) copy-start(bf16[768,48]{0,1:T(8,128)(2,1)} %convolution_convert_fusion.8) | copy-start | bytes 221188
  535.0 14.7 %copy-start.68 = (f32[768]{0:T(1024)S(1)}, f32[768]{0:T(1024)}, u32[]{:S(2)}) copy-start(f32[768]{0:T(1024)} %copy-done.66) | copy-start | bytes 9220
  535.0 14.7 %copy-start.76 = (f32[128]{0:T(128)S(1)}, f32[128]{0:T(128)}, u32[]{:S(2)}) copy-start(f32[128]{0:T(128)} %multiply_exponential_fusion) | copy-start | bytes 1540
  547.7 5.8 copy-start.15
  547.7 5.8 copy-start.54
  685.1 5.7 copy-start.21
  685.1 5.7 copy-start.26
  686.7 5.2 copy-start.12
  686.7 5.2 copy-start.49
  686.7 5.2 copy-start.61
  686.7 5.2 copy-start.70
  686.8 5.2 copy-start.71
  (40 other events, 135.9 us)
Sparse Core Ops, SparseCore 0:
  10.5 31.5 all-gather.5
  44.6 38.7 all-gather.3
  85.8 163.4 all-gather.7

commit v4 on v3

--- a/solution.py
+++ b/solution.py
@@ -340,12 +340,19 @@
     b_down,
     a_gu,
     ffn_all,
+    h1_all,
+    att_all,
+    w_out,
+    b_out,
+    a_out,
     y_all,
-    dn2_all,
     act_all,
     e_all,
     dg_all,
     du_all,
+    dh_all,
+    e_att_all,
+    d_ob_all,
     w_gate,
     w_up,
     w_down,
@@ -357,6 +364,12 @@
     du_buf,
     keep_up,
     keep_gate,
+    h1_buf,
+    att_buf,
+    cot_back,
+    dh_buf,
+    e_att_buf,
+    d_ob_buf,
     part,
     mine,
     got_a,
@@ -364,6 +377,7 @@
     total,
     load_sem,
     in_sem,
+    back_sem,
     out_sem,
     a_send,
     a_recv,
@@ -396,6 +410,12 @@
         slot = lax.rem(c, 2)
         return pltpu.make_async_copy(cot_all.at[c], cot_buf.at[slot], in_sem.at[2 + slot])
 
+    def last_in(i, c):
+        source, target = ((h1_all, h1_buf), (att_all, att_buf), (cot_all, cot_back))[i]
+        return pltpu.make_async_copy(source.at[c], target, back_sem.at[i])
+
+    for i in range(3):
+        last_in(i, 0).start()
     n2_copy(0).start()
     for copy in weights:
         copy.start()
@@ -547,7 +567,7 @@
             values = total[c, lines, :].astype(f32)
             scale = lax.rsqrt(jnp.mean(values * values, axis=-1, keepdims=True) + epsilon)
             unit = values * scale
-            weighted = cot_buf[slot, lines, :].astype(f32) * gain[...]
+            weighted = cot_buf[slot, lines, :].astype(f32) * gain[2:3]
             e_buf[lines, :] = (
                 scale * (weighted - unit * jnp.mean(weighted * unit, axis=-1, keepdims=True))
             ).astype(bf16)
@@ -582,20 +602,91 @@
         exchange(n + c)
         return carry
 
-    def result(c):
-        return pltpu.make_async_copy(total.at[c], dn2_all.at[c], out_sem.at[5 + c])
+    def last_out(i, c):
+        source, target = (
+            (dh_buf, dh_all),
+            (e_att_buf, e_att_all),
+            (d_ob_buf, d_ob_all),
+        )[i]
+        return put(5 + i, source, target, c)
+
+    def last(c):
+        for i in range(3):
+            last_in(i, c).wait()
+
+        @pl.when(c >= 1)
+        def _():
+            for i in range(3):
+                last_out(i, c - 1).wait()
+
+        def lines_of(i, inside):
+            lines = pl.ds(pl.multiple_of(i * 16, 16), 16)
+            values = h1_buf[lines, :]
+            scale = lax.rsqrt(jnp.mean(values * values, axis=-1, keepdims=True) + epsilon)
+            unit = values * scale
+            weighted = total[c, lines, :].astype(f32) * gain[1:2]
+            d_h1 = cot_back[lines, :].astype(f32) + scale * (
+                weighted - unit * jnp.mean(weighted * unit, axis=-1, keepdims=True)
+            )
+            dh_buf[lines, :] = d_h1
+            values = att_buf[lines, :].astype(f32)
+            scale = lax.rsqrt(jnp.mean(values * values, axis=-1, keepdims=True) + epsilon)
+            unit = values * scale
+            weighted = d_h1 * gain[0:1]
+            e_att_buf[lines, :] = (
+                scale * (weighted - unit * jnp.mean(weighted * unit, axis=-1, keepdims=True))
+            ).astype(bf16)
+            return inside
+
+        lax.fori_loop(0, rows // 16, lines_of, 0)
+
+        @pl.when(c + 1 < n)
+        def _():
+            for i in range(3):
+                last_in(i, c + 1).start()
+
+        du_out = dot_nt(e_att_buf[...], b_out[...]).astype(bf16)
+        d_ob_buf[...] = (dot_nn(e_att_buf[...], w_out[...]) + dot_nn(du_out, a_out[...])).astype(
+            bf16
+        )
+        for i in range(3):
+            last_out(i, c).start()
+
+    def backward_and_last(c, carry):
+        backward(c, carry)
+
+        @pl.when(c >= ring)
+        def _():
+            last(c - ring)
+
+        return carry
 
     lax.fori_loop(0, n, forward, 0)
-    lax.fori_loop(0, n, backward, 0)
+    lax.fori_loop(0, n, backward_and_last, 0)
     act_out(n - 1).wait()
     for i in range(3):
         back_out(i, n - 1).wait()
 
+    def end(c, carry):
+        @pl.when(outer)
+        def _():
+            copy_c(n + c).wait_recv()
+            copy_a(n + c).wait_send()
+
+        @pl.when(inner & (c == n - 2))
+        def _():
+            copy_c(n - 1).wait_send()
+            finish(2 * n - 1)
+
+        last(c)
+        return carry
+
+    lax.fori_loop(n - ring, n, end, 0)
+    for i in range(3):
+        last_out(i, n - 1).wait()
+
     @pl.when(inner)
     def _():
-        copy_c(n - 1).wait_send()
-        finish(2 * n - 1)
-
         def drain(k, carry):
             copy_b(k).wait_send()
             return carry
@@ -608,23 +699,23 @@
 
         lax.fori_loop(n, 2 * n, drain_c, 0)
 
-    @pl.when(outer)
-    def _():
-        def drain(k, carry):
-            copy_c(k).wait_recv()
-            copy_a(k).wait_send()
-            return carry
-
-        lax.fori_loop(2 * n - ring, 2 * n, drain, 0)
-
-    for c in range(n):
-        result(c).start()
-    for c in range(n):
-        result(c).wait()
-
 
 def feed_forward(
-    n2, cot, u_gu, gain, b_gate, a_down, b_down, a_gu, ffn_full, collective_id
+    n2,
+    cot,
+    u_gu,
+    gain,
+    b_gate,
+    a_down,
+    b_down,
+    a_gu,
+    ffn_full,
+    h1,
+    y_att,
+    w_out,
+    b_out,
+    a_out,
+    collective_id,
 ):
     rows, width = n2.shape
     hidden = ffn_full.shape[1] // 3
@@ -633,25 +724,33 @@
     n = rows // step
     ring = 4
     full = jax.ShapeDtypeStruct((n, step, width), bf16)
+    shapes = [full] * 5 + [
+        jax.ShapeDtypeStruct((n, step, width), f32),
+        full,
+        jax.ShapeDtypeStruct((n, step, w_out.shape[1]), bf16),
+    ]
     vmem = pl.BlockSpec(memory_space=pltpu.VMEM)
     anywhere = pl.BlockSpec(memory_space=pl.ANY)
     block = pltpu.VMEM((step, width), bf16)
     results = pl.pallas_call(
         ffn_kernel,
-        out_shape=[full] * 6,
-        in_specs=[anywhere] * 2 + [vmem] * 6 + [anywhere],
-        out_specs=[anywhere] * 6,
+        out_shape=shapes,
+        in_specs=[anywhere] * 2 + [vmem] * 6 + [anywhere] * 3 + [vmem] * 3,
+        out_specs=[anywhere] * len(shapes),
         scratch_shapes=[pltpu.VMEM((width, width), bf16)] * 3
         + [pltpu.VMEM((2, step, width), bf16)] * 2
         + [block] * 4
         + [pltpu.VMEM((n, step, width), bf16)] * 2
+        + [pltpu.VMEM((step, width), f32), block, block]
+        + [pltpu.VMEM((step, width), f32), block, pltpu.VMEM((step, w_out.shape[1]), bf16)]
         + [pltpu.VMEM((step, width), f32)]
         + [pltpu.VMEM((ring, step, width), bf16)] * 3
         + [pltpu.VMEM((n, step, width), bf16)]
         + [
             pltpu.SemaphoreType.DMA((3,)),
             pltpu.SemaphoreType.DMA((4,)),
-            pltpu.SemaphoreType.DMA((5 + n,)),
+            pltpu.SemaphoreType.DMA((3,)),
+            pltpu.SemaphoreType.DMA((8,)),
         ]
         + [pltpu.SemaphoreType.DMA((2 * n,))] * 6,
         compiler_params=pltpu.CompilerParams(
@@ -671,8 +770,13 @@
         b_down,
         a_gu,
         ffn_full,
-    )
-    return [value.reshape(rows, width) for value in results]
+        h1.reshape(n, step, width),
+        y_att.reshape(n, step, width),
+        w_out,
+        b_out,
+        a_out,
+    )
+    return [value.reshape(rows, -1) for value in results]
 
 
 def attend_kernel(tile, bases, q, limit, keys, values, out, sums):
@@ -900,27 +1004,27 @@
     ob, sums = attend(qa, limit[:, None], keys, values, bases)
 
     u_out = dot_nn(ob, a_out).astype(bf16)
-    y_att = matmul_sum([ob, u_out], [out_full, b_out[0].T], 1).astype(f32)
-    h1 = residual + rms_norm(y_att, gains[1])
+    y_att = matmul_sum([ob, u_out], [out_full, b_out[0].T], 1)
+    h1 = residual + rms_norm(y_att.astype(f32), gains[1])
     n2 = rms_norm(h1, gains[2]).astype(bf16)
     u_gu = dot_nn(n2, a_gu).astype(bf16)
-    y_ffn, dn2, act, e_ffn, d_gate, d_up = feed_forward(
+    y_ffn, act, e_ffn, d_gate, d_up, dh1, e_att, d_ob = feed_forward(
         n2,
         cotangent[0],
         u_gu,
-        gains[3][None],
+        gains[1:],
         b_gate,
         a_down.T,
         b_out[1],
         jnp.stack([a_in[3].T, a_in[4].T]),
         ffn_full,
+        h1,
+        y_att,
+        out_full,
+        b_out[0],
+        a_out.T,
         2,
     )
-    dn2 = dn2.astype(f32)
-    dh1 = d_final + norm_back(h1, gains[2], dn2)
-    e_att = norm_back(y_att, gains[1], dh1).astype(bf16)
-    du_out = dot_nt(e_att, b_out[0]).astype(bf16)
-    d_ob = (dot_nn(e_att, out_full) + dot_nt(du_out, a_out)).astype(bf16)
     overlap = d_ob.astype(f32) * ob.astype(f32)
     delta = jnp.stack(
         [
@@ -941,13 +1045,14 @@
     d_query = (rotate(dqa, cosine, -sine) * scale).astype(bf16)
     d_near = d_near + swap(d_far, 1).astype(f32)
     d_row = d_near[:, rows:].astype(bf16)
-    d_row, y_ffn, act, e_ffn, d_gate, d_up, e_att, du_out, d_query = lax.optimization_barrier(
-        (d_row, y_ffn, act, e_ffn, d_gate, d_up, e_att, du_out, d_query)
+    d_row, y_ffn, act, e_ffn, d_gate, d_up, e_att, d_query = lax.optimization_barrier(
+        (d_row, y_ffn, act, e_ffn, d_gate, d_up, e_att, d_query)
     )
     d_own = d_near[:, :rows] + swap(d_row, 2).astype(f32)
     final = (h1 + rms_norm(y_ffn.astype(f32), gains[3])).astype(bf16)
     u_down = dot_nn(act, a_down).astype(bf16)
     du_down = dot_nt(e_ffn, b_out[1]).astype(bf16)
+    du_out = dot_nt(e_att, b_out[0]).astype(bf16)
     du_gate = dot_nt(d_gate, b_gate[0]).astype(bf16)
     du_up = dot_nt(d_up, b_gate[1]).astype(bf16)
     du_gu = jnp.concatenate([du_gate, du_up], axis=1)

time: 716 us -> 691 us (0.965)
  other arithmetic: 68 us -> 53.2 us
  waiting for transfers between devices: 82.8 us -> 74.1 us
    reduce_sum x3 -> x1, other arithmetic: 13.9 us -> 1.51 us  [norm_back(): jnp.mean(weighted * unit, axis=-1, keepdims=True)]
    dot_general x9 -> x8, matrix products: 20.7 us -> 18 us  [dot_nn(): lax.dot_general(left, right, (((1,), (0,)), ((), ())), preferred_element_...]
    unnamed x167 -> x131, local copies, waits for them, and re-layouts: 13.7 us -> 14.9 us
  transfers between devices with their start and end apart: 7 -> 7, of which waited for: 4 -> 4; matrix products, arithmetic and copies ran while one was open for 10% -> 11% of each run, Pallas kernels for 15% -> 16%
where the time goes in v4:
time: 691 us; the launch traced here: 682 us
  Pallas kernels  441 us (64%)
  waiting for transfers between devices  74.1 us (11%)
  other arithmetic  53.2 us (8%)
  matrix products  49.8 us (7%)
  local copies, waits for them, and re-layouts  44.1 us (6%)
  between operations  16.7 us (2%)
    pallas_call x1, Pallas kernels, feed_forward(): pl.pallas_call(ffn_kernel, out_shape=shapes, in_specs=[anywhere] * 2 + [v...  204 us
    pallas_call x2, Pallas kernels, matmul_sum(): pl.pallas_call(functools.partial(sum_kernel, len(lefts), width, chunks, s...  203 us
    all_gather x3, waiting for transfers between devices, gathered(): lax.all_gather(jnp.concatenate(parts, axis=1), both, axis=0, tiled=True)  43.4 us
    ppermute x4, waiting for transfers between devices, swap(): lax.ppermute(values, 'ctx', [(i, i ^ step) for i in range(lax.axis_size('...  30.6 us
    pallas_call x1, Pallas kernels, attend_back(): pl.pallas_call(functools.partial(attend_back_kernel, 768), out_shape=[jax...  22.7 us
    dot_general x11, matrix products, dot_tn(): lax.dot_general(left, right, (((0,), (0,)), ((), ())), preferred_element_...  22.5 us
    dot_general x8, matrix products, dot_nn(): lax.dot_general(left, right, (((1,), (0,)), ((), ())), preferred_element_...  18 us
    unnamed x131, local copies, waits for them, and re-layouts  14.9 us
  transfers between devices with their start and end apart: 7, of which 4 were waited for; matrix products, arithmetic and copies ran while one was open for 11% of the time, Pallas kernels for 16%

profile of v4, /device:TPU:0, one launch (start us, length us, event | category | flops | bytes accessed | tf_op | source)
XLA Modules:
  0.0 682.2 jit_solution(2318613904116648797)
XLA Ops:
  7.2 1.9 pad_maximum_fusion.8
  9.2 1.9 pad_maximum_fusion.6
  11.2 3.2 pad_maximum_fusion
  17.5 1.6 dynamic-slice_bitcast_fusion.10
  19.1 1.9 copy.74.refs_3_
  22.9 1.6 slice_reduce_fusion.2
  25.3 1.8 dynamic-slice_bitcast_fusion.14
  28.0 1.8 copy-done.8
  29.8 1.8 convolution_convert_fusion.8
  31.6 10.5 %all-gather.6.cloned.1.call-done.refs_4_ = bf16[2304,512]{1,0:T(8,128)(2,1)} async-done(((bf16[288,512]{1,0:T(8,128)(2,1)}), bf16[2304,512]{1,0:T(8,128)(2,1)}) %all-gather.6.cloned.1.call-update) | async-done | bytes 2359312 | tf_op jit(solution)/shard_map/all_gather | solution.py:958
  42.1 4.7 fusion.120
  46.9 1.7 fusion.24
  48.7 1.9 convolution_add_fusion.2
  50.5 32.9 %all-gather.4.cloned.1.call-done = bf16[2304,1024]{1,0:T(8,128)(2,1)} async-done(((bf16[288,1024]{1,0:T(8,128)(2,1)}), bf16[2304,1024]{1,0:T(8,128)(2,1)}) %all-gather.4.cloned.1.call-update) | async-done | bytes 4718608 | tf_op jit(solution)/shard_map/all_gather | solution.py:958
  83.4 3.7 fusion.117
  88.5 1.9 fusion.70
  94.0 1.7 dynamic-slice_bitcast_fusion.b_gate
  95.7 25.9 %collective-permute-done = bf16[2,768,256]{2,1,0:T(8,128)(2,1)S(1)} collective-permute-done((bf16[2,768,256]{2,1,0:T(8,128)(2,1)S(1)}, bf16[2,768,256]{2,1,0:T(8,128)(2,1)S(1)}, u32[]{:S(2)}, u32[]{:S(2)}) %collective-permute-start) | collective-permute-done | bytes 786464 | tf_op jit(solution)/shard_map/ppermute | solution.py:920
  122.7 2.6 fusion.119
  125.3 1.6 pad_maximum_fusion.1
  127.0 1.9 slice_bitcast_fusion.1
  128.8 11.2 %attend.1 = (bf16[768,512]{1,0:T(8,128)(2,1)S(1)}, f32[2,768,1]{2,1,0:T(8,128)S(1)}) custom-call(s32[4]{0:T(128)S(1)} %add_multiply_fusion.bases, bf16[768,512]{1,0:T(8,128)(2,1)S(1)} %fusion.21.q, s32[768,1]{1,0:T(8,128)S(1)} %add_maximum_fusion.limit, bf16[3072,256]{1,0:T(8,128)(2,1)} %get-tuple-element.95.keys, bf16[3072,256]{1,0:T(8,128)(2,1)} %get-tuple-element.94.values), custom_call_target="tpu_custom_call" | custom-call | flops 4831838208 | bytes 8388608 | tf_op jit(solution)/shard_map/attend/pallas_call | solution.py:804
  141.1 1.7 convolution_convert_fusion.7.refs_1_
  142.8 96.9 %matmul_sum_1.1 = bf16[768,2304]{1,0:T(8,128)(2,1)} custom-call(bf16[768,512]{1,0:T(8,128)(2,1)} %copy-done, bf16[768,16]{1,0:T(8,128)(2,1)} %convolution_convert_fusion.7.refs_1_, bf16[2304,512]{1,0:T(8,128)(2,1)} %get-tuple-element.93.refs_2_.w_out, bf16[2304,16]{1,0:T(8,128)(2,1)} %copy.74.refs_3_), custom_call_target="tpu_custom_call" | custom-call | flops 1868562432 | bytes 6782976 | tf_op jit(solution)/shard_map/matmul_sum_1/pallas_call | solution.py:318
  239.7 2.9 fusion.3
  242.8 3.5 multiply_reduce_fusion.1
  247.0 2.3 copy-done.7
  249.2 1.7 copy-done.11
  253.6 204.2 %feed_forward_2.1 = (bf16[6,128,2304]{2,1,0:T(8,128)(2,1)}, bf16[6,128,2304]{2,1,0:T(8,128)(2,1)}, bf16[6,128,2304]{2,1,0:T(8,128)(2,1)}, bf16[6,128,2304]{2,1,0...) custom-call(bf16[6,128,2304]{2,1,0:T(8,128)(2,1)} %bitcast.172, ...), custom_call_target="tpu_custom_call" | custom-call | flops 48922361856 | bytes 62914560 | tf_op jit(solution)/shard_map/feed_forward_2/pallas_call | solution.py:735
  457.7 1.6 convert_multiply_fusion.7
  460.3 22.7 %attend_back.1 = (f32[768,512]{1,0:T(8,128)}, f32[2,1536,256]{2,1,0:T(8,128)}, bf16[2,1536,256]{2,1,0:T(8,128)(2,1)}) custom-call(s32[4]{0:T(128)} %copy-done.3, bf16[768,512]{1,0:T(8,128)(2,1)} %copy-done.2, bf16[768,512]{1,0:T(8,128)(2,1)} %bitcast.199, s32[1,768]{1,0:T(1,128)} %add_maximum_fusion.1.limit, f32[2,1,768]{2,1,0:T(1,128)} %bitcast.202, ...), custom_call_target="tpu_custom_call" | custom-call | flops 12079595520 | bytes 16777216 | tf_op jit(solution)/shard_map/attend_back/pallas_call | solution.py:881
  484.2 3.6 fusion.52
  491.6 2.6 convolution_convert_fusion.14
  495.5 3.3 fusion.26
  498.8 2.9 fusion.5
  501.8 1.7 convolution_convert_fusion.18
  503.5 2.6 convolution_convert_fusion.13
  506.0 2.0 collective-permute-start.3
  508.1 6.0 fusion.16
  514.1 1.8 convolution_convert_fusion.15
  517.1 4.6 convolution_convert_fusion.2
  521.8 4.8 collective-permute-done.3
  526.5 1.8 slice_add_fusion
  530.3 2.1 fusion.57
  540.1 4.7 fusion.19
  546.5 1.7 copy.77.refs_2_
  550.9 105.8 %matmul_sum_4.1 = (bf16[768,2304]{1,0:T(8,128)(2,1)}, bf16[2,4,48,2304]{3,2,1,0:T(8,128)(2,1)}) custom-call(bf16[768,512]{1,0:T(8,128)(2,1)} %copy-done.20, bf16[768,512]{1,0:T(8,128)(2,1)} %pad_maximum_fusion.5.refs_1_, bf16[768,48]{1,0:T(8,128)(2,1)} %copy.77.refs_2_, bf16[2304,512]{1,0:T(8,128)(2,1)} %get-tuple-element.92.refs_3_, ...), custom_call_target="tpu_custom_call" | custom-call | flops 3793747968 | bytes 10125312 | tf_op jit(solution)/shard_map/matmul_sum_4/pallas_call | solution.py:318
  670.5 4.0 fusion.14
  (213 shorter events, 52.3 us)
Async XLA Ops:
  7.2 4.0 copy-start.26
  7.2 4.0 copy-start.27
  7.2 34.9 %all-gather.6.cloned.1.call-start = ((), (), s32[]{:S(2)}) async-start(), calls=%async_computation.1 | async-start | bytes 2654208 | tf_op jit(solution)/shard_map/all_gather | solution.py:958
  9.1 74.3 %all-gather.4.cloned.1.call-start = ((), (), s32[]{:S(2)}) async-start(), calls=%async_computation | async-start | bytes 5308416 | tf_op jit(solution)/shard_map/all_gather | solution.py:958
  11.1 242.4 %all-gather.8.cloned.1.call-start = ((), (), s32[]{:S(2)}) async-start(), calls=%async_computation.2 | async-start | bytes 35831808 | tf_op jit(solution)/shard_map/all_gather | solution.py:958
  14.5 10.1 %copy-start.4 = (bf16[1,768,2304]{2,1,0:T(8,128)(2,1)S(1)}, bf16[1,768,2304]{2,1,0:T(8,128)(2,1)}, u32[]{:S(2)}) copy-start(bf16[1,768,2304]{2,1,0:T(8,128)(2,1)} %param.19) | copy-start | bytes 10616836
  21.6 66.8 %copy-start.51 = (f32[768]{0:T(1024)}, f32[768]{0:T(1024)S(1)}, u32[]{:S(2)}) copy-start(f32[768]{0:T(1024)S(1)} %add_convert_fusion) | copy-start | bytes 9220
  31.6 51.8 %copy-start.9 = (bf16[768,2304]{1,0:T(8,128)(2,1)S(1)}, bf16[768,2304]{1,0:T(8,128)(2,1)}, u32[]{:S(2)}) copy-start(bf16[768,2304]{1,0:T(8,128)(2,1)} %copy-done.8) | copy-start | bytes 10616836
  42.1 4.8 copy-start.28
  83.4 5.0 copy-start.24
  83.4 5.0 copy-start.56
  87.2 35.6 %slice-start.2 = ((s8[4718592]{0:T(1024)(128)(4,1)}), s8[4194304]{0:T(1024)(128)(4,1)S(1)}, s32[]{:S(2)}) async-start(s8[4718592]{0:T(1024)(128)(4,1)} %bitcast.193), calls=%async_computation.5 | async-start | bytes 8388608
  90.4 31.5 %copy-start.39 = (bf16[1,16,2304]{2,1,0:T(8,128)(2,1)S(1)}, bf16[1,16,2304]{2,1,0:T(8,128)(2,1)}, u32[]{:S(2)}) copy-start(bf16[1,16,2304]{2,1,0:T(8,128)(2,1)} %get-tuple-element.96) | copy-start | bytes 221188
  90.4 31.5 %copy-start.40 = (bf16[1,16,2304]{2,1,0:T(8,128)(2,1)S(1)}, bf16[1,16,2304]{2,1,0:T(8,128)(2,1)}, u32[]{:S(2)}) copy-start(bf16[1,16,2304]{2,1,0:T(8,128)(2,1)} %get-tuple-element.97) | copy-start | bytes 221188
  90.4 32.3 %slice-start.3 = ((s8[4718592]{0:T(1024)(128)(4,1)}), s8[524288]{0:T(1024)(128)(4,1)S(1)}, s32[]{:S(2)}) async-start(s8[4718592]{0:T(1024)(128)(4,1)} %bitcast.193), calls=%async_computation.6 | async-start | bytes 1048576
  90.5 31.0 %collective-permute-start = (bf16[2,768,256]{2,1,0:T(8,128)(2,1)S(1)}, bf16[2,768,256]{2,1,0:T(8,128)(2,1)S(1)}, u32[]{:S(2)}, u32[]{:S(2)}) collective-permute-start(bf16[2,768,256]{2,1,0:T(8,128)(2,1)S(1)} %pad_maximum_fusion.4), channel_id=1, source_target_pairs={{0,8},{4,12},{8,0},{12,4},{1,9},{5,13},{9,1},{13,5},{2,10},{6,14},... | collective-permute-start | bytes 2359304 | tf_op jit(solution)/shard_map/ppermute | solution.py:920
  121.7 3.6 collective-permute-start.1
  121.9 7.0 %copy-start.3 = (s32[4]{0:T(128)}, s32[4]{0:T(128)S(1)}, u32[]{:S(2)}) copy-start(s32[4]{0:T(128)S(1)} %add_multiply_fusion.bases) | copy-start | bytes 52
  122.7 6.1 copy-start.2
  246.3 4.7 copy-start.41
  246.3 4.7 copy-start.42
  460.3 22.8 %copy-start.31 = (bf16[2304,16]{0,1:T(8,128)(2,1)S(1)}, bf16[2304,16]{0,1:T(8,128)(2,1)}, u32[]{:S(2)}) copy-start(bf16[2304,16]{0,1:T(8,128)(2,1)} %copy-done.30) | copy-start | bytes 221188
  460.3 22.8 %copy-start.33 = (bf16[2304,16]{0,1:T(8,128)(2,1)S(1)}, bf16[2304,16]{0,1:T(8,128)(2,1)}, u32[]{:S(2)}) copy-start(bf16[2304,16]{0,1:T(8,128)(2,1)} %copy-done.32) | copy-start | bytes 221188
  460.3 22.8 %copy-start.35 = (bf16[2304,16]{0,1:T(8,128)(2,1)S(1)}, bf16[2304,16]{0,1:T(8,128)(2,1)}, u32[]{:S(2)}) copy-start(bf16[2304,16]{0,1:T(8,128)(2,1)} %copy-done.34) | copy-start | bytes 221188
  460.3 23.9 %copy-start.52 = (f32[768]{0:T(1024)S(1)}, f32[768]{0:T(1024)}, u32[]{:S(2)}) copy-start(f32[768]{0:T(1024)} %copy-done.51) | copy-start | bytes 9220
  460.3 23.9 %copy-start.57 = (f32[128]{0:T(128)S(1)}, f32[128]{0:T(128)}, u32[]{:S(2)}) copy-start(f32[128]{0:T(128)} %multiply_exponential_fusion) | copy-start | bytes 1540
  482.9 4.9 collective-permute-start.2
  484.2 3.7 copy-start.23
  487.9 13.9 %copy-start.20 = (bf16[768,512]{1,0:T(8,128)(2,1)}, bf16[768,512]{1,0:T(8,128)(2,1)S(1)}, u32[]{:S(2)}) copy-start(bf16[768,512]{1,0:T(8,128)(2,1)S(1)} %fusion.22.refs_0_) | copy-start | bytes 2359300
  488.3 5.9 copy-start.37
  491.6 3.9 copy-start.1
  491.6 3.9 copy-start.43
  498.8 4.7 copy-start.13
  501.7 6.3 copy-start.17
  501.7 6.3 copy-start.54
  506.0 20.5 %collective-permute-start.3 = (bf16[2,768,256]{2,1,0:T(8,128)(2,1)}, bf16[2,768,256]{2,1,0:T(8,128)(2,1)}, u32[]{:S(2)}, u32[]{:S(2)}) collective-permute-start(bf16[2,768,256]{2,1,0:T(8,128)(2,1)} %slice.353), channel_id=1, source_target_pairs={{0,8},{4,12},{8,0},{12,4},{1,9},{5,13},{9,1},{13,5},{2,10},{6,14},... | collective-permute-start | bytes 2359304 | tf_op jit(solution)/shard_map/ppermute | solution.py:920
  508.1 6.0 copy-start.21
  508.1 7.8 %copy-start.38 = (bf16[768,32]{0,1:T(8,128)(2,1)S(1)}, bf16[768,32]{0,1:T(8,128)(2,1)}, u32[]{:S(2)}) copy-start(bf16[768,32]{0,1:T(8,128)(2,1)} %copy-done.36) | copy-start | bytes 147460
  521.8 6.7 copy-start.29
  521.8 8.5 %copy-start.53 = (f32[768]{0:T(1024)S(1)}, f32[768]{0:T(1024)}, u32[]{:S(2)}) copy-start(f32[768]{0:T(1024)} %copy-done.51) | copy-start | bytes 9220
  521.8 8.5 %copy-start.58 = (f32[128]{0:T(128)S(1)}, f32[128]{0:T(128)}, u32[]{:S(2)}) copy-start(f32[128]{0:T(128)} %multiply_exponential_fusion) | copy-start | bytes 1540
  528.3 6.1 copy-start.10
  528.3 6.1 copy-start.44
  532.4 5.1 copy-start.12
  532.4 5.1 copy-start.47
  532.4 5.1 copy-start.48
  663.3 7.2 %slice-start = ((s8[7077888]{0:T(1024)(128)(4,1)}), s8[4194304]{0:T(1024)(128)(4,1)S(1)}, s32[]{:S(2)}) async-start(s8[7077888]{0:T(1024)(128)(4,1)} %bitcast.188), calls=%async_computation.3 | async-start | bytes 8388608
  665.6 4.9 slice-start.1
  (22 other events, 56.5 us)
Sparse Core Ops, SparseCore 0:
  10.5 31.6 all-gather.5
  44.6 38.7 all-gather.3
  85.3 164.0 all-gather.7

commit v5 on v4

--- a/solution.py
+++ b/solution.py
@@ -50,6 +50,95 @@
 
 def dot_tn(left, right):
     return lax.dot_general(left, right, (((0,), (0,)), ((), ())), preferred_element_type=f32)
+
+
+def gather_kernel(seqs, shard, out, w_send, w_recv, own_sem):
+    at = lax.axis_index("ctx")
+    core = lax.rem(at, 2)
+    row = lax.div(at, 2)
+    core_peer = at + 1 - 2 * core
+    row_peer = at + 2 - 4 * row
+    seq = lax.axis_index("fsdp")
+    half = shard.shape[1] // 2
+    left = pl.ds(0, half)
+    right = pl.ds(half, half)
+    own = pltpu.make_async_copy(shard, out.at[seq, row, core], own_sem)
+    own.start()
+
+    barrier = pltpu.get_barrier_semaphore()
+
+    def greet(axis, peer):
+        pl.semaphore_signal(barrier, inc=1, device_id={axis: peer}, device_id_type=MESH)
+
+    greet("ctx", core_peer)
+    greet("ctx", row_peer)
+    for d in range(1, seqs):
+        greet("fsdp", lax.rem(seq + d, seqs))
+    pl.semaphore_wait(barrier, seqs + 1)
+
+    def remote(i, source, target, axis, peer):
+        return pltpu.make_async_remote_copy(
+            source,
+            target,
+            w_send.at[i],
+            w_recv.at[i],
+            device_id={axis: peer},
+            device_id_type=MESH,
+        )
+
+    row_first = remote(
+        0, shard.at[:, right], out.at[seq, row, core, :, right], "ctx", row_peer
+    )
+    row_first.start()
+    seq_first = []
+    for d in range(1, seqs):
+        peer = lax.rem(seq + d, seqs)
+        copy = remote(d, shard.at[:, left], out.at[seq, row, core, :, left], "fsdp", peer)
+        copy.start()
+        seq_first.append(copy)
+    own.wait()
+    for copy in seq_first:
+        copy.wait()
+    place = out.at[:, row, core, :, left]
+    row_second = remote(seqs, place, place, "ctx", row_peer)
+    row_second.start()
+    row_first.wait()
+    place = out.at[seq, :, core, :, right]
+    seq_second = []
+    for d in range(1, seqs):
+        copy = remote(seqs + d, place, place, "fsdp", lax.rem(seq + d, seqs))
+        copy.start()
+        seq_second.append(copy)
+    row_second.wait()
+    for copy in seq_second:
+        copy.wait()
+    place = out.at[:, :, core]
+    core_last = remote(2 * seqs, place, place, "ctx", core_peer)
+    core_last.start()
+    core_last.wait()
+
+
+def gather_shards(shard, seqs, collective_id):
+    rows, cols = shard.shape
+    full = pl.pallas_call(
+        functools.partial(gather_kernel, seqs),
+        out_shape=jax.ShapeDtypeStruct((seqs, 2, 2, rows, cols), bf16),
+        in_specs=[pl.BlockSpec(memory_space=pltpu.VMEM)],
+        out_specs=pl.BlockSpec(memory_space=pl.ANY),
+        scratch_shapes=[
+            pltpu.SemaphoreType.DMA((2 * seqs + 1,)),
+            pltpu.SemaphoreType.DMA((2 * seqs + 1,)),
+            pltpu.SemaphoreType.DMA,
+        ],
+        compiler_params=pltpu.CompilerParams(
+            collective_id=collective_id, has_side_effects=True, vmem_limit_bytes=16 * 2**20
+        ),
+        cost_estimate=pl.CostEstimate(
+            flops=0, bytes_accessed=8 * seqs * rows * cols, transcendentals=0
+        ),
+        name=f"gather_{collective_id}",
+    )(shard)
+    return full.reshape(-1, cols)
 
 
 def sum_kernel(count, width, chunks, slots, *refs):
@@ -954,24 +1043,30 @@
     def chosen(table, dim):
         return lax.dynamic_index_in_dim(table, adapter, dim, keepdims=False)
 
-    def gathered(*parts):
-        return lax.all_gather(jnp.concatenate(parts, axis=1), both, axis=0, tiled=True)
-
-    kv_full = gathered(key_weight, value_weight)
-    query_full = gathered(query_weight, output_weight.T)
-    ffn_full = gathered(gate_weight, up_weight, down_weight.T)
+    def gathered(shard):
+        return lax.all_gather(shard, both, axis=0, tiled=True)
+
+    kv_full = gathered(jnp.concatenate([key_weight, value_weight], axis=1))
+    ffn_shard = jnp.concatenate([gate_weight, up_weight, down_weight.T], axis=1)
+    query_shard = jnp.concatenate([query_weight, output_weight.T], axis=1)
+    residual = tokens[0].astype(f32)
+    n1 = rms_norm(residual, gains[0]).astype(bf16)
+    a_in = chosen(adapter_first_input, 1)
+    a_qkv = jnp.concatenate([a_in[0], a_in[1], a_in[2]], axis=1)
+    u_qkv = dot_nn(n1, a_qkv).astype(bf16)
+    query_shard, n1, u_qkv = lax.optimization_barrier((query_shard, n1, u_qkv))
+    query_full = gather_shards(query_shard, lax.axis_size("fsdp"), 3)
+    kv_full, query_full = lax.optimization_barrier((kv_full, query_full))
     qkv_cols = q_cols + 2 * k_cols
     out_full = query_full[:, q_cols:]
     query_full = query_full[:, :q_cols]
 
-    a_in = chosen(adapter_first_input, 1)
     b_query = chosen(adapter_second_query, 0)
     b_kv = chosen(adapter_second_keyvalue, 1)
     b_gate = chosen(adapter_second_gate, 1)
     a_out = chosen(adapter_first_output, 0)
     a_down = chosen(adapter_first_down, 0)
     b_out = chosen(adapter_second_output, 1)
-    a_qkv = jnp.concatenate([a_in[0], a_in[1], a_in[2]], axis=1)
     a_gu = jnp.concatenate([a_in[3], a_in[4]], axis=1)
 
     ctx = lax.axis_index("ctx")
@@ -982,20 +1077,19 @@
     cosine = jnp.cos(angle)
     sine = jnp.sin(angle)
 
-    residual = tokens[0].astype(f32)
-    d_final = cotangent[0].astype(f32)
-    n1 = rms_norm(residual, gains[0]).astype(bf16)
-    u_qkv = dot_nn(n1, a_qkv).astype(bf16)
     lin_kv = dot_nn(n1, kv_full)
-    query = dot_nn(n1, query_full) + dot_nn(u_qkv[:, :rank], b_query)
     key = lin_kv[:, :k_cols] + dot_nn(u_qkv[:, rank : 2 * rank], b_kv[0])
     value = lin_kv[:, k_cols:] + dot_nn(u_qkv[:, 2 * rank :], b_kv[1])
-    qa = (rotate(query, cosine, sine) * scale).astype(bf16)
     ka = rotate(key, cosine, sine).astype(bf16)
     va = value.astype(bf16)
-
     own = jnp.stack([ka, va])
+    query_full, _ = lax.optimization_barrier((query_full, own))
+    query = dot_nn(n1, query_full) + dot_nn(u_qkv[:, :rank], b_query)
+    qa = (rotate(query, cosine, sine) * scale).astype(bf16)
+
     from_row = swap(own, 2)
+    from_row, ffn_shard = lax.optimization_barrier((from_row, ffn_shard))
+    ffn_full = gathered(ffn_shard)
     near = jnp.concatenate([own, from_row], axis=1)
     far = swap(near, 1)
     keys, values = jnp.concatenate([near, far], axis=1)

time: 691 us -> 686 us (level)
  waiting for transfers between devices: 74.1 us -> 23.7 us
  Pallas kernels: 441 us -> 481 us
    all_gather x3 -> x2, waiting for transfers between devices: 43.4 us -> 0.18 us  [gathered(): return lax.all_gather(shard, both, axis=0, tiled=True)]
    pallas_call x0 -> x1, Pallas kernels: none -> 35.9 us  [gather_shards(): pl.pallas_call(functools.partial(gather_kernel, seqs), out_shape=jax.Shap...]
    ppermute x4, waiting for transfers between devices: 30.6 us -> 23.5 us  [swap(): lax.ppermute(values, 'ctx', [(i, i ^ step) for i in range(lax.axis_size('...]
    unnamed x131 -> x137, local copies, waits for them, and re-layouts: 14.9 us -> 17.2 us
  transfers between devices with their start and end apart: 7 -> 6, of which waited for: 4 -> 3; matrix products, arithmetic and copies ran while one was open for 11% -> 10% of each run, Pallas kernels for 16% -> 21%
where the time goes in v5:
time: 686 us; the launch traced here: 677 us
  Pallas kernels  481 us (70%)
  other arithmetic  59.5 us (9%)
  local copies, waits for them, and re-layouts  48.4 us (7%)
  matrix products  46 us (7%)
  waiting for transfers between devices  23.7 us (3%)
  between operations  16.8 us (2%)
    pallas_call x1, Pallas kernels, feed_forward(): pl.pallas_call(ffn_kernel, out_shape=shapes, in_specs=[anywhere] * 2 + [v...  209 us
    pallas_call x2, Pallas kernels, matmul_sum(): pl.pallas_call(functools.partial(sum_kernel, len(lefts), width, chunks, s...  202 us
    pallas_call x1, Pallas kernels, gather_shards(): pl.pallas_call(functools.partial(gather_kernel, seqs), out_shape=jax.Shap...  35.9 us
    ppermute x4, waiting for transfers between devices, swap(): lax.ppermute(values, 'ctx', [(i, i ^ step) for i in range(lax.axis_size('...  23.5 us
    dot_general x11, matrix products, dot_tn(): lax.dot_general(left, right, (((0,), (0,)), ((), ())), preferred_element_...  23.1 us
    pallas_call x1, Pallas kernels, attend_back(): pl.pallas_call(functools.partial(attend_back_kernel, 768), out_shape=[jax...  22.7 us
    unnamed x137, local copies, waits for them, and re-layouts  17.2 us
  transfers between devices with their start and end apart: 6, of which 3 were waited for; matrix products, arithmetic and copies ran while one was open for 10% of the time, Pallas kernels for 21%

profile of v5, /device:TPU:0, one launch (start us, length us, event | category | flops | bytes accessed | tf_op | source)
XLA Modules:
  0.0 676.8 jit_solution(14444477997948202724)
XLA Ops:
  7.2 1.9 pad_maximum_fusion.8
  9.8 1.6 slice_reduce_fusion.2
  12.6 2.8 fusion.15
  15.4 1.8 dynamic-slice_bitcast_fusion.14
  18.1 1.7 copy-done.9
  19.8 1.8 convolution_convert_fusion.8
  21.6 35.9 %gather_3.1 = bf16[2,2,2,288,1024]{4,3,2,1,0:T(8,128)(2,1)S(1)} custom-call(bf16[288,1024]{1,0:T(8,128)(2,1)S(1)} %pad_maximum_fusion.6.shard), custom_call_target="tpu_custom_call" | custom-call | bytes 4718592 | tf_op jit(solution)/shard_map/gather_3/pallas_call | solution.py:123
  57.6 2.2 copy-done
  60.3 3.7 fusion.118
  66.3 1.8 fusion.70
  69.6 2.0 pad_maximum_fusion
  71.6 17.6 %collective-permute-done = bf16[2,768,256]{2,1,0:T(8,128)(2,1)} collective-permute-done((bf16[2,768,256]{2,1,0:T(8,128)(2,1)}, bf16[2,768,256]{2,1,0:T(8,128)(2,1)}, u32[]{:S(2)}, u32[]{:S(2)}) %collective-permute-start) | collective-permute-done | bytes 786464 | tf_op jit(solution)/shard_map/ppermute | solution.py:1009
  91.3 1.6 dynamic-slice_bitcast_fusion.10
  92.9 1.9 copy.74.refs_3_
  98.5 1.6 dynamic-slice_bitcast_fusion.b_gate
  100.1 1.6 pad_maximum_fusion.14.a_gu
  101.7 1.6 pad_maximum_fusion.2
  103.4 4.7 fusion.117
  108.1 2.0 fusion.119
  111.2 1.8 fusion.64
  113.2 2.9 pad_maximum_fusion.1
  116.1 1.8 slice_bitcast_fusion.1
  118.0 11.2 %attend.1 = (bf16[768,512]{1,0:T(8,128)(2,1)S(1)}, f32[2,768,1]{2,1,0:T(8,128)S(1)}) custom-call(s32[4]{0:T(128)S(1)} %add_multiply_fusion.bases, bf16[768,512]{1,0:T(8,128)(2,1)S(1)} %fusion.21.q, s32[768,1]{1,0:T(8,128)S(1)} %add_maximum_fusion.limit, bf16[3072,256]{1,0:T(8,128)(2,1)} %get-tuple-element.111.keys, bf16[3072,256]{1,0:T(8,128)(2,1)} %get-tuple-element.110.values), custom_call_target="tpu_custom_call" | custom-call | flops 4831838208 | bytes 8388608 | tf_op jit(solution)/shard_map/attend/pallas_call | solution.py:893
  130.2 1.7 convolution_convert_fusion.7.refs_1_
  132.0 96.6 %matmul_sum_1.1 = bf16[768,2304]{1,0:T(8,128)(2,1)} custom-call(bf16[768,512]{1,0:T(8,128)(2,1)} %copy-done.1, bf16[768,16]{1,0:T(8,128)(2,1)} %convolution_convert_fusion.7.refs_1_, bf16[2304,512]{1,0:T(8,128)(2,1)} %get-tuple-element.108.refs_2_.w_out, bf16[2304,16]{1,0:T(8,128)(2,1)} %copy.74.refs_3_), custom_call_target="tpu_custom_call" | custom-call | flops 1868562432 | bytes 6782976 | tf_op jit(solution)/shard_map/matmul_sum_1/pallas_call | solution.py:407
  228.6 3.0 fusion.3
  231.8 3.5 multiply_reduce_fusion.1
  236.0 2.3 copy-done.8
  238.3 1.8 copy-done.12
  242.9 208.9 %feed_forward_2.1 = (bf16[6,128,2304]{2,1,0:T(8,128)(2,1)}, bf16[6,128,2304]{2,1,0:T(8,128)(2,1)}, bf16[6,128,2304]{2,1,0:T(8,128)(2,1)}, bf16[6,128,2304]{2,1,0...) custom-call(bf16[6,128,2304]{2,1,0:T(8,128)(2,1)} %bitcast.175, ...), custom_call_target="tpu_custom_call" | custom-call | flops 48922361856 | bytes 62914560 | tf_op jit(solution)/shard_map/feed_forward_2/pallas_call | solution.py:824
  451.8 1.6 convert_multiply_fusion.7
  454.4 22.7 %attend_back.1 = (f32[768,512]{1,0:T(8,128)}, f32[2,1536,256]{2,1,0:T(8,128)}, bf16[2,1536,256]{2,1,0:T(8,128)(2,1)}) custom-call(s32[4]{0:T(128)} %copy-done.4, bf16[768,512]{1,0:T(8,128)(2,1)} %copy-done.3, bf16[768,512]{1,0:T(8,128)(2,1)} %bitcast.200, s32[1,768]{1,0:T(1,128)} %add_maximum_fusion.1.limit, f32[2,1,768]{2,1,0:T(1,128)} %bitcast.203, ...), custom_call_target="tpu_custom_call" | custom-call | flops 12079595520 | bytes 16777216 | tf_op jit(solution)/shard_map/attend_back/pallas_call | solution.py:970
  478.3 3.6 fusion.52
  485.7 2.6 convolution_convert_fusion.14
  489.6 3.9 fusion.26
  493.5 2.9 fusion.5
  496.5 1.7 convolution_convert_fusion.18
  498.2 2.5 convolution_convert_fusion.13
  501.3 6.0 fusion.16
  507.3 1.8 convolution_convert_fusion.15
  510.4 4.6 convolution_convert_fusion.2
  515.0 5.9 collective-permute-done.3
  520.9 1.8 slice_add_fusion
  524.7 2.0 fusion.57
  534.5 4.7 fusion.19
  540.9 1.7 copy.77.refs_2_
  545.3 105.6 %matmul_sum_4.1 = (bf16[768,2304]{1,0:T(8,128)(2,1)}, bf16[2,4,48,2304]{3,2,1,0:T(8,128)(2,1)}) custom-call(bf16[768,512]{1,0:T(8,128)(2,1)} %copy-done.21, bf16[768,512]{1,0:T(8,128)(2,1)} %pad_maximum_fusion.5.refs_1_, bf16[768,48]{1,0:T(8,128)(2,1)} %copy.77.refs_2_, bf16[2304,512]{1,0:T(8,128)(2,1)} %copy-done.30, ...), custom_call_target="tpu_custom_call" | custom-call | flops 3793747968 | bytes 10125312 | tf_op jit(solution)/shard_map/matmul_sum_4/pallas_call | solution.py:407
  664.8 4.0 fusion.14
  (217 shorter events, 54.7 us)
Async XLA Ops:
  7.2 10.0 %copy-start.5 = (bf16[1,768,2304]{2,1,0:T(8,128)(2,1)S(1)}, bf16[1,768,2304]{2,1,0:T(8,128)(2,1)}, u32[]{:S(2)}) copy-start(bf16[1,768,2304]{2,1,0:T(8,128)(2,1)} %param.19) | copy-start | bytes 10616836
  7.2 53.1 %all-gather.3.cloned.1.call-start = ((), (), s32[]{:S(2)}) async-start(), calls=%async_computation | async-start | bytes 2654208 | tf_op jit(solution)/shard_map/all_gather | solution.py:1047
  9.1 233.8 %all-gather.5.cloned.1.call-start = ((), (), s32[]{:S(2)}) async-start(), calls=%async_computation.1 | async-start | bytes 35831808 | tf_op jit(solution)/shard_map/all_gather | solution.py:1047
  11.5 6.6 copy-start.50
  21.6 38.6 %copy-start.10 = (bf16[768,2304]{1,0:T(8,128)(2,1)S(1)}, bf16[768,2304]{1,0:T(8,128)(2,1)}, u32[]{:S(2)}) copy-start(bf16[768,2304]{1,0:T(8,128)(2,1)} %copy-done.9) | copy-start | bytes 10616836
  60.3 50.9 %copy-start.54 = (f32[768]{0:T(1024)}, f32[768]{0:T(1024)S(1)}, u32[]{:S(2)}) copy-start(f32[768]{0:T(1024)S(1)} %add_convert_fusion) | copy-start | bytes 9220
  60.3 3.7 copy-start.35
  60.3 6.0 copy-start.61
  64.0 5.6 copy-start.32
  64.0 5.6 copy-start.33
  64.0 5.6 copy-start.34
  69.1 20.1 %collective-permute-start = (bf16[2,768,256]{2,1,0:T(8,128)(2,1)}, bf16[2,768,256]{2,1,0:T(8,128)(2,1)}, u32[]{:S(2)}, u32[]{:S(2)}) collective-permute-start(bf16[2,768,256]{2,1,0:T(8,128)(2,1)} %pad_maximum_fusion.4), channel_id=1, source_target_pairs={{0,8},{4,12},{8,0},{12,4},{1,9},{5,13},{9,1},{13,5},{2,10},{6,14},... | collective-permute-start | bytes 2359304 | tf_op jit(solution)/shard_map/ppermute | solution.py:1009
  94.9 23.1 %copy-start.4 = (s32[4]{0:T(128)}, s32[4]{0:T(128)S(1)}, u32[]{:S(2)}) copy-start(s32[4]{0:T(128)S(1)} %add_multiply_fusion.bases) | copy-start | bytes 52
  103.3 9.9 %collective-permute-start.1 = (bf16[2,1536,256]{2,1,0:T(8,128)(2,1)S(1)}, bf16[2,1536,256]{2,1,0:T(8,128)(2,1)S(1)}, u32[]{:S(2)}, u32[]{:S(2)}) collective-permute-start(bf16[2,1536,256]{2,1,0:T(8,128)(2,1)S(1)} %pad_maximum_fusion.2), channel_id=1, source_target_pairs={{0,4},{4,0},{8,12},{12,8},{1,5},{5,1},{9,13},{13,9},{2,6},{6,2},{1... | collective-permute-start | bytes 4718600 | tf_op jit(solution)/shard_map/ppermute | solution.py:1009
  113.2 4.8 copy-start.3
  231.8 3.5 copy-start.60
  235.4 4.7 copy-start.46
  235.4 4.7 copy-start.47
  454.3 22.9 %copy-start.38 = (bf16[2304,16]{0,1:T(8,128)(2,1)S(1)}, bf16[2304,16]{0,1:T(8,128)(2,1)}, u32[]{:S(2)}) copy-start(bf16[2304,16]{0,1:T(8,128)(2,1)} %copy-done.37) | copy-start | bytes 221188
  454.3 22.9 %copy-start.40 = (bf16[2304,16]{0,1:T(8,128)(2,1)S(1)}, bf16[2304,16]{0,1:T(8,128)(2,1)}, u32[]{:S(2)}) copy-start(bf16[2304,16]{0,1:T(8,128)(2,1)} %copy-done.39) | copy-start | bytes 221188
  454.3 22.9 %copy-start.42 = (bf16[2304,16]{0,1:T(8,128)(2,1)S(1)}, bf16[2304,16]{0,1:T(8,128)(2,1)}, u32[]{:S(2)}) copy-start(bf16[2304,16]{0,1:T(8,128)(2,1)} %copy-done.41) | copy-start | bytes 221188
  454.3 24.0 %copy-start.55 = (f32[768]{0:T(1024)S(1)}, f32[768]{0:T(1024)}, u32[]{:S(2)}) copy-start(f32[768]{0:T(1024)} %copy-done.54) | copy-start | bytes 9220
  454.4 24.0 %copy-start.63 = (f32[128]{0:T(128)S(1)}, f32[128]{0:T(128)}, u32[]{:S(2)}) copy-start(f32[128]{0:T(128)} %multiply_exponential_fusion) | copy-start | bytes 1540
  477.1 4.9 collective-permute-start.2
  478.3 3.7 copy-start.29
  482.0 14.5 %copy-start.21 = (bf16[768,512]{1,0:T(8,128)(2,1)}, bf16[768,512]{1,0:T(8,128)(2,1)S(1)}, u32[]{:S(2)}) copy-start(bf16[768,512]{1,0:T(8,128)(2,1)S(1)} %fusion.22.refs_0_) | copy-start | bytes 2359300
  482.0 3.7 copy-start.15
  482.4 5.9 copy-start.44
  485.7 3.8 copy-start.2
  485.7 3.8 copy-start.48
  493.5 4.7 copy-start.14
  496.4 4.9 copy-start.18
  496.4 4.9 copy-start.59
  500.7 20.2 %collective-permute-start.3 = (bf16[2,768,256]{2,1,0:T(8,128)(2,1)}, bf16[2,768,256]{2,1,0:T(8,128)(2,1)}, u32[]{:S(2)}, u32[]{:S(2)}) collective-permute-start(bf16[2,768,256]{2,1,0:T(8,128)(2,1)} %slice.346), channel_id=1, source_target_pairs={{0,8},{4,12},{8,0},{12,4},{1,9},{5,13},{9,1},{13,5},{2,10},{6,14},... | collective-permute-start | bytes 2359304 | tf_op jit(solution)/shard_map/ppermute | solution.py:1009
  501.3 6.0 copy-start.22
  501.3 7.8 %copy-start.45 = (bf16[768,32]{0,1:T(8,128)(2,1)S(1)}, bf16[768,32]{0,1:T(8,128)(2,1)}, u32[]{:S(2)}) copy-start(bf16[768,32]{0,1:T(8,128)(2,1)} %copy-done.43) | copy-start | bytes 147460
  515.0 7.8 %copy-start.36 = (bf16[768,48]{0,1:T(8,128)(2,1)S(1)}, bf16[768,48]{0,1:T(8,128)(2,1)}, u32[]{:S(2)}) copy-start(bf16[768,48]{0,1:T(8,128)(2,1)} %convolution_convert_fusion.8) | copy-start | bytes 221188
  522.7 6.1 copy-start.11
  522.7 6.1 copy-start.49
  526.8 5.1 copy-start.13
  526.8 5.1 copy-start.52
  526.8 5.1 copy-start.53
  534.5 8.1 %copy-start.58 = (bf16[16,512]{1,0:T(8,128)(2,1)S(1)}, bf16[16,512]{1,0:T(8,128)(2,1)}, u32[]{:S(2)}) copy-start(bf16[16,512]{1,0:T(8,128)(2,1)} %fusion.26) | copy-start | bytes 49156
  656.3 3.6 copy-start.7
  656.3 3.6 copy-start.51
  656.3 3.5 copy-start.57
  657.5 7.2 %slice-start = ((s8[7077888]{0:T(1024)(128)(4,1)}), s8[4194304]{0:T(1024)(128)(4,1)S(1)}, s32[]{:S(2)}) async-start(s8[7077888]{0:T(1024)(128)(4,1)} %bitcast.191), calls=%async_computation.2 | async-start | bytes 8388608
  659.9 4.9 slice-start.1
  (24 other events, 50.8 us)
Sparse Core Ops, SparseCore 0:
  10.5 37.6 all-gather.2
  89.3 153.4 all-gather.4

commit v6 on v5

--- a/solution.py
+++ b/solution.py
@@ -1056,7 +1056,8 @@
     u_qkv = dot_nn(n1, a_qkv).astype(bf16)
     query_shard, n1, u_qkv = lax.optimization_barrier((query_shard, n1, u_qkv))
     query_full = gather_shards(query_shard, lax.axis_size("fsdp"), 3)
-    kv_full, query_full = lax.optimization_barrier((kv_full, query_full))
+    kv_full, query_full, ffn_shard = lax.optimization_barrier((kv_full, query_full, ffn_shard))
+    ffn_full = gathered(ffn_shard)
     qkv_cols = q_cols + 2 * k_cols
     out_full = query_full[:, q_cols:]
     query_full = query_full[:, :q_cols]
@@ -1067,7 +1068,6 @@
     a_out = chosen(adapter_first_output, 0)
     a_down = chosen(adapter_first_down, 0)
     b_out = chosen(adapter_second_output, 1)
-    a_gu = jnp.concatenate([a_in[3], a_in[4]], axis=1)
 
     ctx = lax.axis_index("ctx")
     query_pos = ctx * rows + jnp.arange(rows, dtype=jnp.int32)
@@ -1088,8 +1088,9 @@
     qa = (rotate(query, cosine, sine) * scale).astype(bf16)
 
     from_row = swap(own, 2)
-    from_row, ffn_shard = lax.optimization_barrier((from_row, ffn_shard))
-    ffn_full = gathered(ffn_shard)
+    from_row, qa, a_gu, b_gate, a_down_t, a_out_t = lax.optimization_barrier(
+        (from_row, qa, jnp.stack([a_in[3].T, a_in[4].T]), b_gate, a_down.T, a_out.T)
+    )
     near = jnp.concatenate([own, from_row], axis=1)
     far = swap(near, 1)
     keys, values = jnp.concatenate([near, far], axis=1)
@@ -1101,22 +1102,22 @@
     y_att = matmul_sum([ob, u_out], [out_full, b_out[0].T], 1)
     h1 = residual + rms_norm(y_att.astype(f32), gains[1])
     n2 = rms_norm(h1, gains[2]).astype(bf16)
-    u_gu = dot_nn(n2, a_gu).astype(bf16)
+    u_gu = dot_nt(n2, a_gu.reshape(2 * rank, width)).astype(bf16)
     y_ffn, act, e_ffn, d_gate, d_up, dh1, e_att, d_ob = feed_forward(
         n2,
         cotangent[0],
         u_gu,
         gains[1:],
         b_gate,
-        a_down.T,
+        a_down_t,
         b_out[1],
-        jnp.stack([a_in[3].T, a_in[4].T]),
+        a_gu,
         ffn_full,
         h1,
         y_att,
         out_full,
         b_out[0],
-        a_out.T,
+        a_out_t,
         2,
     )
     overlap = d_ob.astype(f32) * ob.astype(f32)

time: 686 us -> 684 us (level)
  waiting for transfers between devices: 23.7 us -> 35.8 us
    ppermute x4, waiting for transfers between devices: 23.5 us -> 35.7 us  [swap(): lax.ppermute(values, 'ctx', [(i, i ^ step) for i in range(lax.axis_size('...]
  transfers between devices with their start and end apart: 6 -> 6, of which waited for: 3 -> 2; matrix products, arithmetic and copies ran while one was open for 10% -> 11% of each run, Pallas kernels for 21% -> 22%
where the time goes in v6:
time: 684 us; the launch traced here: 675 us
  Pallas kernels  479 us (70%)
  other arithmetic  55.8 us (8%)
  matrix products  44.6 us (7%)
  local copies, waits for them, and re-layouts  42.8 us (6%)
  waiting for transfers between devices  35.8 us (5%)
  between operations  16.7 us (2%)
    pallas_call x1, Pallas kernels, feed_forward(): pl.pallas_call(ffn_kernel, out_shape=shapes, in_specs=[anywhere] * 2 + [v...  204 us
    pallas_call x2, Pallas kernels, matmul_sum(): pl.pallas_call(functools.partial(sum_kernel, len(lefts), width, chunks, s...  202 us
    pallas_call x1, Pallas kernels, gather_shards(): pl.pallas_call(functools.partial(gather_kernel, seqs), out_shape=jax.Shap...  38.4 us
    ppermute x4, waiting for transfers between devices, swap(): lax.ppermute(values, 'ctx', [(i, i ^ step) for i in range(lax.axis_size('...  35.7 us
    dot_general x11, matrix products, dot_tn(): lax.dot_general(left, right, (((0,), (0,)), ((), ())), preferred_element_...  23.2 us
    pallas_call x1, Pallas kernels, attend_back(): pl.pallas_call(functools.partial(attend_back_kernel, 768), out_shape=[jax...  22.7 us
    unnamed x137, local copies, waits for them, and re-layouts  16.1 us
  transfers between devices with their start and end apart: 6, of which 2 were waited for; matrix products, arithmetic and copies ran while one was open for 11% of the time, Pallas kernels for 22%

profile of v6, /device:TPU:0, one launch (start us, length us, event | category | flops | bytes accessed | tf_op | source)
XLA Modules:
  0.0 675.1 jit_solution(15339635280859578458)
XLA Ops:
  7.2 1.9 pad_maximum_fusion.8
  9.8 1.6 slice_reduce_fusion.2
  12.6 2.8 fusion.15
  15.4 1.7 dynamic-slice_bitcast_fusion.3
  18.0 1.8 convolution_convert_fusion.8
  19.9 38.4 %gather_3.1 = bf16[2,2,2,288,1024]{4,3,2,1,0:T(8,128)(2,1)S(1)} custom-call(bf16[288,1024]{1,0:T(8,128)(2,1)S(1)} %pad_maximum_fusion.6.shard), custom_call_target="tpu_custom_call" | custom-call | bytes 4718592 | tf_op jit(solution)/shard_map/gather_3/pallas_call | solution.py:123
  58.3 2.2 copy-done
  60.5 2.0 pad_maximum_fusion
  64.1 1.5 dynamic-slice_bitcast_fusion.9.a_down
  65.6 1.6 dynamic-slice_bitcast_fusion.b_gate
  67.2 1.7 pad_maximum_fusion.14.a_gu
  68.9 4.3 fusion.116
  75.3 1.8 fusion.70
  77.4 1.8 fusion.115
  79.2 2.0 fusion.117
  82.3 1.8 fusion.64
  84.3 30.1 %collective-permute-done = bf16[2,768,256]{2,1,0:T(8,128)(2,1)S(1)} collective-permute-done((bf16[2,768,256]{2,1,0:T(8,128)(2,1)S(1)}, bf16[2,768,256]{2,1,0:T(8,128)(2,1)S(1)}, u32[]{:S(2)}, u32[]{:S(2)}) %collective-permute-start) | collective-permute-done | bytes 786464 | tf_op jit(solution)/shard_map/ppermute | solution.py:1009
  116.6 1.6 dynamic-slice_bitcast_fusion.8
  120.0 2.2 pad_maximum_fusion.1
  122.1 1.8 slice_bitcast_fusion.1
  124.0 11.2 %attend.1 = (bf16[768,512]{1,0:T(8,128)(2,1)S(1)}, f32[2,768,1]{2,1,0:T(8,128)S(1)}) custom-call(s32[4]{0:T(128)S(1)} %add_multiply_fusion.bases, bf16[768,512]{1,0:T(8,128)(2,1)S(1)} %fusion.21.q, s32[768,1]{1,0:T(8,128)S(1)} %add_maximum_fusion.limit, bf16[3072,256]{1,0:T(8,128)(2,1)} %get-tuple-element.121.keys, bf16[3072,256]{1,0:T(8,128)(2,1)} %get-tuple-element.120.values), custom_call_target="tpu_custom_call" | custom-call | flops 4831838208 | bytes 8388608 | tf_op jit(solution)/shard_map/attend/pallas_call | solution.py:893
  136.2 1.7 convolution_convert_fusion.7.refs_1_
  138.0 96.9 %matmul_sum_1.1 = bf16[768,2304]{1,0:T(8,128)(2,1)} custom-call(bf16[768,512]{1,0:T(8,128)(2,1)} %copy-done.1, bf16[768,16]{1,0:T(8,128)(2,1)} %convolution_convert_fusion.7.refs_1_, bf16[2304,512]{1,0:T(8,128)(2,1)} %get-tuple-element.118.refs_2_.w_out, bf16[2304,16]{1,0:T(8,128)(2,1)} %copy.75.refs_3_), custom_call_target="tpu_custom_call" | custom-call | flops 1868562432 | bytes 6782976 | tf_op jit(solution)/shard_map/matmul_sum_1/pallas_call | solution.py:407
  234.9 2.9 fusion.3
  237.9 3.5 multiply_reduce_fusion.1
  242.1 2.3 copy-done.8
  244.4 1.8 copy-done.12
  248.8 204.0 %feed_forward_2.1 = (bf16[6,128,2304]{2,1,0:T(8,128)(2,1)}, bf16[6,128,2304]{2,1,0:T(8,128)(2,1)}, bf16[6,128,2304]{2,1,0:T(8,128)(2,1)}, bf16[6,128,2304]{2,1,0...) custom-call(bf16[6,128,2304]{2,1,0:T(8,128)(2,1)} %bitcast.177, ...), custom_call_target="tpu_custom_call" | custom-call | flops 48922361856 | bytes 62914560 | tf_op jit(solution)/shard_map/feed_forward_2/pallas_call | solution.py:824
  452.8 1.6 convert_multiply_fusion.7
  455.3 22.7 %attend_back.1 = (f32[768,512]{1,0:T(8,128)}, f32[2,1536,256]{2,1,0:T(8,128)}, bf16[2,1536,256]{2,1,0:T(8,128)(2,1)}) custom-call(s32[4]{0:T(128)} %copy-done.4, bf16[768,512]{1,0:T(8,128)(2,1)} %copy-done.3, bf16[768,512]{1,0:T(8,128)(2,1)} %bitcast.202, s32[1,768]{1,0:T(1,128)} %add_maximum_fusion.1.limit, f32[2,1,768]{2,1,0:T(1,128)} %bitcast.206, ...), custom_call_target="tpu_custom_call" | custom-call | flops 12079595520 | bytes 16777216 | tf_op jit(solution)/shard_map/attend_back/pallas_call | solution.py:970
  479.3 3.6 fusion.52
  486.7 1.7 convolution_convert_fusion.14
  489.5 3.9 fusion.26
  493.5 2.9 fusion.5
  496.4 1.8 convolution_convert_fusion.18
  499.9 6.0 fusion.16
  505.9 1.8 convolution_convert_fusion.15
  507.7 1.7 convolution_convert_fusion.13
  509.4 4.6 convolution_convert_fusion.2
  514.0 5.6 collective-permute-done.3
  519.6 1.8 slice_add_fusion
  523.4 2.0 fusion.57
  533.2 4.7 fusion.19
  539.6 1.7 copy.78.refs_2_
  544.0 105.3 %matmul_sum_4.1 = (bf16[768,2304]{1,0:T(8,128)(2,1)}, bf16[2,4,48,2304]{3,2,1,0:T(8,128)(2,1)}) custom-call(bf16[768,512]{1,0:T(8,128)(2,1)} %copy-done.21, bf16[768,512]{1,0:T(8,128)(2,1)} %pad_maximum_fusion.5.refs_1_, bf16[768,48]{1,0:T(8,128)(2,1)} %copy.78.refs_2_, bf16[2304,512]{1,0:T(8,128)(2,1)} %copy-done.28, ...), custom_call_target="tpu_custom_call" | custom-call | flops 3793747968 | bytes 10125312 | tf_op jit(solution)/shard_map/matmul_sum_4/pallas_call | solution.py:407
  658.2 1.5 fusion.10
  661.5 1.6 copy.84
  663.1 4.0 fusion.14
  (218 shorter events, 49.0 us)
Async XLA Ops:
  7.2 9.9 %copy-start.5 = (bf16[1,768,2304]{2,1,0:T(8,128)(2,1)S(1)}, bf16[1,768,2304]{2,1,0:T(8,128)(2,1)}, u32[]{:S(2)}) copy-start(bf16[1,768,2304]{2,1,0:T(8,128)(2,1)} %param.19) | copy-start | bytes 10616836
  7.2 55.4 %all-gather.3.cloned.1.call-start = ((), (), s32[]{:S(2)}) async-start(), calls=%async_computation | async-start | bytes 2654208 | tf_op jit(solution)/shard_map/all_gather | solution.py:1047
  9.1 239.7 %all-gather.5.cloned.1.call-start = ((), (), s32[]{:S(2)}) async-start(), calls=%async_computation.1 | async-start | bytes 35831808 | tf_op jit(solution)/shard_map/all_gather | solution.py:1047
  11.5 6.5 copy-start.48
  18.0 40.3 %copy-start.9 = (bf16[768,2304]{1,0:T(8,128)(2,1)}, bf16[768,2304]{1,0:T(8,128)(2,1)S(1)}, u32[]{:S(2)}) copy-start(bf16[768,2304]{1,0:T(8,128)(2,1)S(1)} %fusion.9) | copy-start | bytes 10616836
  19.9 40.6 %copy-start.30 = (bf16[2304,288]{0,1:T(8,128)(2,1)S(1)}, bf16[2304,288]{0,1:T(8,128)(2,1)}, u32[]{:S(2)}) copy-start(bf16[2304,288]{0,1:T(8,128)(2,1)} %param.30) | copy-start | bytes 3981316
  19.9 40.6 %copy-start.31 = (bf16[288,2304]{1,0:T(8,128)(2,1)S(1)}, bf16[288,2304]{1,0:T(8,128)(2,1)}, u32[]{:S(2)}) copy-start(bf16[288,2304]{1,0:T(8,128)(2,1)} %param.29) | copy-start | bytes 3981316
  19.9 40.6 %copy-start.32 = (bf16[288,2304]{1,0:T(8,128)(2,1)S(1)}, bf16[288,2304]{1,0:T(8,128)(2,1)}, u32[]{:S(2)}) copy-start(bf16[288,2304]{1,0:T(8,128)(2,1)} %param.28) | copy-start | bytes 3981316
  62.5 6.4 copy-start.10
  62.6 19.7 %copy-start.60 = (f32[128]{0:T(128)}, f32[128]{0:T(128)S(1)}, u32[]{:S(2)}) copy-start(f32[128]{0:T(128)S(1)} %multiply_exponential_fusion) | copy-start | bytes 1540
  62.6 19.7 %copy-start.53 = (f32[768]{0:T(1024)}, f32[768]{0:T(1024)S(1)}, u32[]{:S(2)}) copy-start(f32[768]{0:T(1024)S(1)} %add_convert_fusion) | copy-start | bytes 9220
  67.2 10.2 %slice-start = ((s8[4718592]{0:T(1024)(128)(4,1)}), s8[4194304]{0:T(1024)(128)(4,1)S(1)}, s32[]{:S(2)}) async-start(s8[4718592]{0:T(1024)(128)(4,1)} %bitcast.173), calls=%async_computation.2 | async-start | bytes 8388608
  68.9 4.3 copy-start.33
  68.9 8.5 %slice-start.1 = ((s8[4718592]{0:T(1024)(128)(4,1)}), s8[524288]{0:T(1024)(128)(4,1)S(1)}, s32[]{:S(2)}) async-start(s8[4718592]{0:T(1024)(128)(4,1)} %bitcast.173), calls=%async_computation.3 | async-start | bytes 1048576
  74.3 40.1 %copy-start.23 = (bf16[1,768,256]{2,1,0:T(8,128)(2,1)}, bf16[1,768,256]{2,1,0:T(8,128)(2,1)S(1)}, u32[]{:S(2)}) copy-start(bf16[1,768,256]{2,1,0:T(8,128)(2,1)S(1)} %fusion.24) | copy-start | bytes 1179652
  77.1 37.3 %copy-start.24 = (bf16[1,768,128]{2,1,0:T(8,128)(2,1)}, bf16[1,768,128]{2,1,0:T(8,128)(2,1)S(1)}, u32[]{:S(2)}) copy-start(bf16[1,768,128]{2,1,0:T(8,128)(2,1)S(1)} %get-tuple-element.144) | copy-start | bytes 589828
  77.1 37.3 %copy-start.25 = (bf16[1,768,128]{2,1,0:T(8,128)(2,1)}, bf16[1,768,128]{2,1,0:T(8,128)(2,1)S(1)}, u32[]{:S(2)}) copy-start(bf16[1,768,128]{2,1,0:T(8,128)(2,1)S(1)} %get-tuple-element.145) | copy-start | bytes 589828
  77.2 37.2 %collective-permute-start = (bf16[2,768,256]{2,1,0:T(8,128)(2,1)S(1)}, bf16[2,768,256]{2,1,0:T(8,128)(2,1)S(1)}, u32[]{:S(2)}, u32[]{:S(2)}) collective-permute-start(bf16[2,768,256]{2,1,0:T(8,128)(2,1)S(1)} %pad_maximum_fusion.4), channel_id=1, source_target_pairs={{0,8},{4,12},{8,0},{12,4},{1,9},{5,13},{9,1},{13,5},{2,10},{6,14},... | collective-permute-start | bytes 2359304 | tf_op jit(solution)/shard_map/ppermute | solution.py:1009
  84.2 31.1 %copy-start.50 = (f32[4,2304]{1,0:T(4,128)S(1)}, f32[4,2304]{1,0:T(4,128)}, u32[]{:S(2)}) copy-start(f32[4,2304]{1,0:T(4,128)} %param.23) | copy-start | bytes 110596
  84.3 39.7 %copy-start.3 = (bf16[768,512]{1,0:T(8,128)(2,1)}, bf16[768,512]{1,0:T(8,128)(2,1)S(1)}, u32[]{:S(2)}) copy-start(bf16[768,512]{1,0:T(8,128)(2,1)S(1)} %fusion.21.q) | copy-start | bytes 2359300
  115.3 4.7 collective-permute-start.1
  119.3 4.7 copy-start.4
  241.5 4.7 copy-start.41
  455.3 22.8 %copy-start.36 = (bf16[2304,16]{0,1:T(8,128)(2,1)S(1)}, bf16[2304,16]{0,1:T(8,128)(2,1)}, u32[]{:S(2)}) copy-start(bf16[2304,16]{0,1:T(8,128)(2,1)} %copy-done.35) | copy-start | bytes 221188
  455.3 22.8 %copy-start.38 = (bf16[2304,16]{0,1:T(8,128)(2,1)S(1)}, bf16[2304,16]{0,1:T(8,128)(2,1)}, u32[]{:S(2)}) copy-start(bf16[2304,16]{0,1:T(8,128)(2,1)} %copy-done.37) | copy-start | bytes 221188
  455.3 22.9 %copy-start.40 = (bf16[2304,16]{0,1:T(8,128)(2,1)S(1)}, bf16[2304,16]{0,1:T(8,128)(2,1)}, u32[]{:S(2)}) copy-start(bf16[2304,16]{0,1:T(8,128)(2,1)} %copy-done.39) | copy-start | bytes 221188
  455.3 24.0 %copy-start.54 = (f32[768]{0:T(1024)S(1)}, f32[768]{0:T(1024)}, u32[]{:S(2)}) copy-start(f32[768]{0:T(1024)} %copy-done.53) | copy-start | bytes 9220
  455.3 24.0 %copy-start.61 = (f32[128]{0:T(128)S(1)}, f32[128]{0:T(128)}, u32[]{:S(2)}) copy-start(f32[128]{0:T(128)} %copy-done.60) | copy-start | bytes 1540
  478.0 4.9 collective-permute-start.2
  479.3 3.7 copy-start.27
  482.9 13.5 %copy-start.21 = (bf16[768,512]{1,0:T(8,128)(2,1)}, bf16[768,512]{1,0:T(8,128)(2,1)S(1)}, u32[]{:S(2)}) copy-start(bf16[768,512]{1,0:T(8,128)(2,1)S(1)} %fusion.22.refs_0_) | copy-start | bytes 2359300
  483.0 3.7 copy-start.15
  483.4 5.0 copy-start.45
  493.5 4.7 copy-start.14
  493.5 6.4 copy-start.18
  493.5 6.4 copy-start.58
  499.4 20.2 %collective-permute-start.3 = (bf16[2,768,256]{2,1,0:T(8,128)(2,1)}, bf16[2,768,256]{2,1,0:T(8,128)(2,1)}, u32[]{:S(2)}, u32[]{:S(2)}) collective-permute-start(bf16[2,768,256]{2,1,0:T(8,128)(2,1)} %slice.350), channel_id=1, source_target_pairs={{0,8},{4,12},{8,0},{12,4},{1,9},{5,13},{9,1},{13,5},{2,10},{6,14},... | collective-permute-start | bytes 2359304 | tf_op jit(solution)/shard_map/ppermute | solution.py:1009
  499.9 6.1 copy-start.22
  499.9 7.8 %copy-start.43 = (bf16[2,16,2304]{2,1,0:T(8,128)(2,1)S(1)}, bf16[2,16,2304]{2,1,0:T(8,128)(2,1)}, u32[]{:S(2)}) copy-start(bf16[2,16,2304]{2,1,0:T(8,128)(2,1)} %dynamic-slice_bitcast_fusion.b_gate) | copy-start | bytes 442372
  514.0 7.5 %copy-start.34 = (bf16[768,48]{0,1:T(8,128)(2,1)S(1)}, bf16[768,48]{0,1:T(8,128)(2,1)}, u32[]{:S(2)}) copy-start(bf16[768,48]{0,1:T(8,128)(2,1)} %convolution_convert_fusion.8) | copy-start | bytes 221188
  521.4 6.1 copy-start.11
  521.4 6.1 copy-start.47
  525.5 5.1 copy-start.13
  525.5 5.1 copy-start.51
  525.5 5.1 copy-start.52
  533.2 8.1 %copy-start.57 = (bf16[16,512]{1,0:T(8,128)(2,1)S(1)}, bf16[16,512]{1,0:T(8,128)(2,1)}, u32[]{:S(2)}) copy-start(bf16[16,512]{1,0:T(8,128)(2,1)} %fusion.26) | copy-start | bytes 49156
  655.9 7.2 %slice-start.2 = ((s8[7077888]{0:T(1024)(128)(4,1)}), s8[4194304]{0:T(1024)(128)(4,1)S(1)}, s32[]{:S(2)}) async-start(s8[7077888]{0:T(1024)(128)(4,1)} %bitcast.193), calls=%async_computation.4 | async-start | bytes 8388608
  658.2 4.9 slice-start.3
  (24 other events, 59.3 us)
Sparse Core Ops, SparseCore 0:
  10.5 40.1 all-gather.2
  62.7 170.1 all-gather.4
